TPU v7x, 256 devices: a whole 4x4x8 slice. The times are simulated.
256 devices in a mesh: section: 2 (over core), dp: 8 (over y_hi, x), tensor: 16 (over z, y_lo).
Axes of the slice: x: 4, y: 4 (y_hi: 2, y_lo: 2; y = y_hi * 2 + y_lo), z: 8, core: 2. Of those that a mesh axis runs over, the one named last changes fastest.
Arguments:
- tokens_in: bfloat16 [1024, 8192], P('dp', ('section', 'tensor')), may hold values from -70 to 70
- gain_attn: bfloat16 [8192], replicated, may hold values from 0.5 to 1.5
- w_query: bfloat16 [8192, 8192], P(None, ('section', 'tensor')), may hold values from -6 to 6
- w_keyval: bfloat16 [8192, 2048], P(None, ('section', 'tensor')), may hold values from -0.0625 to 0.0625
- w_out: bfloat16 [8192, 8192], P(('section', 'tensor')), may hold values from -0.0625 to 0.0625
- gain_mlp: bfloat16 [8192], replicated, may hold values from 0.5 to 1.5
- w_gate: bfloat16 [8192, 16384], P('dp', ('section', 'tensor')), may hold values from -0.0625 to 0.0625
- w_up: bfloat16 [8192, 16384], P('dp', ('section', 'tensor')), may hold values from -0.0625 to 0.0625
- w_down: bfloat16 [16384, 8192], P(('section', 'tensor'), 'dp'), may hold values from -0.046875 to 0.046875
Outputs:
- layer_out: bfloat16 [1024, 8192], P(('section', 'tensor'), 'dp')
All inputs are finite; a program needn't handle non-finite values.
Results may differ from a plain program's by a relative error of at most 0.0068.
Values may be sent and summed in bfloat16 or wider, within the bound.
No kernel may reach another device: no remote copies, remote signals or barrier semaphores. Data moves between devices by JAX's collectives and lax.ppermute only.
A program may use at most 64 MiB of HBM per device.

v0:
```python
import jax
import jax.numpy as jnp
from jax import lax
from jax.experimental import pallas as pl
from jax.experimental.pallas import tpu as pltpu
from jax.sharding import Mesh
from jax.sharding import PartitionSpec as P


HD = 128
EPS = 1e-05
THETA = 10000.0

F32 = jnp.float32
BF16 = jnp.bfloat16
DP = ("yh", "x")
Z = ("zh", "zl")
GROUP = ("c", "zh", "zl", "yl")
EVERY = ("c", "yh", "x", "zh", "zl", "yl")
SIZES = (2, 2, 4, 4, 2, 2)
SWAP = [(0, 1), (1, 0)]
NX = 4


def dot(a, b):
    return jnp.dot(a, b, preferred_element_type=F32)


def dot_t(a, b):
    return lax.dot_general(a, b, (((1,), (1,)), ((), ())), preferred_element_type=F32)


def to_all(array, axis):
    length = lax.axis_size(axis)
    return exchange(jnp.broadcast_to(array[None], (length, *array.shape)), axis)


def exchange(tiles, axis):
    return lax.all_to_all(tiles, axis, 0, 0, tiled=True)


def from_sq(array, s):
    return lax.ppermute(array, ("zl", "yl"), [(i, i ^ s) for i in range(4)])


def move(array, target):
    moves = []
    for n in range(256):
        at, rest = {}, n
        for name, size in zip(reversed(EVERY), reversed(SIZES)):
            at[name] = rest % size
            rest //= size
        goal, to = {**at, **target(**at)}, 0
        for name, size in zip(EVERY, SIZES):
            to = to * size + goal[name]
        moves.append((n, to))
    return lax.ppermute(array, EVERY, moves)


VMEM = pl.BlockSpec(memory_space=pltpu.VMEM)
SMEM = pl.BlockSpec(memory_space=pltpu.SMEM)
HBM = pl.BlockSpec(memory_space=pl.ANY)


def in_vmem(*arrays):
    return [pltpu.with_memory_space_constraint(t, pltpu.VMEM) for t in arrays]


def out_terms(place, attended, w_out, give):
    depth, block = w_out.shape[0], w_out.shape[1] // (2 * NX)
    heads = depth // HD
    rows = attended.shape[0] // heads
    quarter = rows // 4

    def body(place_ref, lhs_ref, w_hbm, out_ref, w, sem):
        half = 1 - place_ref[0] if give else place_ref[0]

        def copy(k):
            at = (half * NX + (place_ref[2] + k) % NX) * block
            return pltpu.make_async_copy(w_hbm.at[:, pl.ds(at, block)], w.at[k], sem.at[k])

        for k in range(NX):
            copy(k).start()
        lhs = []
        for s in range(4):
            at = (place_ref[1] ^ s) * quarter
            parts = [lhs_ref[pl.ds(h * rows + at, quarter)] for h in range(heads)]
            lhs.append(jnp.concatenate(parts, axis=1))
        lhs = jnp.concatenate(lhs, axis=0)
        for k in range(NX):
            copy(k).wait()
            out_ref[k] = dot(lhs, w[k]).astype(out_ref.dtype)

    return pl.pallas_call(
        body,
        out_shape=pltpu.VMEM((NX, rows, block), BF16 if give else F32),
        in_specs=[SMEM, VMEM, HBM],
        out_specs=VMEM,
        scratch_shapes=[
            pltpu.VMEM((NX, depth, block), BF16),
            pltpu.SemaphoreType.DMA((NX,)),
        ],
        name="out_give" if give else "out_keep",
    )(place, *in_vmem(attended), w_out)


def gate_up_terms(place, pieces, weights):
    n, part, depth = pieces[0].shape
    rows, cols, count = 4 * part, weights[0].shape[1], len(pieces)

    def body(place_ref, *refs):
        pieces, weights, refs = refs[:count], refs[count : count + n], refs[count + n :]
        give_ref, keep_ref, square_ref, w, acc, sq, sem = refs
        copies = [
            pltpu.make_async_copy(weights[k], w.at[k], sem.at[k]) for k in range(n)
        ]
        for copy in copies:
            copy.start()
        for k in range(n):
            lhs = jnp.concatenate([p[k] for p in pieces], axis=0)
            wide = lhs.astype(F32)
            square = jnp.sum(wide * wide, axis=1, keepdims=True)
            copies[k].wait()
            out = dot(lhs, w[k])
            if k == 0:
                acc[...], sq[...] = out, jnp.broadcast_to(square, sq.shape)
            else:
                acc[...] += out
                sq[...] += square
        keep = pl.multiple_of((place_ref[3] ^ place_ref[0]) * rows, rows)
        give = pl.multiple_of(((1 - place_ref[3]) ^ place_ref[0]) * rows, rows)
        give_ref[:, :cols] = acc[pl.ds(give, rows)].astype(BF16)
        square = sq[pl.ds(give, rows)]
        top = square.astype(BF16)
        low = (square - top.astype(F32)).astype(BF16)
        lane = lax.broadcasted_iota(jnp.int32, square.shape, 1)
        give_ref[:, cols:] = jnp.where(lane == 0, top.astype(F32), low.astype(F32)).astype(BF16)
        keep_ref[...] = acc[pl.ds(keep, rows)]
        square_ref[...] = sq[pl.ds(keep, rows)]

    return pl.pallas_call(
        body,
        out_shape=[
            pltpu.VMEM((rows, cols + 128), BF16),
            pltpu.VMEM((rows, cols), F32),
            pltpu.VMEM((rows, 128), F32),
        ],
        in_specs=[SMEM] + [VMEM] * count + [HBM] * n,
        out_specs=[VMEM] * 3,
        scratch_shapes=[
            pltpu.VMEM((n, depth, cols), BF16),
            pltpu.VMEM((2 * rows, cols), F32),
            pltpu.VMEM((2 * rows, 128), F32),
            pltpu.SemaphoreType.DMA((n,)),
        ],
        name="gate_up",
    )(place, *in_vmem(*pieces), *weights)


def hidden_units(keep, square, sent, dim):
    rows, cols = keep.shape

    def body(keep_ref, square_ref, sent_ref, out_ref):
        extra = sent_ref[:, cols:].astype(F32)
        mean = (square_ref[:, :1] + extra[:, :1] + extra[:, 1:2]) / dim
        out = (keep_ref[...] + sent_ref[:, :cols].astype(F32)) * lax.rsqrt(mean + EPS)
        gate, up = out[:, : cols // 2], out[:, cols // 2 :]
        out_ref[...] = (gate / (1.0 + jnp.exp(-gate)) * up).astype(BF16)

    return pl.pallas_call(
        body,
        out_shape=pltpu.VMEM((rows, cols // 2), BF16),
        in_specs=[VMEM] * 3,
        out_specs=VMEM,
        name="hidden",
    )(*in_vmem(keep, square, sent))


def down_terms(place, hidden, other, weights, give):
    n, rows = len(weights), hidden.shape[0]
    depth, cols = weights[0].shape

    def body(place_ref, hidden_ref, other_ref, *refs):
        weights, out_ref, w, sem = refs[:n], refs[n], refs[n + 1], refs[n + 2]
        copies = [
            pltpu.make_async_copy(weights[k], w.at[k], sem.at[k]) for k in range(n)
        ]
        for copy in copies:
            copy.start()
        same = place_ref[0] == place_ref[3]
        own = jnp.logical_not(same) if give else same
        lhs = jnp.where(own, hidden_ref[...], other_ref[...])
        for k in range(n):
            copies[k].wait()
            out_ref[k] = dot(lhs, w[k]).astype(out_ref.dtype)

    return pl.pallas_call(
        body,
        out_shape=pltpu.VMEM((n, rows, cols), BF16 if give else F32),
        in_specs=[SMEM, VMEM, VMEM] + [HBM] * n,
        out_specs=VMEM,
        scratch_shapes=[pltpu.VMEM((n, depth, cols), BF16), pltpu.SemaphoreType.DMA((n,))],
        name="down_give" if give else "down_keep",
    )(place, *in_vmem(hidden, other), *weights)


def rope_tables(positions):
    half = HD // 2
    frequency = THETA ** (-jnp.arange(half, dtype=F32) * 2.0 / HD)
    angles = positions.astype(F32)[:, None] * frequency[None, :]
    return jnp.cos(angles), jnp.sin(angles)


def pick(array, index, axis=0):
    return lax.dynamic_index_in_dim(array, index, axis, keepdims=False)


def from_x(array, r):
    return lax.ppermute(array, "x", [(i, (i - r) % NX) for i in range(NX)])


def project(place, pieces, gains, w_query, w_keyval, sums):
    arrays = [piece for piece, _, _ in pieces]
    n_z, rows, width = arrays[0].shape
    n_q, n_kv = w_query.shape[1], w_keyval.shape[0]
    steps = n_z * len(arrays)
    last = sums is not None

    def body(place_ref, gain_ref, wq_hbm, wkv_hbm, *refs):
        refs, rest = refs[: len(arrays)], refs[len(arrays) :]
        before, rest = (rest[:3], rest[3:]) if last else (None, rest)
        q_ref, kv_ref, sq_ref, wq, wkv, sem_q, sem_kv = rest

        def at(i):
            _, s, rc = pieces[i // n_z]
            return ((place_ref[0] ^ rc) * n_z + i % n_z) * 4 + (place_ref[1] ^ s)

        def copies(i):
            g = at(i) * width
            return (
                pltpu.make_async_copy(wq_hbm.at[pl.ds(g, width)], wq.at[i], sem_q.at[i]),
                pltpu.make_async_copy(wkv_hbm.at[:, pl.ds(g, width)], wkv.at[i], sem_kv.at[i]),
            )

        for i in range(steps):
            for copy in copies(i):
                copy.start()
        if last:
            for ref, old in zip((q_ref, kv_ref, sq_ref), before):
                ref[...] = old[...]
        else:
            for ref in (q_ref, kv_ref, sq_ref):
                ref[...] = jnp.zeros(ref.shape, F32)
        for p, ref in enumerate(refs):
            q, kv = q_ref[...], kv_ref[...]
            for r in range(n_z):
                i = p * n_z + r
                piece = ref[r].astype(F32)
                lhs = (piece * gain_ref[at(i)]).astype(BF16)
                sq_ref[...] += piece * piece
                for copy in copies(i):
                    copy.wait()
                q, kv = q + dot(lhs, wq[i]), kv + dot_t(wkv[i], lhs)
            q_ref[...], kv_ref[...] = q, kv
        if last:
            mean = jnp.sum(sq_ref[...], axis=1, keepdims=True) / (32 * width)
            factor = lax.rsqrt(mean + EPS)
            q_ref[...] = q_ref[...] * factor
            across = jnp.broadcast_to(factor, (rows, rows)).T[:1]
            kv_ref[...] = kv_ref[...] * across

    shapes = [(rows, n_q), (n_kv, rows), (rows, width)]
    return pl.pallas_call(
        body,
        out_shape=[pltpu.VMEM(shape, F32) for shape in shapes],
        in_specs=[SMEM, VMEM, HBM, HBM] + [VMEM] * (len(arrays) + (3 if last else 0)),
        out_specs=[VMEM] * 3,
        scratch_shapes=[
            pltpu.VMEM((steps, width, n_q), BF16),
            pltpu.VMEM((steps, n_kv, width), BF16),
            pltpu.SemaphoreType.DMA((steps,)),
            pltpu.SemaphoreType.DMA((steps,)),
        ],
        name="project_last" if last else "project_first",
    )(place, *in_vmem(gains), w_query, w_keyval, *in_vmem(*arrays, *(sums or ())))


def summed(terms, sent):
    quarter = terms.shape[1] // 4

    def both(s):
        rows = slice(s * quarter, (s + 1) * quarter)
        return terms[:, rows] + sent[:, rows].astype(F32)

    got = [from_sq(both(s).astype(BF16), s) for s in (1, 2, 3)]
    mine = both(0) + sum(t.astype(F32) for t in got)
    tiles = exchange(mine.astype(BF16), "zh")
    return tiles.astype(F32).sum(axis=0)


def gathered(piece):
    near = to_all(piece, "zh")
    ours = [near] + [from_sq(near, s) for s in (1, 2, 3)]
    theirs = [lax.ppermute(t, "c", SWAP) for t in ours]
    return ours, theirs


def layer(tokens_in, gain_attn, w_query, w_keyval, w_out, gain_mlp, w_gate, w_up, w_down):
    core, y_hi, x = lax.axis_index("c"), lax.axis_index("yh"), lax.axis_index("x")
    z_hi, z_lo, y_lo = lax.axis_index("zh"), lax.axis_index("zl"), lax.axis_index("yl")
    block, spot = lax.axis_index(DP), z_lo * 2 + y_lo
    rows, width = tokens_in.shape
    n_dp, n_z = lax.axis_size(DP), lax.axis_size(Z)
    dim = w_query.shape[0]
    block_d = dim // 8
    total = rows * n_dp
    quarter = rows // 4

    down_next, down_last = from_x(w_down, 1), from_x(w_down, 3)
    gain_cols = lax.dynamic_slice_in_dim(gain_mlp, block * block_d, block_d, 0)
    gate_up_w = jnp.concatenate([w_gate, w_up], axis=1).astype(F32)
    gate_up_w = (gate_up_w * gain_cols.astype(F32)[:, None]).astype(BF16)
    gate_up_all = [gate_up_w] + [from_x(gate_up_w, r) for r in range(1, NX)]
    down_all = [w_down, down_next, from_x(w_down, 2), down_last]

    ours, theirs = gathered(tokens_in)
    place = jnp.stack([core, spot, x, y_hi]).astype(jnp.int32)
    gains = gain_attn.astype(F32).reshape(4 * n_z, 1, width)
    pieces = [(t, s, rc) for rc, side in ((0, ours), (1, theirs)) for s, t in enumerate(side)]
    early = [p for p in pieces if p[1] == 0]
    late = [p for p in pieces if p[1] != 0]
    w_kv = w_keyval.T
    sums = project(place, early, gains, w_query, w_kv, None)
    query, kv_part, _ = project(place, late, gains, w_query, w_kv, sums)

    kv_here = kv_part.astype(BF16)
    parts = []
    for t in range(4):
        parts.append(
            move(
                kv_here,
                lambda c, zh, zl, yl, t=t, **_: {
                    "c": zh // 2,
                    "zh": (zh % 2) * 2 + zl,
                    "zl": c ^ (t >> 1),
                    "yl": yl ^ (t & 1),
                },
            )
        )
    parts = jnp.stack(parts, axis=0)
    parts = jnp.concatenate([pick(parts, j ^ spot) for j in range(4)], axis=0)
    parts = jnp.stack([parts, lax.ppermute(parts, "yh", SWAP)], axis=0)
    parts = jnp.stack([parts] + [from_x(parts, r) for r in range(1, NX)], axis=0)
    parts = parts.reshape(n_dp, 2, HD, rows)
    key_t = jnp.moveaxis(parts[:, 0], 0, 1).reshape(HD, total)
    value_t = jnp.moveaxis(parts[:, 1], 0, 1).reshape(HD, total)

    blocks = jnp.stack(
        [(y_hi ^ ry) * NX + (x + r) % NX for r in range(NX) for ry in range(2)]
    )
    key_pos = blocks.astype(jnp.int32)[:, None] * rows + jnp.arange(rows, dtype=jnp.int32)
    key_pos = key_pos.reshape(total)
    cos_k, sin_k = rope_tables(key_pos)
    cos_k, sin_k = cos_k.T, sin_k.T
    k1, k2 = key_t[: HD // 2].astype(F32), key_t[HD // 2 :].astype(F32)
    key_rot = jnp.concatenate(
        [k1 * cos_k - k2 * sin_k, k2 * cos_k + k1 * sin_k], axis=0
    ).astype(BF16)
    pos = block * rows + jnp.arange(rows, dtype=jnp.int32)
    cos_q, sin_q = rope_tables(pos)
    heads = w_query.shape[1] // HD
    q_rot = []
    for h in range(heads):
        q1 = query[:, h * HD : h * HD + HD // 2]
        q2 = query[:, h * HD + HD // 2 : (h + 1) * HD]
        q_rot.append(jnp.concatenate([q1 * cos_q - q2 * sin_q, q2 * cos_q + q1 * sin_q], axis=1))
    q_rot = jnp.concatenate(q_rot, axis=0).astype(BF16)
    scores = dot(q_rot, key_rot) * HD ** (-0.5)
    allowed = key_pos[None, :] <= jnp.tile(pos, heads)[:, None]
    scores = jnp.where(allowed, scores, -1e30)
    expo = jnp.exp(scores - jnp.max(scores, axis=-1, keepdims=True))
    probs = (expo / jnp.sum(expo, axis=-1, keepdims=True)).astype(BF16)
    attended = lax.dot_general(
        probs, value_t, (((1,), (1,)), ((), ())), preferred_element_type=F32
    ).astype(BF16)
    sent = lax.ppermute(out_terms(place, attended, w_out, True), "c", SWAP)
    terms = out_terms(place, attended, w_out, False)
    resid = [
        lax.dynamic_slice(t, ((x + z_hi) % NX, spot * quarter, 0), (1, quarter, width))[0]
        for t in ours
    ]
    resid = jnp.stack(resid, axis=0)
    resid = jnp.concatenate([pick(resid, j ^ spot) for j in range(4)], axis=1)
    mid_part = (resid.astype(F32) + summed(terms, sent)).astype(BF16)
    mid_own = move(mid_part, lambda c, yh, **_: {"c": yh, "yh": c})

    ours, theirs = gathered(mid_own)

    sent, keep, square = gate_up_terms(place, ours + theirs, gate_up_all)
    sent = lax.ppermute(sent, "yh", SWAP)
    hidden = hidden_units(keep, square, sent, dim)

    other = lax.ppermute(hidden, "yh", SWAP)
    sent = down_terms(place, hidden, other, down_all, True)
    sent = lax.ppermute(sent, "c", SWAP)
    terms = down_terms(place, hidden, other, down_all, False)
    done = (mid_own.astype(F32) + summed(terms, sent)).astype(BF16)
    return move(done, lambda x, zh, **_: {"x": (x + zh) % NX, "zh": x})


def solution(mesh):
    fine = Mesh(mesh.devices.reshape(SIZES), EVERY)
    placed = (
        P(DP, GROUP),
        P(),
        P(None, GROUP),
        P(None, GROUP),
        P(GROUP, None),
        P(),
        P(DP, GROUP),
        P(DP, GROUP),
        P(GROUP, DP),
    )
    return jax.shard_map(layer, mesh=fine, in_specs=placed, out_specs=P(GROUP, DP), check_vma=False)
```

profile of v0, /device:TPU:28, one launch (start us, length us, event | category | flops | bytes accessed | tf_op | source)
XLA Modules:
  0.0 282.9 jit_solution(4556591086794083774)
XLA Ops:
  1.6 8.5 %all-to-all-start = ((bf16[4,128,256]{2,1,0:T(8,128)(2,1)}), bf16[4,128,256]{2,1,0:T(8,128)(2,1)S(1)}, u32[]{:S(2)}, u32[]{:S(2)}) async-start(bf16[4,128,256]{2,1,0:T(8,128)(2,1)} %broadcast_in_dim.7), calls=%async_computation | async-start | bytes 524288 | tf_op jit(solution)/shard_map/all_to_all | solution.py:39
  10.1 10.6 %all-to-all-done.refs_0_ = bf16[4,128,256]{2,1,0:T(8,128)(2,1)S(1)} async-done(((bf16[4,128,256]{2,1,0:T(8,128)(2,1)}), bf16[4,128,256]{2,1,0:T(8,128)(2,1)S(1)}, u32[]{:S(2)}, u32[]{:S(2)}) %all-to-all-start) | async-done | bytes 262176 | tf_op jit(solution)/shard_map/all_to_all | solution.py:39
  24.2 5.7 %collective-permute-done.refs_0_ = bf16[4,128,256]{2,1,0:T(8,128)(2,1)S(1)} collective-permute-done((bf16[4,128,256]{2,1,0:T(8,128)(2,1)S(1)}, bf16[4,128,256]{2,1,0:T(8,128)(2,1)S(1)}, u32[]{:S(2)}, u32[]{:S(2)}) %collective-permute-start) | collective-permute-done | bytes 262176 | tf_op jit(solution)/shard_map/ppermute | solution.py:43
  36.8 4.7 %project_last.1 = (f32[128,256]{1,0:T(8,128)S(1)}, f32[64,128]{1,0:T(8,128)S(1)}, f32[128,256]{1,0:T(8,128)}) custom-call(s32[4]{0:T(128)} %pad_add_fusion.place_ref, f32[32,1,256]{2,1,0:T(1,128)S(1)} %bitcast.70, bf16[8192,256]{1,0:T(8,128)(2,1)} %wq_hbm.3, bf16[64,8192]{1,0:T(8,128)(2,1)} %bitcast.72, ...), custom_call_target="tpu_custom_call" | custom-call | tf_op jit(solution)/shard_map/project_last/pallas_call | solution.py:273
  43.0 3.7 %collective-permute-start.9 = (bf16[64,128]{1,0:T(8,128)(2,1)S(1)}, bf16[64,128]{1,0:T(8,128)(2,1)S(1)}, u32[]{:S(2)}, u32[]{:S(2)}) collective-permute-start(bf16[64,128]{1,0:T(8,128)(2,1)S(1)} %convert_element_type.133), channel_id=1, source_target_pairs={{0,2},{1,3},{2,6},{3,7},{4,10},{5,11},{6,14},{7,15},{8,130},{9,131... | collective-permute-start | bytes 49160 | tf_op jit(solution)/shard_map/ppermute | solution.py:57
  46.7 3.9 %collective-permute-start.10 = (bf16[64,128]{1,0:T(8,128)(2,1)S(1)}, bf16[64,128]{1,0:T(8,128)(2,1)S(1)}, u32[]{:S(2)}, u32[]{:S(2)}) collective-permute-start(bf16[64,128]{1,0:T(8,128)(2,1)S(1)} %convert_element_type.133), channel_id=1, source_target_pairs={{0,3},{1,2},{2,7},{3,6},{4,11},{5,10},{6,15},{7,14},{8,131},{9,130... | collective-permute-start | bytes 49160 | tf_op jit(solution)/shard_map/ppermute | solution.py:57
  53.5 4.5 %collective-permute-done.11 = bf16[256,128]{1,0:T(8,128)(2,1)S(1)} collective-permute-done((bf16[256,128]{1,0:T(8,128)(2,1)S(1)}, bf16[256,128]{1,0:T(8,128)(2,1)S(1)}, u32[]{:S(2)}, u32[]{:S(2)}) %collective-permute-start.11) | collective-permute-done | bytes 65568 | tf_op jit(solution)/shard_map/ppermute | solution.py:352
  92.0 5.9 %collective-permute-done.17 = bf16[4,32,1024]{2,1,0:T(8,128)(2,1)S(1)} collective-permute-done((bf16[4,32,1024]{2,1,0:T(8,128)(2,1)S(1)}, bf16[4,32,1024]{2,1,0:T(8,128)(2,1)S(1)}, u32[]{:S(2)}, u32[]{:S(2)}) %collective-permute-start.17) | collective-permute-done | bytes 262176 | tf_op jit(solution)/shard_map/ppermute | solution.py:43
  97.8 4.5 %collective-permute-done.18 = bf16[4,32,1024]{2,1,0:T(8,128)(2,1)} collective-permute-done((bf16[4,32,1024]{2,1,0:T(8,128)(2,1)S(1)}, bf16[4,32,1024]{2,1,0:T(8,128)(2,1)}, u32[]{:S(2)}, u32[]{:S(2)}) %collective-permute-start.18) | collective-permute-done | bytes 262176 | tf_op jit(solution)/shard_map/ppermute | solution.py:43
  104.3 6.4 %all-to-all-start.1 = ((bf16[4,32,1024]{2,1,0:T(8,128)(2,1)}), bf16[4,32,1024]{2,1,0:T(8,128)(2,1)S(1)}, u32[]{:S(2)}, u32[]{:S(2)}) async-start(bf16[4,32,1024]{2,1,0:T(8,128)(2,1)} %fusion.11), calls=%async_computation.1 | async-start | bytes 524288 | tf_op jit(solution)/shard_map/all_to_all | solution.py:39
  112.1 8.6 %all-to-all-done.1 = bf16[4,32,1024]{2,1,0:T(8,128)(2,1)S(1)} async-done(((bf16[4,32,1024]{2,1,0:T(8,128)(2,1)}), bf16[4,32,1024]{2,1,0:T(8,128)(2,1)S(1)}, u32[]{:S(2)}, u32[]{:S(2)}) %all-to-all-start.1) | async-done | bytes 262176 | tf_op jit(solution)/shard_map/all_to_all | solution.py:39
  122.7 5.2 %collective-permute-done.19 = bf16[32,1024]{1,0:T(8,128)(2,1)S(1)} collective-permute-done((bf16[32,1024]{1,0:T(8,128)(2,1)S(1)}, bf16[32,1024]{1,0:T(8,128)(2,1)S(1)}, u32[]{:S(2)}, u32[]{:S(2)}) %collective-permute-start.19) | collective-permute-done | bytes 65568 | tf_op jit(solution)/shard_map/ppermute | solution.py:57
  127.9 14.5 %all_to_all.20.refs_0_ = bf16[4,32,1024]{2,1,0:T(8,128)(2,1)S(1)} all-to-all(bf16[4,32,1024]{2,1,0:T(8,128)(2,1)S(1)} %broadcast_in_dim.9), channel_id=1, replica_groups=mesh['c'=2,'yh'=2,'x'=4,'zh'=4,'zl'=2,'yl'=2] {'zh'}, dimensions={0} | all-to-all | bytes 524288 | tf_op jit(solution)/shard_map/all_to_all | solution.py:39
  145.9 30.9 %collective-permute-start.32 = (bf16[512,1024]{1,0:T(8,128)(2,1)}, bf16[512,1024]{1,0:T(8,128)(2,1)}, u32[]{:S(2)}, u32[]{:S(2)}) collective-permute-start(bf16[512,1024]{1,0:T(8,128)(2,1)} %refs_0_.3), channel_id=1, source_target_pairs={{0,48},{16,0},{32,16},{48,32},{1,49},{17,1},{33,17},{49,33},{2,50}... | collective-permute-start | bytes 3145736 | tf_op jit(solution)/shard_map/ppermute | solution.py:219
  176.9 3.8 %collective-permute-start.33 = (bf16[512,1024]{1,0:T(8,128)(2,1)}, bf16[512,1024]{1,0:T(8,128)(2,1)}, u32[]{:S(2)}, u32[]{:S(2)}) collective-permute-start(bf16[512,1024]{1,0:T(8,128)(2,1)} %refs_0_.3), channel_id=1, source_target_pairs={{0,32},{16,48},{32,0},{48,16},{1,33},{17,49},{33,1},{49,17},{2,34}... | collective-permute-start | bytes 3145736 | tf_op jit(solution)/shard_map/ppermute | solution.py:219
  184.3 4.9 %gate_up.1 = (bf16[128,1152]{1,0:T(8,128)(2,1)S(1)}, f32[128,1024]{1,0:T(8,128)S(1)}, f32[128,128]{1,0:T(8,128)S(1)}) custom-call(s32[4]{0:T(128)} %pad_add_fusion.place_ref, bf16[4,32,1024]{2,1,0:T(8,128)(2,1)S(1)} %all_to_all.20.refs_0_, bf16[4,32,1024]{2,1,0:T(8,128)(2,1)S(1)} %collective-permute-done.20.refs_1_, ...), custom_call_target="tpu_custom_call" | custom-call | tf_op jit(solution)/shard_map/gate_up/pallas_call | solution.py:141
  191.1 9.4 %collective-permute-done.30.sent_ref = bf16[128,1152]{1,0:T(8,128)(2,1)S(1)} collective-permute-done((bf16[128,1152]{1,0:T(8,128)(2,1)S(1)}, bf16[128,1152]{1,0:T(8,128)(2,1)S(1)}, u32[]{:S(2)}, u32[]{:S(2)}) %collective-permute-start.30) | collective-permute-done | bytes 294944 | tf_op jit(solution)/shard_map/ppermute | solution.py:400
  205.1 21.2 %collective-permute-done.34.refs_3_ = bf16[512,1024]{1,0:T(8,128)(2,1)} collective-permute-done((bf16[512,1024]{1,0:T(8,128)(2,1)}, bf16[512,1024]{1,0:T(8,128)(2,1)}, u32[]{:S(2)}, u32[]{:S(2)}) %collective-permute-start.34) | collective-permute-done | bytes 1048608 | tf_op jit(solution)/shard_map/ppermute | solution.py:219
  226.3 3.2 %down_give.1 = bf16[4,128,1024]{2,1,0:T(8,128)(2,1)S(1)} custom-call(s32[4]{0:T(128)} %pad_add_fusion.place_ref, bf16[128,512]{1,0:T(8,128)(2,1)S(1)} %hidden.1.hidden_ref, bf16[128,512]{1,0:T(8,128)(2,1)S(1)} %collective-permute-done.31.other_ref, bf16[512,1024]{1,0:T(8,128)(2,1)} %refs_0_.3, bf16[512,1024]{1,0:T(8,128)(2,1)} %collective-permute-done.32.refs_1_, ...), custom_call_target="tpu_custom_call" | custom-call | tf_op jit(solution)/shard_map/down_give/pallas_call | solution.py:197
  229.6 3.2 %down_keep.1 = f32[4,128,1024]{2,1,0:T(8,128)S(1)} custom-call(s32[4]{0:T(128)} %pad_add_fusion.place_ref, bf16[128,512]{1,0:T(8,128)(2,1)S(1)} %hidden.1.hidden_ref, bf16[128,512]{1,0:T(8,128)(2,1)S(1)} %collective-permute-done.31.other_ref, bf16[512,1024]{1,0:T(8,128)(2,1)} %refs_0_.3, bf16[512,1024]{1,0:T(8,128)(2,1)} %collective-permute-done.32.refs_1_, ...), custom_call_target="tpu_custom_call" | custom-call | tf_op jit(solution)/shard_map/down_keep/pallas_call | solution.py:197
  238.2 4.7 %collective-permute-done.36 = bf16[4,32,1024]{2,1,0:T(8,128)(2,1)S(1)} collective-permute-done((bf16[4,32,1024]{2,1,0:T(8,128)(2,1)S(1)}, bf16[4,32,1024]{2,1,0:T(8,128)(2,1)S(1)}, u32[]{:S(2)}, u32[]{:S(2)}) %collective-permute-start.36) | collective-permute-done | bytes 262176 | tf_op jit(solution)/shard_map/ppermute | solution.py:43
  244.8 5.8 %collective-permute-done.38 = bf16[4,32,1024]{2,1,0:T(8,128)(2,1)S(1)} collective-permute-done((bf16[4,32,1024]{2,1,0:T(8,128)(2,1)S(1)}, bf16[4,32,1024]{2,1,0:T(8,128)(2,1)S(1)}, u32[]{:S(2)}, u32[]{:S(2)}) %collective-permute-start.38) | collective-permute-done | bytes 262176 | tf_op jit(solution)/shard_map/ppermute | solution.py:43
  251.7 18.1 %all_to_all.21 = bf16[4,32,1024]{2,1,0:T(8,128)(2,1)S(1)} all-to-all(bf16[4,32,1024]{2,1,0:T(8,128)(2,1)S(1)} %fusion.6), channel_id=1, replica_groups=mesh['c'=2,'yh'=2,'x'=4,'zh'=4,'zl'=2,'yl'=2] {'zh'}, dimensions={0} | all-to-all | bytes 524288 | tf_op jit(solution)/shard_map/all_to_all | solution.py:39
  272.3 10.0 %collective-permute-done.39 = bf16[32,1024]{1,0:T(8,128)(2,1)S(1)} collective-permute-done((bf16[32,1024]{1,0:T(8,128)(2,1)S(1)}, bf16[32,1024]{1,0:T(8,128)(2,1)S(1)}, u32[]{:S(2)}, u32[]{:S(2)}) %collective-permute-start.39) | collective-permute-done | bytes 65568 | tf_op jit(solution)/shard_map/ppermute | solution.py:57
  (126 shorter events, 80.7 us)
Async XLA Ops:
  1.6 19.2 %all-to-all-start = ((bf16[4,128,256]{2,1,0:T(8,128)(2,1)}), bf16[4,128,256]{2,1,0:T(8,128)(2,1)S(1)}, u32[]{:S(2)}, u32[]{:S(2)}) async-start(bf16[4,128,256]{2,1,0:T(8,128)(2,1)} %broadcast_in_dim.7), calls=%async_computation | async-start | bytes 524288 | tf_op jit(solution)/shard_map/all_to_all | solution.py:39
  20.7 9.2 %collective-permute-start = (bf16[4,128,256]{2,1,0:T(8,128)(2,1)S(1)}, bf16[4,128,256]{2,1,0:T(8,128)(2,1)S(1)}, u32[]{:S(2)}, u32[]{:S(2)}) collective-permute-start(bf16[4,128,256]{2,1,0:T(8,128)(2,1)S(1)} %all-to-all-done.refs_0_), channel_id=1, source_target_pairs={{0,1},{1,0},{2,3},{3,2},{4,5},{5,4},{6,7},{7,6},{8,9},{9,8},{10,11... | collective-permute-start | bytes 786440 | tf_op jit(solution)/shard_map/ppermute | solution.py:43
  22.3 10.6 %collective-permute-start.2 = (bf16[4,128,256]{2,1,0:T(8,128)(2,1)S(1)}, bf16[4,128,256]{2,1,0:T(8,128)(2,1)S(1)}, u32[]{:S(2)}, u32[]{:S(2)}) collective-permute-start(bf16[4,128,256]{2,1,0:T(8,128)(2,1)S(1)} %all-to-all-done.refs_0_), channel_id=1, source_target_pairs={{0,3},{1,2},{2,1},{3,0},{4,7},{5,6},{6,5},{7,4},{8,11},{9,10},{10,... | collective-permute-start | bytes 786440 | tf_op jit(solution)/shard_map/ppermute | solution.py:43
  24.2 10.0 %collective-permute-start.6 = (bf16[4,128,256]{2,1,0:T(8,128)(2,1)S(1)}, bf16[4,128,256]{2,1,0:T(8,128)(2,1)S(1)}, u32[]{:S(2)}, u32[]{:S(2)}) collective-permute-start(bf16[4,128,256]{2,1,0:T(8,128)(2,1)S(1)} %all-to-all-done.refs_0_), channel_id=1, source_target_pairs={{0,128},{128,0},{1,129},{129,1},{2,130},{130,2},{3,131},{131,3},{4... | collective-permute-start | bytes 786440 | tf_op jit(solution)/shard_map/ppermute | solution.py:304
  41.6 9.1 %collective-permute-start.7 = (bf16[64,128]{1,0:T(8,128)(2,1)S(1)}, bf16[64,128]{1,0:T(8,128)(2,1)S(1)}, u32[]{:S(2)}, u32[]{:S(2)}) collective-permute-start(bf16[64,128]{1,0:T(8,128)(2,1)S(1)} %convert_element_type.133), channel_id=1, source_target_pairs={{0,0},{1,1},{2,4},{3,5},{4,8},{5,9},{6,12},{7,13},{8,128},{9,129},... | collective-permute-start | bytes 49160 | tf_op jit(solution)/shard_map/ppermute | solution.py:57
  79.4 11.3 %collective-permute-start.16 = (bf16[4,32,1024]{2,1,0:T(8,128)(2,1)S(1)}, bf16[4,32,1024]{2,1,0:T(8,128)(2,1)S(1)}, u32[]{:S(2)}, u32[]{:S(2)}) collective-permute-start(bf16[4,32,1024]{2,1,0:T(8,128)(2,1)S(1)} %get-tuple-element.24), channel_id=1, source_target_pairs={{0,1},{1,0},{2,3},{3,2},{4,5},{5,4},{6,7},{7,6},{8,9},{9,8},{10,11... | collective-permute-start | bytes 786440 | tf_op jit(solution)/shard_map/ppermute | solution.py:43
  82.4 62.4 %collective-permute-start.27 = (bf16[1024,1024]{1,0:T(8,128)(2,1)}, bf16[1024,1024]{1,0:T(8,128)(2,1)}, u32[]{:S(2)}, u32[]{:S(2)}) collective-permute-start(bf16[1024,1024]{1,0:T(8,128)(2,1)} %multiply_convert_fusion.refs_8_), channel_id=1, source_target_pairs={{0,48},{16,0},{32,16},{48,32},{1,49},{17,1},{33,17},{49,33},{2,50}... | collective-permute-start | bytes 6291464 | tf_op jit(solution)/shard_map/ppermute | solution.py:219
  82.8 63.1 %collective-permute-start.28 = (bf16[1024,1024]{1,0:T(8,128)(2,1)}, bf16[1024,1024]{1,0:T(8,128)(2,1)}, u32[]{:S(2)}, u32[]{:S(2)}) collective-permute-start(bf16[1024,1024]{1,0:T(8,128)(2,1)} %multiply_convert_fusion.refs_8_), channel_id=1, source_target_pairs={{0,32},{16,48},{32,0},{48,16},{1,33},{17,49},{33,1},{49,17},{2,34}... | collective-permute-start | bytes 6291464 | tf_op jit(solution)/shard_map/ppermute | solution.py:219
  85.6 91.4 %collective-permute-start.29 = (bf16[1024,1024]{1,0:T(8,128)(2,1)}, bf16[1024,1024]{1,0:T(8,128)(2,1)}, u32[]{:S(2)}, u32[]{:S(2)}) collective-permute-start(bf16[1024,1024]{1,0:T(8,128)(2,1)} %multiply_convert_fusion.refs_8_), channel_id=1, source_target_pairs={{0,16},{16,32},{32,48},{48,0},{1,17},{17,33},{33,49},{49,1},{2,18}... | collective-permute-start | bytes 6291464 | tf_op jit(solution)/shard_map/ppermute | solution.py:219
  87.7 10.1 %collective-permute-start.17 = (bf16[4,32,1024]{2,1,0:T(8,128)(2,1)S(1)}, bf16[4,32,1024]{2,1,0:T(8,128)(2,1)S(1)}, u32[]{:S(2)}, u32[]{:S(2)}) collective-permute-start(bf16[4,32,1024]{2,1,0:T(8,128)(2,1)S(1)} %get-tuple-element.26), channel_id=1, source_target_pairs={{0,2},{1,3},{2,0},{3,1},{4,6},{5,7},{6,4},{7,5},{8,10},{9,11},{10,... | collective-permute-start | bytes 786440 | tf_op jit(solution)/shard_map/ppermute | solution.py:43
  90.7 11.7 %collective-permute-start.18 = (bf16[4,32,1024]{2,1,0:T(8,128)(2,1)S(1)}, bf16[4,32,1024]{2,1,0:T(8,128)(2,1)}, u32[]{:S(2)}, u32[]{:S(2)}) collective-permute-start(bf16[4,32,1024]{2,1,0:T(8,128)(2,1)S(1)} %get-tuple-element.25), channel_id=1, source_target_pairs={{0,3},{1,2},{2,1},{3,0},{4,7},{5,6},{6,5},{7,4},{8,11},{9,10},{10,... | collective-permute-start | bytes 786440 | tf_op jit(solution)/shard_map/ppermute | solution.py:43
  104.3 16.4 %all-to-all-start.1 = ((bf16[4,32,1024]{2,1,0:T(8,128)(2,1)}), bf16[4,32,1024]{2,1,0:T(8,128)(2,1)S(1)}, u32[]{:S(2)}, u32[]{:S(2)}) async-start(bf16[4,32,1024]{2,1,0:T(8,128)(2,1)} %fusion.11), calls=%async_computation.1 | async-start | bytes 524288 | tf_op jit(solution)/shard_map/all_to_all | solution.py:39
  142.4 38.3 %collective-permute-start.20 = (bf16[4,32,1024]{2,1,0:T(8,128)(2,1)S(1)}, bf16[4,32,1024]{2,1,0:T(8,128)(2,1)S(1)}, u32[]{:S(2)}, u32[]{:S(2)}) collective-permute-start(bf16[4,32,1024]{2,1,0:T(8,128)(2,1)S(1)} %all_to_all.20.refs_0_), channel_id=1, source_target_pairs={{0,1},{1,0},{2,3},{3,2},{4,5},{5,4},{6,7},{7,6},{8,9},{9,8},{10,11... | collective-permute-start | bytes 786440 | tf_op jit(solution)/shard_map/ppermute | solution.py:43
  143.7 37.0 %collective-permute-start.21 = (bf16[4,32,1024]{2,1,0:T(8,128)(2,1)S(1)}, bf16[4,32,1024]{2,1,0:T(8,128)(2,1)S(1)}, u32[]{:S(2)}, u32[]{:S(2)}) collective-permute-start(bf16[4,32,1024]{2,1,0:T(8,128)(2,1)S(1)} %all_to_all.20.refs_0_), channel_id=1, source_target_pairs={{0,2},{1,3},{2,0},{3,1},{4,6},{5,7},{6,4},{7,5},{8,10},{9,11},{10,... | collective-permute-start | bytes 786440 | tf_op jit(solution)/shard_map/ppermute | solution.py:43
  144.8 36.0 %collective-permute-start.22 = (bf16[4,32,1024]{2,1,0:T(8,128)(2,1)S(1)}, bf16[4,32,1024]{2,1,0:T(8,128)(2,1)S(1)}, u32[]{:S(2)}, u32[]{:S(2)}) collective-permute-start(bf16[4,32,1024]{2,1,0:T(8,128)(2,1)S(1)} %all_to_all.20.refs_0_), channel_id=1, source_target_pairs={{0,3},{1,2},{2,1},{3,0},{4,7},{5,6},{6,5},{7,4},{8,11},{9,10},{10,... | collective-permute-start | bytes 786440 | tf_op jit(solution)/shard_map/ppermute | solution.py:43
  145.9 57.2 %collective-permute-start.32 = (bf16[512,1024]{1,0:T(8,128)(2,1)}, bf16[512,1024]{1,0:T(8,128)(2,1)}, u32[]{:S(2)}, u32[]{:S(2)}) collective-permute-start(bf16[512,1024]{1,0:T(8,128)(2,1)} %refs_0_.3), channel_id=1, source_target_pairs={{0,48},{16,0},{32,16},{48,32},{1,49},{17,1},{33,17},{49,33},{2,50}... | collective-permute-start | bytes 3145736 | tf_op jit(solution)/shard_map/ppermute | solution.py:219
  176.9 28.2 %collective-permute-start.33 = (bf16[512,1024]{1,0:T(8,128)(2,1)}, bf16[512,1024]{1,0:T(8,128)(2,1)}, u32[]{:S(2)}, u32[]{:S(2)}) collective-permute-start(bf16[512,1024]{1,0:T(8,128)(2,1)} %refs_0_.3), channel_id=1, source_target_pairs={{0,32},{16,48},{32,0},{48,16},{1,33},{17,49},{33,1},{49,17},{2,34}... | collective-permute-start | bytes 3145736 | tf_op jit(solution)/shard_map/ppermute | solution.py:219
  180.7 45.6 %collective-permute-start.34 = (bf16[512,1024]{1,0:T(8,128)(2,1)}, bf16[512,1024]{1,0:T(8,128)(2,1)}, u32[]{:S(2)}, u32[]{:S(2)}) collective-permute-start(bf16[512,1024]{1,0:T(8,128)(2,1)} %refs_0_.3), channel_id=1, source_target_pairs={{0,16},{16,32},{32,48},{48,0},{1,17},{17,33},{33,49},{49,1},{2,18}... | collective-permute-start | bytes 3145736 | tf_op jit(solution)/shard_map/ppermute | solution.py:219
  190.0 10.6 %collective-permute-start.30 = (bf16[128,1152]{1,0:T(8,128)(2,1)S(1)}, bf16[128,1152]{1,0:T(8,128)(2,1)S(1)}, u32[]{:S(2)}, u32[]{:S(2)}) collective-permute-start(bf16[128,1152]{1,0:T(8,128)(2,1)S(1)} %get-tuple-element.20), channel_id=1, source_target_pairs={{0,64},{64,0},{1,65},{65,1},{2,66},{66,2},{3,67},{67,3},{4,68},{68... | collective-permute-start | bytes 884744 | tf_op jit(solution)/shard_map/ppermute | solution.py:400
  201.8 24.5 %collective-permute-start.31 = (bf16[128,512]{1,0:T(8,128)(2,1)S(1)}, bf16[128,512]{1,0:T(8,128)(2,1)S(1)}, u32[]{:S(2)}, u32[]{:S(2)}) collective-permute-start(bf16[128,512]{1,0:T(8,128)(2,1)S(1)} %hidden.1.hidden_ref), channel_id=1, source_target_pairs={{0,64},{64,0},{1,65},{65,1},{2,66},{66,2},{3,67},{67,3},{4,68},{68... | collective-permute-start | bytes 393224 | tf_op jit(solution)/shard_map/ppermute | solution.py:403
  234.2 8.8 %collective-permute-start.36 = (bf16[4,32,1024]{2,1,0:T(8,128)(2,1)S(1)}, bf16[4,32,1024]{2,1,0:T(8,128)(2,1)S(1)}, u32[]{:S(2)}, u32[]{:S(2)}) collective-permute-start(bf16[4,32,1024]{2,1,0:T(8,128)(2,1)S(1)} %get-tuple-element.21), channel_id=1, source_target_pairs={{0,1},{1,0},{2,3},{3,2},{4,5},{5,4},{6,7},{7,6},{8,9},{9,8},{10,11... | collective-permute-start | bytes 786440 | tf_op jit(solution)/shard_map/ppermute | solution.py:43
  235.3 9.4 %collective-permute-start.37 = (bf16[4,32,1024]{2,1,0:T(8,128)(2,1)S(1)}, bf16[4,32,1024]{2,1,0:T(8,128)(2,1)S(1)}, u32[]{:S(2)}, u32[]{:S(2)}) collective-permute-start(bf16[4,32,1024]{2,1,0:T(8,128)(2,1)S(1)} %get-tuple-element.23), channel_id=1, source_target_pairs={{0,2},{1,3},{2,0},{3,1},{4,6},{5,7},{6,4},{7,5},{8,10},{9,11},{10,... | collective-permute-start | bytes 786440 | tf_op jit(solution)/shard_map/ppermute | solution.py:43
  237.6 12.9 %collective-permute-start.38 = (bf16[4,32,1024]{2,1,0:T(8,128)(2,1)S(1)}, bf16[4,32,1024]{2,1,0:T(8,128)(2,1)S(1)}, u32[]{:S(2)}, u32[]{:S(2)}) collective-permute-start(bf16[4,32,1024]{2,1,0:T(8,128)(2,1)S(1)} %get-tuple-element.22), channel_id=1, source_target_pairs={{0,3},{1,2},{2,1},{3,0},{4,7},{5,6},{6,5},{7,4},{8,11},{9,10},{10,... | collective-permute-start | bytes 786440 | tf_op jit(solution)/shard_map/ppermute | solution.py:43
  269.8 12.5 %collective-permute-start.39 = (bf16[32,1024]{1,0:T(8,128)(2,1)S(1)}, bf16[32,1024]{1,0:T(8,128)(2,1)S(1)}, u32[]{:S(2)}, u32[]{:S(2)}) collective-permute-start(bf16[32,1024]{1,0:T(8,128)(2,1)S(1)} %add_convert_fusion), channel_id=1, source_target_pairs={{0,0},{1,1},{2,2},{3,3},{4,16},{5,17},{6,18},{7,19},{8,32},{9,33},... | collective-permute-start | bytes 196616 | tf_op jit(solution)/shard_map/ppermute | solution.py:57
  (25 other events, 121.0 us)
where the time goes:
time: 284 us; the launch traced here: 283 us
  waiting for transfers between devices  114 us (40%)
  starting transfers between devices  92.7 us (33%)
  blocking collectives  32.6 us (11%)
  Pallas kernels  24.1 us (8%)
  other arithmetic  11.9 us (4%)
  local copies, waits for them, and re-layouts  6.56 us (2%)
    ppermute x9, starting transfers between devices, from_x(): return lax.ppermute(array, 'x', [(i, (i - r) % NX) for i in range(NX)])  43.3 us
    all_to_all x2, blocking collectives, exchange(): return lax.all_to_all(tiles, axis, 0, 0, tiled=True)  32.6 us
    ppermute x12, waiting for transfers between devices, from_sq(): return lax.ppermute(array, ('zl', 'yl'), [(i, i ^ s) for i in range(4)])  30.8 us
    ppermute x9, waiting for transfers between devices, from_x(): return lax.ppermute(array, 'x', [(i, (i - r) % NX) for i in range(NX)])  30.7 us
    all_to_all x2, waiting for transfers between devices, exchange(): return lax.all_to_all(tiles, axis, 0, 0, tiled=True)  19.2 us
    ppermute x6, waiting for transfers between devices, move(): return lax.ppermute(array, EVERY, moves)  16.6 us
    ppermute x12, starting transfers between devices, from_sq(): return lax.ppermute(array, ('zl', 'yl'), [(i, i ^ s) for i in range(4)])  15.8 us
    all_to_all x2, starting transfers between devices, exchange(): return lax.all_to_all(tiles, axis, 0, 0, tiled=True)  14.8 us
  transfers between devices with their start and end apart: 42, of which 24 were waited for; matrix products, arithmetic and copies ran while one was open for 3% of the time, Pallas kernels for 5%

commit v1 on v0

--- a/solution.py
+++ b/solution.py
@@ -104,11 +104,11 @@
     )(place, *in_vmem(attended), w_out)
 
 
-def gate_up_terms(place, pieces, weights):
+def gate_up_terms(place, gains, pieces, weights):
     n, part, depth = pieces[0].shape
     rows, cols, count = 4 * part, weights[0].shape[1], len(pieces)
 
-    def body(place_ref, *refs):
+    def body(place_ref, gain_ref, *refs):
         pieces, weights, refs = refs[:count], refs[count : count + n], refs[count + n :]
         give_ref, keep_ref, square_ref, w, acc, sq, sem = refs
         copies = [
@@ -121,7 +121,8 @@
             wide = lhs.astype(F32)
             square = jnp.sum(wide * wide, axis=1, keepdims=True)
             copies[k].wait()
-            out = dot(lhs, w[k])
+            gain = gain_ref[place_ref[3] * n + (place_ref[2] + k) % n]
+            out = dot((wide * gain).astype(BF16), w[k])
             if k == 0:
                 acc[...], sq[...] = out, jnp.broadcast_to(square, sq.shape)
             else:
@@ -142,10 +143,10 @@
         body,
         out_shape=[
             pltpu.VMEM((rows, cols + 128), BF16),
-            pltpu.VMEM((rows, cols), F32),
-            pltpu.VMEM((rows, 128), F32),
+            jax.ShapeDtypeStruct((rows, cols), F32),
+            jax.ShapeDtypeStruct((rows, 128), F32),
         ],
-        in_specs=[SMEM] + [VMEM] * count + [HBM] * n,
+        in_specs=[SMEM, VMEM] + [VMEM] * count + [HBM] * n,
         out_specs=[VMEM] * 3,
         scratch_shapes=[
             pltpu.VMEM((n, depth, cols), BF16),
@@ -154,7 +155,7 @@
             pltpu.SemaphoreType.DMA((n,)),
         ],
         name="gate_up",
-    )(place, *in_vmem(*pieces), *weights)
+    )(place, gains, *in_vmem(*pieces), *weights)
 
 
 def hidden_units(keep, square, sent, dim):
@@ -173,7 +174,7 @@
         in_specs=[VMEM] * 3,
         out_specs=VMEM,
         name="hidden",
-    )(*in_vmem(keep, square, sent))
+    )(keep, square, *in_vmem(sent))
 
 
 def down_terms(place, hidden, other, weights, give):
@@ -316,11 +317,10 @@
     total = rows * n_dp
     quarter = rows // 4
 
+    gate_up_w = jnp.concatenate([w_gate, w_up], axis=1)
+    gate_up_next, gate_up_last = from_x(gate_up_w, 1), from_x(gate_up_w, 3)
+    gate_up_all = [gate_up_w, gate_up_next, from_x(gate_up_w, 2), gate_up_last]
     down_next, down_last = from_x(w_down, 1), from_x(w_down, 3)
-    gain_cols = lax.dynamic_slice_in_dim(gain_mlp, block * block_d, block_d, 0)
-    gate_up_w = jnp.concatenate([w_gate, w_up], axis=1).astype(F32)
-    gate_up_w = (gate_up_w * gain_cols.astype(F32)[:, None]).astype(BF16)
-    gate_up_all = [gate_up_w] + [from_x(gate_up_w, r) for r in range(1, NX)]
     down_all = [w_down, down_next, from_x(w_down, 2), down_last]
 
     ours, theirs = gathered(tokens_in)
@@ -333,33 +333,15 @@
     sums = project(place, early, gains, w_query, w_kv, None)
     query, kv_part, _ = project(place, late, gains, w_query, w_kv, sums)
 
-    kv_here = kv_part.astype(BF16)
-    parts = []
-    for t in range(4):
-        parts.append(
-            move(
-                kv_here,
-                lambda c, zh, zl, yl, t=t, **_: {
-                    "c": zh // 2,
-                    "zh": (zh % 2) * 2 + zl,
-                    "zl": c ^ (t >> 1),
-                    "yl": yl ^ (t & 1),
-                },
-            )
-        )
-    parts = jnp.stack(parts, axis=0)
-    parts = jnp.concatenate([pick(parts, j ^ spot) for j in range(4)], axis=0)
-    parts = jnp.stack([parts, lax.ppermute(parts, "yh", SWAP)], axis=0)
-    parts = jnp.stack([parts] + [from_x(parts, r) for r in range(1, NX)], axis=0)
-    parts = parts.reshape(n_dp, 2, HD, rows)
+    kv_here = move(
+        kv_part.astype(BF16),
+        lambda c, zh, zl, **_: {"c": zh // 2, "zh": (zh % 2) * 2 + zl, "zl": c},
+    )
+    parts = to_all(kv_here, ("yh", "x", "zl", "yl")).reshape(n_dp, 2, HD, rows)
     key_t = jnp.moveaxis(parts[:, 0], 0, 1).reshape(HD, total)
     value_t = jnp.moveaxis(parts[:, 1], 0, 1).reshape(HD, total)
 
-    blocks = jnp.stack(
-        [(y_hi ^ ry) * NX + (x + r) % NX for r in range(NX) for ry in range(2)]
-    )
-    key_pos = blocks.astype(jnp.int32)[:, None] * rows + jnp.arange(rows, dtype=jnp.int32)
-    key_pos = key_pos.reshape(total)
+    key_pos = jnp.arange(total, dtype=jnp.int32)
     cos_k, sin_k = rope_tables(key_pos)
     cos_k, sin_k = cos_k.T, sin_k.T
     k1, k2 = key_t[: HD // 2].astype(F32), key_t[HD // 2 :].astype(F32)
@@ -396,7 +378,8 @@
 
     ours, theirs = gathered(mid_own)
 
-    sent, keep, square = gate_up_terms(place, ours + theirs, gate_up_all)
+    gains_mlp = gain_mlp.astype(F32).reshape(n_dp, 1, block_d)
+    sent, keep, square = gate_up_terms(place, gains_mlp, ours + theirs, gate_up_all)
     sent = lax.ppermute(sent, "yh", SWAP)
     hidden = hidden_units(keep, square, sent, dim)
 

time: 284 us -> 279 us (0.982)
  the two profiles are of different devices: /device:TPU:28 before, /device:TPU:4 now
where the time goes in v1:
time: 279 us; the launch traced here: 278 us
  waiting for transfers between devices  137 us (49%)
  starting transfers between devices  48.9 us (18%)
  blocking collectives  46.9 us (17%)
  Pallas kernels  26.2 us (9%)
  other arithmetic  10.7 us (4%)
  local copies, waits for them, and re-layouts  7.07 us (3%)
    ppermute x6, waiting for transfers between devices, from_x(): return lax.ppermute(array, 'x', [(i, (i - r) % NX) for i in range(NX)])  65 us
    all_to_all x3, blocking collectives, exchange(): return lax.all_to_all(tiles, axis, 0, 0, tiled=True)  46.9 us
    ppermute x12, waiting for transfers between devices, from_sq(): return lax.ppermute(array, ('zl', 'yl'), [(i, i ^ s) for i in range(4)])  33.2 us
    all_to_all x2, waiting for transfers between devices, exchange(): return lax.all_to_all(tiles, axis, 0, 0, tiled=True)  17.6 us
    all_to_all x2, starting transfers between devices, exchange(): return lax.all_to_all(tiles, axis, 0, 0, tiled=True)  17.4 us
    ppermute x12, starting transfers between devices, from_sq(): return lax.ppermute(array, ('zl', 'yl'), [(i, i ^ s) for i in range(4)])  11.4 us
    ppermute x6, starting transfers between devices, from_x(): return lax.ppermute(array, 'x', [(i, (i - r) % NX) for i in range(NX)])  10.3 us
    ppermute x1, waiting for transfers between devices, layer(): sent = lax.ppermute(sent, 'yh', SWAP)  9.65 us
  transfers between devices with their start and end apart: 35, of which 21 were waited for; matrix products, arithmetic and copies ran while one was open for 3% of the time, Pallas kernels for 6%

profile of v1, /device:TPU:4, one launch (start us, length us, event | category | flops | bytes accessed | tf_op | source)
XLA Modules:
  0.0 277.6 jit_solution(7148380072495581509)
XLA Ops:
  0.9 19.3 %all_to_all.25.refs_0_ = bf16[4,128,256]{2,1,0:T(8,128)(2,1)S(1)} all-to-all(bf16[4,128,256]{2,1,0:T(8,128)(2,1)S(1)} %broadcast_in_dim.9), channel_id=1, replica_groups=mesh['c'=2,'yh'=2,'x'=4,'zh'=4,'zl'=2,'yl'=2] {'zh'}, dimensions={0} | all-to-all | bytes 524288 | tf_op jit(solution)/shard_map/all_to_all | solution.py:39
  23.7 5.7 %collective-permute-done.refs_0_ = bf16[4,128,256]{2,1,0:T(8,128)(2,1)S(1)} collective-permute-done((bf16[4,128,256]{2,1,0:T(8,128)(2,1)S(1)}, bf16[4,128,256]{2,1,0:T(8,128)(2,1)S(1)}, u32[]{:S(2)}, u32[]{:S(2)}) %collective-permute-start) | collective-permute-done | bytes 262176 | tf_op jit(solution)/shard_map/ppermute | solution.py:43
  30.1 2.7 collective-permute-done.2.refs_2_
  36.7 4.7 %project_last.1 = (f32[128,256]{1,0:T(8,128)S(1)}, f32[64,128]{1,0:T(8,128)S(1)}, f32[128,256]{1,0:T(8,128)}) custom-call(s32[4]{0:T(128)} %pad_add_fusion.place_ref, f32[32,1,256]{2,1,0:T(1,128)S(1)} %bitcast.39, bf16[8192,256]{1,0:T(8,128)(2,1)} %wq_hbm.3, bf16[64,8192]{1,0:T(8,128)(2,1)} %bitcast.41, ...), custom_call_target="tpu_custom_call" | custom-call | tf_op jit(solution)/shard_map/project_last/pallas_call | solution.py:274
  43.0 12.9 %all-to-all-start.1 = ((bf16[32,64,128]{2,1,0:T(8,128)(2,1)}), bf16[32,64,128]{2,1,0:T(8,128)(2,1)S(1)}, u32[]{:S(2)}, u32[]{:S(2)}) async-start(bf16[32,64,128]{2,1,0:T(8,128)(2,1)} %broadcast_in_dim.10), calls=%async_computation.1 | async-start | bytes 1048576 | tf_op jit(solution)/shard_map/all_to_all | solution.py:39
  56.3 8.3 %all-to-all-done.1 = bf16[32,64,128]{2,1,0:T(8,128)(2,1)S(1)} async-done(((bf16[32,64,128]{2,1,0:T(8,128)(2,1)}), bf16[32,64,128]{2,1,0:T(8,128)(2,1)S(1)}, u32[]{:S(2)}, u32[]{:S(2)}) %all-to-all-start.1) | async-done | bytes 524320 | tf_op jit(solution)/shard_map/all_to_all | solution.py:39
  67.1 2.8 %out_give.1 = bf16[4,128,1024]{2,1,0:T(8,128)(2,1)S(1)} custom-call(s32[4]{0:T(128)} %pad_add_fusion.place_ref, bf16[256,128]{1,0:T(8,128)(2,1)S(1)} %convolution_convert_fusion.lhs_ref, bf16[256,8192]{1,0:T(8,128)(2,1)} %w_hbm.3), custom_call_target="tpu_custom_call" | custom-call | tf_op jit(solution)/shard_map/out_give/pallas_call | solution.py:94
  73.4 2.7 out_keep.1
  88.5 5.3 %collective-permute-done.11 = bf16[4,32,1024]{2,1,0:T(8,128)(2,1)} collective-permute-done((bf16[4,32,1024]{2,1,0:T(8,128)(2,1)}, bf16[4,32,1024]{2,1,0:T(8,128)(2,1)}, u32[]{:S(2)}, u32[]{:S(2)}) %collective-permute-start.11) | collective-permute-done | bytes 262176 | tf_op jit(solution)/shard_map/ppermute | solution.py:43
  93.8 5.5 %collective-permute-done.9 = bf16[4,32,1024]{2,1,0:T(8,128)(2,1)} collective-permute-done((bf16[4,32,1024]{2,1,0:T(8,128)(2,1)}, bf16[4,32,1024]{2,1,0:T(8,128)(2,1)}, u32[]{:S(2)}, u32[]{:S(2)}) %collective-permute-start.9) | collective-permute-done | bytes 262176 | tf_op jit(solution)/shard_map/ppermute | solution.py:43
  101.4 4.5 %all-to-all-start.2 = ((bf16[4,32,1024]{2,1,0:T(8,128)(2,1)}), bf16[4,32,1024]{2,1,0:T(8,128)(2,1)S(1)}, u32[]{:S(2)}, u32[]{:S(2)}) async-start(bf16[4,32,1024]{2,1,0:T(8,128)(2,1)} %fusion.11), calls=%async_computation.2 | async-start | bytes 524288 | tf_op jit(solution)/shard_map/all_to_all | solution.py:39
  107.4 9.3 %all-to-all-done.2 = bf16[4,32,1024]{2,1,0:T(8,128)(2,1)S(1)} async-done(((bf16[4,32,1024]{2,1,0:T(8,128)(2,1)}), bf16[4,32,1024]{2,1,0:T(8,128)(2,1)S(1)}, u32[]{:S(2)}, u32[]{:S(2)}) %all-to-all-start.2) | async-done | bytes 262176 | tf_op jit(solution)/shard_map/all_to_all | solution.py:39
  117.5 12.9 %all_to_all.26.refs_0_ = bf16[4,32,1024]{2,1,0:T(8,128)(2,1)S(1)} all-to-all(bf16[4,32,1024]{2,1,0:T(8,128)(2,1)S(1)} %broadcast_in_dim.12), channel_id=1, replica_groups=mesh['c'=2,'yh'=2,'x'=4,'zh'=4,'zl'=2,'yl'=2] {'zh'}, dimensions={0} | all-to-all | bytes 524288 | tf_op jit(solution)/shard_map/all_to_all | solution.py:39
  131.9 40.4 %collective-permute-done.20.refs_9_ = bf16[1024,1024]{1,0:T(8,128)(2,1)} collective-permute-done((bf16[1024,1024]{1,0:T(8,128)(2,1)}, bf16[1024,1024]{1,0:T(8,128)(2,1)}, u32[]{:S(2)}, u32[]{:S(2)}) %collective-permute-start.20) | collective-permute-done | bytes 2097184 | tf_op jit(solution)/shard_map/ppermute | solution.py:220
  182.7 5.9 %gate_up.1 = (bf16[128,1152]{1,0:T(8,128)(2,1)S(1)}, f32[128,1024]{1,0:T(8,128)}, f32[128,128]{1,0:T(8,128)}) custom-call(s32[4]{0:T(128)} %pad_add_fusion.place_ref, f32[8,1,1024]{2,1,0:T(1,128)} %bitcast.44, bf16[4,32,1024]{2,1,0:T(8,128)(2,1)S(1)} %all_to_all.26.refs_0_, bf16[4,32,1024]{2,1,0:T(8,128)(2,1)S(1)} %collective-permute-done.13.refs_1_, ...), custom_call_target="tpu_custom_call" | custom-call | tf_op jit(solution)/shard_map/gate_up/pallas_call | solution.py:142
  189.6 9.6 %collective-permute-done.23.sent_ref = bf16[128,1152]{1,0:T(8,128)(2,1)S(1)} collective-permute-done((bf16[128,1152]{1,0:T(8,128)(2,1)S(1)}, bf16[128,1152]{1,0:T(8,128)(2,1)S(1)}, u32[]{:S(2)}, u32[]{:S(2)}) %collective-permute-start.23) | collective-permute-done | bytes 294944 | tf_op jit(solution)/shard_map/ppermute | solution.py:383
  203.7 21.5 %collective-permute-done.27.refs_3_ = bf16[512,1024]{1,0:T(8,128)(2,1)} collective-permute-done((bf16[512,1024]{1,0:T(8,128)(2,1)S(1)}, bf16[512,1024]{1,0:T(8,128)(2,1)}, u32[]{:S(2)}, u32[]{:S(2)}) %collective-permute-start.27) | collective-permute-done | bytes 1048608 | tf_op jit(solution)/shard_map/ppermute | solution.py:220
  225.2 3.2 %down_give.1 = bf16[4,128,1024]{2,1,0:T(8,128)(2,1)S(1)} custom-call(s32[4]{0:T(128)} %pad_add_fusion.place_ref, bf16[128,512]{1,0:T(8,128)(2,1)S(1)} %hidden.1.hidden_ref, bf16[128,512]{1,0:T(8,128)(2,1)S(1)} %collective-permute-done.24.other_ref, bf16[512,1024]{1,0:T(8,128)(2,1)} %refs_0_.3, bf16[512,1024]{1,0:T(8,128)(2,1)} %collective-permute-done.25.refs_1_, ...), custom_call_target="tpu_custom_call" | custom-call | tf_op jit(solution)/shard_map/down_give/pallas_call | solution.py:198
  228.5 3.2 %down_keep.1 = f32[4,128,1024]{2,1,0:T(8,128)S(1)} custom-call(s32[4]{0:T(128)} %pad_add_fusion.place_ref, bf16[128,512]{1,0:T(8,128)(2,1)S(1)} %hidden.1.hidden_ref, bf16[128,512]{1,0:T(8,128)(2,1)S(1)} %collective-permute-done.24.other_ref, bf16[512,1024]{1,0:T(8,128)(2,1)} %refs_0_.3, bf16[512,1024]{1,0:T(8,128)(2,1)} %collective-permute-done.25.refs_1_, ...), custom_call_target="tpu_custom_call" | custom-call | tf_op jit(solution)/shard_map/down_keep/pallas_call | solution.py:198
  236.6 5.2 %collective-permute-done.29 = bf16[4,32,1024]{2,1,0:T(8,128)(2,1)S(1)} collective-permute-done((bf16[4,32,1024]{2,1,0:T(8,128)(2,1)S(1)}, bf16[4,32,1024]{2,1,0:T(8,128)(2,1)S(1)}, u32[]{:S(2)}, u32[]{:S(2)}) %collective-permute-start.29) | collective-permute-done | bytes 262176 | tf_op jit(solution)/shard_map/ppermute | solution.py:43
  242.9 5.8 %collective-permute-done.31 = bf16[4,32,1024]{2,1,0:T(8,128)(2,1)S(1)} collective-permute-done((bf16[4,32,1024]{2,1,0:T(8,128)(2,1)S(1)}, bf16[4,32,1024]{2,1,0:T(8,128)(2,1)S(1)}, u32[]{:S(2)}, u32[]{:S(2)}) %collective-permute-start.31) | collective-permute-done | bytes 262176 | tf_op jit(solution)/shard_map/ppermute | solution.py:43
  249.8 14.7 %all_to_all.27 = bf16[4,32,1024]{2,1,0:T(8,128)(2,1)S(1)} all-to-all(bf16[4,32,1024]{2,1,0:T(8,128)(2,1)S(1)} %fusion.6), channel_id=1, replica_groups=mesh['c'=2,'yh'=2,'x'=4,'zh'=4,'zl'=2,'yl'=2] {'zh'}, dimensions={0} | all-to-all | bytes 524288 | tf_op jit(solution)/shard_map/all_to_all | solution.py:39
  264.5 3.5 %collective-permute-start.32 = (bf16[32,1024]{1,0:T(8,128)(2,1)S(1)}, bf16[32,1024]{1,0:T(8,128)(2,1)S(1)}, u32[]{:S(2)}, u32[]{:S(2)}) collective-permute-start(bf16[32,1024]{1,0:T(8,128)(2,1)S(1)} %add_convert_fusion), channel_id=1, source_target_pairs={{0,0},{1,1},{2,2},{3,3},{4,16},{5,17},{6,18},{7,19},{8,32},{9,33},... | collective-permute-start | bytes 196616 | tf_op jit(solution)/shard_map/ppermute | solution.py:57
  268.0 9.0 %collective-permute-done.32 = bf16[32,1024]{1,0:T(8,128)(2,1)S(1)} collective-permute-done((bf16[32,1024]{1,0:T(8,128)(2,1)S(1)}, bf16[32,1024]{1,0:T(8,128)(2,1)S(1)}, u32[]{:S(2)}, u32[]{:S(2)}) %collective-permute-start.32) | collective-permute-done | bytes 65568 | tf_op jit(solution)/shard_map/ppermute | solution.py:57
  (108 shorter events, 58.8 us)
Async XLA Ops:
  20.2 9.2 %collective-permute-start = (bf16[4,128,256]{2,1,0:T(8,128)(2,1)S(1)}, bf16[4,128,256]{2,1,0:T(8,128)(2,1)S(1)}, u32[]{:S(2)}, u32[]{:S(2)}) collective-permute-start(bf16[4,128,256]{2,1,0:T(8,128)(2,1)S(1)} %all_to_all.25.refs_0_), channel_id=1, source_target_pairs={{0,1},{1,0},{2,3},{3,2},{4,5},{5,4},{6,7},{7,6},{8,9},{9,8},{10,11... | collective-permute-start | bytes 786440 | tf_op jit(solution)/shard_map/ppermute | solution.py:43
  21.8 8.3 %collective-permute-start.1 = (bf16[4,128,256]{2,1,0:T(8,128)(2,1)S(1)}, bf16[4,128,256]{2,1,0:T(8,128)(2,1)S(1)}, u32[]{:S(2)}, u32[]{:S(2)}) collective-permute-start(bf16[4,128,256]{2,1,0:T(8,128)(2,1)S(1)} %all_to_all.25.refs_0_), channel_id=1, source_target_pairs={{0,2},{1,3},{2,0},{3,1},{4,6},{5,7},{6,4},{7,5},{8,10},{9,11},{10,... | collective-permute-start | bytes 786440 | tf_op jit(solution)/shard_map/ppermute | solution.py:43
  22.7 10.1 %collective-permute-start.2 = (bf16[4,128,256]{2,1,0:T(8,128)(2,1)S(1)}, bf16[4,128,256]{2,1,0:T(8,128)(2,1)S(1)}, u32[]{:S(2)}, u32[]{:S(2)}) collective-permute-start(bf16[4,128,256]{2,1,0:T(8,128)(2,1)S(1)} %all_to_all.25.refs_0_), channel_id=1, source_target_pairs={{0,3},{1,2},{2,1},{3,0},{4,7},{5,6},{6,5},{7,4},{8,11},{9,10},{10,... | collective-permute-start | bytes 786440 | tf_op jit(solution)/shard_map/ppermute | solution.py:43
  23.7 10.4 %collective-permute-start.6 = (bf16[4,128,256]{2,1,0:T(8,128)(2,1)S(1)}, bf16[4,128,256]{2,1,0:T(8,128)(2,1)S(1)}, u32[]{:S(2)}, u32[]{:S(2)}) collective-permute-start(bf16[4,128,256]{2,1,0:T(8,128)(2,1)S(1)} %all_to_all.25.refs_0_), channel_id=1, source_target_pairs={{0,128},{128,0},{1,129},{129,1},{2,130},{130,2},{3,131},{131,3},{4... | collective-permute-start | bytes 786440 | tf_op jit(solution)/shard_map/ppermute | solution.py:305
  43.0 21.5 %all-to-all-start.1 = ((bf16[32,64,128]{2,1,0:T(8,128)(2,1)}), bf16[32,64,128]{2,1,0:T(8,128)(2,1)S(1)}, u32[]{:S(2)}, u32[]{:S(2)}) async-start(bf16[32,64,128]{2,1,0:T(8,128)(2,1)} %broadcast_in_dim.10), calls=%async_computation.1 | async-start | bytes 1048576 | tf_op jit(solution)/shard_map/all_to_all | solution.py:39
  78.3 8.3 %collective-permute-start.10 = (bf16[4,32,1024]{2,1,0:T(8,128)(2,1)S(1)}, bf16[4,32,1024]{2,1,0:T(8,128)(2,1)}, u32[]{:S(2)}, u32[]{:S(2)}) collective-permute-start(bf16[4,32,1024]{2,1,0:T(8,128)(2,1)S(1)} %get-tuple-element.26), channel_id=1, source_target_pairs={{0,2},{1,3},{2,0},{3,1},{4,6},{5,7},{6,4},{7,5},{8,10},{9,11},{10,... | collective-permute-start | bytes 786440 | tf_op jit(solution)/shard_map/ppermute | solution.py:43
  80.3 92.1 %collective-permute-start.20 = (bf16[1024,1024]{1,0:T(8,128)(2,1)}, bf16[1024,1024]{1,0:T(8,128)(2,1)}, u32[]{:S(2)}, u32[]{:S(2)}) collective-permute-start(bf16[1024,1024]{1,0:T(8,128)(2,1)} %constant_dynamic-update-slice_fusion.refs_8_), channel_id=1, source_target_pairs={{0,48},{16,0},{32,16},{48,32},{1,49},{17,1},{33,17},{49,33},{2,50}... | collective-permute-start | bytes 6291464 | tf_op jit(solution)/shard_map/ppermute | solution.py:220
  82.2 90.1 %collective-permute-start.21 = (bf16[1024,1024]{1,0:T(8,128)(2,1)}, bf16[1024,1024]{1,0:T(8,128)(2,1)}, u32[]{:S(2)}, u32[]{:S(2)}) collective-permute-start(bf16[1024,1024]{1,0:T(8,128)(2,1)} %constant_dynamic-update-slice_fusion.refs_8_), channel_id=1, source_target_pairs={{0,32},{16,48},{32,0},{48,16},{1,33},{17,49},{33,1},{49,17},{2,34}... | collective-permute-start | bytes 6291464 | tf_op jit(solution)/shard_map/ppermute | solution.py:220
  84.1 91.9 %collective-permute-start.22 = (bf16[1024,1024]{1,0:T(8,128)(2,1)}, bf16[1024,1024]{1,0:T(8,128)(2,1)}, u32[]{:S(2)}, u32[]{:S(2)}) collective-permute-start(bf16[1024,1024]{1,0:T(8,128)(2,1)} %constant_dynamic-update-slice_fusion.refs_8_), channel_id=1, source_target_pairs={{0,16},{16,32},{32,48},{48,0},{1,17},{17,33},{33,49},{49,1},{2,18}... | collective-permute-start | bytes 6291464 | tf_op jit(solution)/shard_map/ppermute | solution.py:220
  85.4 8.4 %collective-permute-start.11 = (bf16[4,32,1024]{2,1,0:T(8,128)(2,1)}, bf16[4,32,1024]{2,1,0:T(8,128)(2,1)}, u32[]{:S(2)}, u32[]{:S(2)}) collective-permute-start(bf16[4,32,1024]{2,1,0:T(8,128)(2,1)} %get-tuple-element.25), channel_id=1, source_target_pairs={{0,3},{1,2},{2,1},{3,0},{4,7},{5,6},{6,5},{7,4},{8,11},{9,10},{10,... | collective-permute-start | bytes 786440 | tf_op jit(solution)/shard_map/ppermute | solution.py:43
  86.7 12.7 %collective-permute-start.9 = (bf16[4,32,1024]{2,1,0:T(8,128)(2,1)}, bf16[4,32,1024]{2,1,0:T(8,128)(2,1)}, u32[]{:S(2)}, u32[]{:S(2)}) collective-permute-start(bf16[4,32,1024]{2,1,0:T(8,128)(2,1)} %get-tuple-element.24), channel_id=1, source_target_pairs={{0,1},{1,0},{2,3},{3,2},{4,5},{5,4},{6,7},{7,6},{8,9},{9,8},{10,11... | collective-permute-start | bytes 786440 | tf_op jit(solution)/shard_map/ppermute | solution.py:43
  101.4 15.3 %all-to-all-start.2 = ((bf16[4,32,1024]{2,1,0:T(8,128)(2,1)}), bf16[4,32,1024]{2,1,0:T(8,128)(2,1)S(1)}, u32[]{:S(2)}, u32[]{:S(2)}) async-start(bf16[4,32,1024]{2,1,0:T(8,128)(2,1)} %fusion.11), calls=%async_computation.2 | async-start | bytes 524288 | tf_op jit(solution)/shard_map/all_to_all | solution.py:39
  130.4 47.6 %collective-permute-start.13 = (bf16[4,32,1024]{2,1,0:T(8,128)(2,1)S(1)}, bf16[4,32,1024]{2,1,0:T(8,128)(2,1)S(1)}, u32[]{:S(2)}, u32[]{:S(2)}) collective-permute-start(bf16[4,32,1024]{2,1,0:T(8,128)(2,1)S(1)} %all_to_all.26.refs_0_), channel_id=1, source_target_pairs={{0,1},{1,0},{2,3},{3,2},{4,5},{5,4},{6,7},{7,6},{8,9},{9,8},{10,11... | collective-permute-start | bytes 786440 | tf_op jit(solution)/shard_map/ppermute | solution.py:43
  131.0 47.7 %collective-permute-start.14 = (bf16[4,32,1024]{2,1,0:T(8,128)(2,1)S(1)}, bf16[4,32,1024]{2,1,0:T(8,128)(2,1)S(1)}, u32[]{:S(2)}, u32[]{:S(2)}) collective-permute-start(bf16[4,32,1024]{2,1,0:T(8,128)(2,1)S(1)} %all_to_all.26.refs_0_), channel_id=1, source_target_pairs={{0,2},{1,3},{2,0},{3,1},{4,6},{5,7},{6,4},{7,5},{8,10},{9,11},{10,... | collective-permute-start | bytes 786440 | tf_op jit(solution)/shard_map/ppermute | solution.py:43
  172.3 7.3 %collective-permute-start.15 = (bf16[4,32,1024]{2,1,0:T(8,128)(2,1)S(1)}, bf16[4,32,1024]{2,1,0:T(8,128)(2,1)S(1)}, u32[]{:S(2)}, u32[]{:S(2)}) collective-permute-start(bf16[4,32,1024]{2,1,0:T(8,128)(2,1)S(1)} %all_to_all.26.refs_0_), channel_id=1, source_target_pairs={{0,3},{1,2},{2,1},{3,0},{4,7},{5,6},{6,5},{7,4},{8,11},{9,10},{10,... | collective-permute-start | bytes 786440 | tf_op jit(solution)/shard_map/ppermute | solution.py:43
  172.3 29.4 %collective-permute-start.25 = (bf16[512,1024]{1,0:T(8,128)(2,1)S(1)}, bf16[512,1024]{1,0:T(8,128)(2,1)}, u32[]{:S(2)}, u32[]{:S(2)}) collective-permute-start(bf16[512,1024]{1,0:T(8,128)(2,1)S(1)} %copy-done.3), channel_id=1, source_target_pairs={{0,48},{16,0},{32,16},{48,32},{1,49},{17,1},{33,17},{49,33},{2,50}... | collective-permute-start | bytes 3145736 | tf_op jit(solution)/shard_map/ppermute | solution.py:220
  176.0 27.7 %collective-permute-start.26 = (bf16[512,1024]{1,0:T(8,128)(2,1)S(1)}, bf16[512,1024]{1,0:T(8,128)(2,1)}, u32[]{:S(2)}, u32[]{:S(2)}) collective-permute-start(bf16[512,1024]{1,0:T(8,128)(2,1)S(1)} %copy-done.3), channel_id=1, source_target_pairs={{0,32},{16,48},{32,0},{48,16},{1,33},{17,49},{33,1},{49,17},{2,34}... | collective-permute-start | bytes 3145736 | tf_op jit(solution)/shard_map/ppermute | solution.py:220
  178.0 47.2 %collective-permute-start.27 = (bf16[512,1024]{1,0:T(8,128)(2,1)S(1)}, bf16[512,1024]{1,0:T(8,128)(2,1)}, u32[]{:S(2)}, u32[]{:S(2)}) collective-permute-start(bf16[512,1024]{1,0:T(8,128)(2,1)S(1)} %copy-done.3), channel_id=1, source_target_pairs={{0,16},{16,32},{32,48},{48,0},{1,17},{17,33},{33,49},{49,1},{2,18}... | collective-permute-start | bytes 3145736 | tf_op jit(solution)/shard_map/ppermute | solution.py:220
  188.6 10.6 %collective-permute-start.23 = (bf16[128,1152]{1,0:T(8,128)(2,1)S(1)}, bf16[128,1152]{1,0:T(8,128)(2,1)S(1)}, u32[]{:S(2)}, u32[]{:S(2)}) collective-permute-start(bf16[128,1152]{1,0:T(8,128)(2,1)S(1)} %get-tuple-element.20), channel_id=1, source_target_pairs={{0,64},{64,0},{1,65},{65,1},{2,66},{66,2},{3,67},{67,3},{4,68},{68... | collective-permute-start | bytes 884744 | tf_op jit(solution)/shard_map/ppermute | solution.py:383
  200.5 24.7 %collective-permute-start.24 = (bf16[128,512]{1,0:T(8,128)(2,1)S(1)}, bf16[128,512]{1,0:T(8,128)(2,1)S(1)}, u32[]{:S(2)}, u32[]{:S(2)}) collective-permute-start(bf16[128,512]{1,0:T(8,128)(2,1)S(1)} %hidden.1.hidden_ref), channel_id=1, source_target_pairs={{0,64},{64,0},{1,65},{65,1},{2,66},{66,2},{3,67},{67,3},{4,68},{68... | collective-permute-start | bytes 393224 | tf_op jit(solution)/shard_map/ppermute | solution.py:386
  233.0 8.8 %collective-permute-start.29 = (bf16[4,32,1024]{2,1,0:T(8,128)(2,1)S(1)}, bf16[4,32,1024]{2,1,0:T(8,128)(2,1)S(1)}, u32[]{:S(2)}, u32[]{:S(2)}) collective-permute-start(bf16[4,32,1024]{2,1,0:T(8,128)(2,1)S(1)} %get-tuple-element.21), channel_id=1, source_target_pairs={{0,1},{1,0},{2,3},{3,2},{4,5},{5,4},{6,7},{7,6},{8,9},{9,8},{10,11... | collective-permute-start | bytes 786440 | tf_op jit(solution)/shard_map/ppermute | solution.py:43
  233.7 9.2 %collective-permute-start.30 = (bf16[4,32,1024]{2,1,0:T(8,128)(2,1)S(1)}, bf16[4,32,1024]{2,1,0:T(8,128)(2,1)S(1)}, u32[]{:S(2)}, u32[]{:S(2)}) collective-permute-start(bf16[4,32,1024]{2,1,0:T(8,128)(2,1)S(1)} %get-tuple-element.23), channel_id=1, source_target_pairs={{0,2},{1,3},{2,0},{3,1},{4,6},{5,7},{6,4},{7,5},{8,10},{9,11},{10,... | collective-permute-start | bytes 786440 | tf_op jit(solution)/shard_map/ppermute | solution.py:43
  234.0 14.7 %collective-permute-start.31 = (bf16[4,32,1024]{2,1,0:T(8,128)(2,1)S(1)}, bf16[4,32,1024]{2,1,0:T(8,128)(2,1)S(1)}, u32[]{:S(2)}, u32[]{:S(2)}) collective-permute-start(bf16[4,32,1024]{2,1,0:T(8,128)(2,1)S(1)} %get-tuple-element.22), channel_id=1, source_target_pairs={{0,3},{1,2},{2,1},{3,0},{4,7},{5,6},{6,5},{7,4},{8,11},{9,10},{10,... | collective-permute-start | bytes 786440 | tf_op jit(solution)/shard_map/ppermute | solution.py:43
  264.5 12.5 %collective-permute-start.32 = (bf16[32,1024]{1,0:T(8,128)(2,1)S(1)}, bf16[32,1024]{1,0:T(8,128)(2,1)S(1)}, u32[]{:S(2)}, u32[]{:S(2)}) collective-permute-start(bf16[32,1024]{1,0:T(8,128)(2,1)S(1)} %add_convert_fusion), channel_id=1, source_target_pairs={{0,0},{1,1},{2,2},{3,3},{4,16},{5,17},{6,18},{7,19},{8,32},{9,33},... | collective-permute-start | bytes 196616 | tf_op jit(solution)/shard_map/ppermute | solution.py:57
  (18 other events, 237.2 us)

commit v2 on v1

--- a/solution.py
+++ b/solution.py
@@ -104,23 +104,31 @@
     )(place, *in_vmem(attended), w_out)
 
 
-def gate_up_terms(place, gains, pieces, weights):
+def gate_up_terms(place, gains, pieces, gates, ups):
     n, part, depth = pieces[0].shape
-    rows, cols, count = 4 * part, weights[0].shape[1], len(pieces)
+    rows, hid, count = 4 * part, gates[0].shape[1], len(pieces)
+    cols = 2 * hid
 
     def body(place_ref, gain_ref, *refs):
-        pieces, weights, refs = refs[:count], refs[count : count + n], refs[count + n :]
+        pieces, refs = refs[:count], refs[count:]
+        gates, ups, refs = refs[:n], refs[n : 2 * n], refs[2 * n :]
         give_ref, keep_ref, square_ref, w, acc, sq, sem = refs
         copies = [
-            pltpu.make_async_copy(weights[k], w.at[k], sem.at[k]) for k in range(n)
+            (
+                pltpu.make_async_copy(gates[k], w.at[k, :, pl.ds(0, hid)], sem.at[2 * k]),
+                pltpu.make_async_copy(ups[k], w.at[k, :, pl.ds(hid, hid)], sem.at[2 * k + 1]),
+            )
+            for k in range(n)
         ]
-        for copy in copies:
-            copy.start()
+        for pair in copies:
+            for copy in pair:
+                copy.start()
         for k in range(n):
             lhs = jnp.concatenate([p[k] for p in pieces], axis=0)
             wide = lhs.astype(F32)
             square = jnp.sum(wide * wide, axis=1, keepdims=True)
-            copies[k].wait()
+            for copy in copies[k]:
+                copy.wait()
             gain = gain_ref[place_ref[3] * n + (place_ref[2] + k) % n]
             out = dot((wide * gain).astype(BF16), w[k])
             if k == 0:
@@ -146,16 +154,16 @@
             jax.ShapeDtypeStruct((rows, cols), F32),
             jax.ShapeDtypeStruct((rows, 128), F32),
         ],
-        in_specs=[SMEM, VMEM] + [VMEM] * count + [HBM] * n,
+        in_specs=[SMEM, VMEM] + [VMEM] * count + [HBM] * (2 * n),
         out_specs=[VMEM] * 3,
         scratch_shapes=[
             pltpu.VMEM((n, depth, cols), BF16),
             pltpu.VMEM((2 * rows, cols), F32),
             pltpu.VMEM((2 * rows, 128), F32),
-            pltpu.SemaphoreType.DMA((n,)),
+            pltpu.SemaphoreType.DMA((2 * n,)),
         ],
         name="gate_up",
-    )(place, gains, *in_vmem(*pieces), *weights)
+    )(place, gains, *in_vmem(*pieces), *gates, *ups)
 
 
 def hidden_units(keep, square, sent, dim):
@@ -179,12 +187,15 @@
 
 def down_terms(place, hidden, other, weights, give):
     n, rows = len(weights), hidden.shape[0]
-    depth, cols = weights[0].shape
+    depth, cols = weights[0][0].shape
+    arrays = [(t, k, i * t.shape[0]) for k, parts in enumerate(weights) for i, t in enumerate(parts)]
+    count = len(arrays)
 
     def body(place_ref, hidden_ref, other_ref, *refs):
-        weights, out_ref, w, sem = refs[:n], refs[n], refs[n + 1], refs[n + 2]
+        weights, out_ref, w, sem = refs[:count], refs[count], refs[count + 1], refs[count + 2]
         copies = [
-            pltpu.make_async_copy(weights[k], w.at[k], sem.at[k]) for k in range(n)
+            pltpu.make_async_copy(ref, w.at[k, pl.ds(at, t.shape[0])], sem.at[i])
+            for i, (ref, (t, k, at)) in enumerate(zip(weights, arrays))
         ]
         for copy in copies:
             copy.start()
@@ -192,17 +203,19 @@
         own = jnp.logical_not(same) if give else same
         lhs = jnp.where(own, hidden_ref[...], other_ref[...])
         for k in range(n):
-            copies[k].wait()
+            for copy, (_, owner, _) in zip(copies, arrays):
+                if owner == k:
+                    copy.wait()
             out_ref[k] = dot(lhs, w[k]).astype(out_ref.dtype)
 
     return pl.pallas_call(
         body,
         out_shape=pltpu.VMEM((n, rows, cols), BF16 if give else F32),
-        in_specs=[SMEM, VMEM, VMEM] + [HBM] * n,
+        in_specs=[SMEM, VMEM, VMEM] + [HBM] * count,
         out_specs=VMEM,
-        scratch_shapes=[pltpu.VMEM((n, depth, cols), BF16), pltpu.SemaphoreType.DMA((n,))],
+        scratch_shapes=[pltpu.VMEM((n, depth, cols), BF16), pltpu.SemaphoreType.DMA((count,))],
         name="down_give" if give else "down_keep",
-    )(place, *in_vmem(hidden, other), *weights)
+    )(place, *in_vmem(hidden, other), *[t for t, _, _ in arrays])
 
 
 def rope_tables(positions):
@@ -316,12 +329,16 @@
     block_d = dim // 8
     total = rows * n_dp
     quarter = rows // 4
-
-    gate_up_w = jnp.concatenate([w_gate, w_up], axis=1)
-    gate_up_next, gate_up_last = from_x(gate_up_w, 1), from_x(gate_up_w, 3)
-    gate_up_all = [gate_up_w, gate_up_next, from_x(gate_up_w, 2), gate_up_last]
+    hid = w_gate.shape[1]
+
+    gate_next, gate_last = from_x(w_gate, 1), from_x(w_gate, 3)
+    up_next, up_last = from_x(w_up, 1), from_x(w_up, 3)
+    gate_all = [w_gate, gate_next, from_x(gate_next, 1), gate_last]
+    up_all = [w_up, up_next, from_x(up_last, 3), up_last]
     down_next, down_last = from_x(w_down, 1), from_x(w_down, 3)
-    down_all = [w_down, down_next, from_x(w_down, 2), down_last]
+    part = hid // 2
+    down_far = (from_x(down_next[:part], 1), from_x(down_last[part:], 3))
+    down_all = [(w_down,), (down_next,), down_far, (down_last,)]
 
     ours, theirs = gathered(tokens_in)
     place = jnp.stack([core, spot, x, y_hi]).astype(jnp.int32)
@@ -379,7 +396,7 @@
     ours, theirs = gathered(mid_own)
 
     gains_mlp = gain_mlp.astype(F32).reshape(n_dp, 1, block_d)
-    sent, keep, square = gate_up_terms(place, gains_mlp, ours + theirs, gate_up_all)
+    sent, keep, square = gate_up_terms(place, gains_mlp, ours + theirs, gate_all, up_all)
     sent = lax.ppermute(sent, "yh", SWAP)
     hidden = hidden_units(keep, square, sent, dim)
 

time: 279 us -> 253 us (0.907)
  waiting for transfers between devices: 137 us -> 111 us
  blocking collectives: 46.9 us -> 34.7 us
  starting transfers between devices: 48.9 us -> 57.7 us
  local copies, waits for them, and re-layouts: 7.07 us -> 10.1 us
    ppermute x6 -> x10, waiting for transfers between devices: 65 us -> 36.9 us  [from_x(): return lax.ppermute(array, 'x', [(i, (i - r) % NX) for i in range(NX)])]
    all_to_all x3 -> x2, blocking collectives: 46.9 us -> 34.7 us  [exchange(): return lax.all_to_all(tiles, axis, 0, 0, tiled=True)]
    all_to_all x2 -> x3, waiting for transfers between devices: 17.6 us -> 25.4 us  [exchange(): return lax.all_to_all(tiles, axis, 0, 0, tiled=True)]
    ppermute x12, waiting for transfers between devices: 33.2 us -> 29 us  [from_sq(): return lax.ppermute(array, ('zl', 'yl'), [(i, i ^ s) for i in range(4)])]
    all_to_all x2 -> x3, starting transfers between devices: 17.4 us -> 21.4 us  [exchange(): return lax.all_to_all(tiles, axis, 0, 0, tiled=True)]
    slice x0 -> x2, local copies, waits for them, and re-layouts: none -> 3.77 us  [layer(): down_far = (from_x(down_next[:part], 1), from_x(down_last[part:], 3))]
    ppermute x1, waiting for transfers between devices: 0.01 us -> 3.57 us  [layer(): other = lax.ppermute(hidden, 'yh', SWAP)]
    ppermute x1, waiting for transfers between devices: 9.65 us -> 6.13 us  [layer(): sent = lax.ppermute(sent, 'yh', SWAP)]
  transfers between devices with their start and end apart: 35 -> 40, of which waited for: 21 -> 18; matrix products, arithmetic and copies ran while one was open for 3% -> 5% of each run, Pallas kernels for 6% -> 6%
where the time goes in v2:
time: 253 us; the launch traced here: 252 us
  waiting for transfers between devices  111 us (44%)
  starting transfers between devices  57.7 us (23%)
  blocking collectives  34.7 us (14%)
  Pallas kernels  26.1 us (10%)
  other arithmetic  10.6 us (4%)
  local copies, waits for them, and re-layouts  10.1 us (4%)
    ppermute x10, waiting for transfers between devices, from_x(): return lax.ppermute(array, 'x', [(i, (i - r) % NX) for i in range(NX)])  36.9 us
    all_to_all x2, blocking collectives, exchange(): return lax.all_to_all(tiles, axis, 0, 0, tiled=True)  34.7 us
    ppermute x12, waiting for transfers between devices, from_sq(): return lax.ppermute(array, ('zl', 'yl'), [(i, i ^ s) for i in range(4)])  29 us
    all_to_all x3, waiting for transfers between devices, exchange(): return lax.all_to_all(tiles, axis, 0, 0, tiled=True)  25.4 us
    all_to_all x3, starting transfers between devices, exchange(): return lax.all_to_all(tiles, axis, 0, 0, tiled=True)  21.4 us
    ppermute x12, starting transfers between devices, from_sq(): return lax.ppermute(array, ('zl', 'yl'), [(i, i ^ s) for i in range(4)])  13.4 us
    ppermute x10, starting transfers between devices, from_x(): return lax.ppermute(array, 'x', [(i, (i - r) % NX) for i in range(NX)])  11.3 us
    ppermute x3, waiting for transfers between devices, move(): return lax.ppermute(array, EVERY, moves)  10.1 us
  transfers between devices with their start and end apart: 40, of which 18 were waited for; matrix products, arithmetic and copies ran while one was open for 5% of the time, Pallas kernels for 6%

profile of v2, /device:TPU:4, one launch (start us, length us, event | category | flops | bytes accessed | tf_op | source)
XLA Modules:
  0.0 251.6 jit_solution(8513402301157134691)
XLA Ops:
  0.9 19.3 %all_to_all.25.refs_0_ = bf16[4,128,256]{2,1,0:T(8,128)(2,1)S(1)} all-to-all(bf16[4,128,256]{2,1,0:T(8,128)(2,1)S(1)} %broadcast_in_dim.9), channel_id=1, replica_groups=mesh['c'=2,'yh'=2,'x'=4,'zh'=4,'zl'=2,'yl'=2] {'zh'}, dimensions={0} | all-to-all | bytes 524288 | tf_op jit(solution)/shard_map/all_to_all | solution.py:39
  23.7 5.7 %collective-permute-done.refs_0_ = bf16[4,128,256]{2,1,0:T(8,128)(2,1)S(1)} collective-permute-done((bf16[4,128,256]{2,1,0:T(8,128)(2,1)S(1)}, bf16[4,128,256]{2,1,0:T(8,128)(2,1)S(1)}, u32[]{:S(2)}, u32[]{:S(2)}) %collective-permute-start) | collective-permute-done | bytes 262176 | tf_op jit(solution)/shard_map/ppermute | solution.py:43
  36.7 4.7 %project_last.1 = (f32[128,256]{1,0:T(8,128)S(1)}, f32[64,128]{1,0:T(8,128)S(1)}, f32[128,256]{1,0:T(8,128)}) custom-call(s32[4]{0:T(128)} %pad_add_fusion.place_ref, f32[32,1,256]{2,1,0:T(1,128)S(1)} %bitcast.39, bf16[8192,256]{1,0:T(8,128)(2,1)} %wq_hbm.3, bf16[64,8192]{1,0:T(8,128)(2,1)} %bitcast.41, ...), custom_call_target="tpu_custom_call" | custom-call | tf_op jit(solution)/shard_map/project_last/pallas_call | solution.py:287
  43.0 12.9 %all-to-all-start.1 = ((bf16[32,64,128]{2,1,0:T(8,128)(2,1)}), bf16[32,64,128]{2,1,0:T(8,128)(2,1)S(1)}, u32[]{:S(2)}, u32[]{:S(2)}) async-start(bf16[32,64,128]{2,1,0:T(8,128)(2,1)} %broadcast_in_dim.10), calls=%async_computation.1 | async-start | bytes 1048576 | tf_op jit(solution)/shard_map/all_to_all | solution.py:39
  56.3 8.3 %all-to-all-done.1 = bf16[32,64,128]{2,1,0:T(8,128)(2,1)S(1)} async-done(((bf16[32,64,128]{2,1,0:T(8,128)(2,1)}), bf16[32,64,128]{2,1,0:T(8,128)(2,1)S(1)}, u32[]{:S(2)}, u32[]{:S(2)}) %all-to-all-start.1) | async-done | bytes 524320 | tf_op jit(solution)/shard_map/all_to_all | solution.py:39
  83.3 4.2 %collective-permute-done.10 = bf16[4,32,1024]{2,1,0:T(8,128)(2,1)S(1)} collective-permute-done((bf16[4,32,1024]{2,1,0:T(8,128)(2,1)S(1)}, bf16[4,32,1024]{2,1,0:T(8,128)(2,1)S(1)}, u32[]{:S(2)}, u32[]{:S(2)}) %collective-permute-start.10) | collective-permute-done | bytes 262176 | tf_op jit(solution)/shard_map/ppermute | solution.py:43
  88.3 3.7 %collective-permute-done.11 = bf16[4,32,1024]{2,1,0:T(8,128)(2,1)} collective-permute-done((bf16[4,32,1024]{2,1,0:T(8,128)(2,1)}, bf16[4,32,1024]{2,1,0:T(8,128)(2,1)}, u32[]{:S(2)}, u32[]{:S(2)}) %collective-permute-start.11) | collective-permute-done | bytes 262176 | tf_op jit(solution)/shard_map/ppermute | solution.py:43
  97.3 4.4 %all-to-all-start.2 = ((bf16[4,32,1024]{2,1,0:T(8,128)(2,1)}), bf16[4,32,1024]{2,1,0:T(8,128)(2,1)S(1)}, u32[]{:S(2)}, u32[]{:S(2)}) async-start(bf16[4,32,1024]{2,1,0:T(8,128)(2,1)} %fusion.11), calls=%async_computation.2 | async-start | bytes 524288 | tf_op jit(solution)/shard_map/all_to_all | solution.py:39
  103.8 8.0 %all-to-all-done.2 = bf16[4,32,1024]{2,1,0:T(8,128)(2,1)S(1)} async-done(((bf16[4,32,1024]{2,1,0:T(8,128)(2,1)}), bf16[4,32,1024]{2,1,0:T(8,128)(2,1)S(1)}, u32[]{:S(2)}, u32[]{:S(2)}) %all-to-all-start.2) | async-done | bytes 262176 | tf_op jit(solution)/shard_map/all_to_all | solution.py:39
  113.0 17.6 %collective-permute-done.22.refs_11_ = bf16[1024,512]{1,0:T(8,128)(2,1)S(1)} collective-permute-done((bf16[1024,512]{1,0:T(8,128)(2,1)}, bf16[1024,512]{1,0:T(8,128)(2,1)S(1)}, u32[]{:S(2)}, u32[]{:S(2)}) %collective-permute-start.22) | collective-permute-done | bytes 1048608 | tf_op jit(solution)/shard_map/ppermute | solution.py:233
  133.5 4.1 %all-to-all-start.3 = ((bf16[4,32,1024]{2,1,0:T(8,128)(2,1)}), bf16[4,32,1024]{2,1,0:T(8,128)(2,1)S(1)}, u32[]{:S(2)}, u32[]{:S(2)}) async-start(bf16[4,32,1024]{2,1,0:T(8,128)(2,1)} %broadcast_in_dim.12), calls=%async_computation.3 | async-start | bytes 524288 | tf_op jit(solution)/shard_map/all_to_all | solution.py:39
  137.6 9.1 %all-to-all-done.3.refs_0_ = bf16[4,32,1024]{2,1,0:T(8,128)(2,1)S(1)} async-done(((bf16[4,32,1024]{2,1,0:T(8,128)(2,1)}), bf16[4,32,1024]{2,1,0:T(8,128)(2,1)S(1)}, u32[]{:S(2)}, u32[]{:S(2)}) %all-to-all-start.3) | async-done | bytes 262176 | tf_op jit(solution)/shard_map/all_to_all | solution.py:39
  148.1 5.0 %collective-permute-done.30.refs_4_ = bf16[512,1024]{1,0:T(8,128)(2,1)} collective-permute-done((bf16[512,1024]{1,0:T(8,128)(2,1)}, bf16[512,1024]{1,0:T(8,128)(2,1)}, u32[]{:S(2)}, u32[]{:S(2)}) %collective-permute-start.30) | collective-permute-done | bytes 1048608 | tf_op jit(solution)/shard_map/ppermute | solution.py:233
  154.6 10.6 %collective-permute-done.21.refs_10_ = bf16[1024,512]{1,0:T(8,128)(2,1)} collective-permute-done((bf16[1024,512]{1,0:T(8,128)(2,1)}, bf16[1024,512]{1,0:T(8,128)(2,1)}, u32[]{:S(2)}, u32[]{:S(2)}) %collective-permute-start.21) | collective-permute-done | bytes 1048608 | tf_op jit(solution)/shard_map/ppermute | solution.py:233
  170.0 3.6 %collective-permute-done.25.refs_14_ = bf16[1024,512]{1,0:T(8,128)(2,1)} collective-permute-done((bf16[1024,512]{1,0:T(8,128)(2,1)}, bf16[1024,512]{1,0:T(8,128)(2,1)}, u32[]{:S(2)}, u32[]{:S(2)}) %collective-permute-start.25) | collective-permute-done | bytes 1048608 | tf_op jit(solution)/shard_map/ppermute | solution.py:233
  176.3 5.8 %gate_up.1 = (bf16[128,1152]{1,0:T(8,128)(2,1)S(1)}, f32[128,1024]{1,0:T(8,128)}, f32[128,128]{1,0:T(8,128)}) custom-call(s32[4]{0:T(128)} %pad_add_fusion.place_ref, f32[8,1,1024]{2,1,0:T(1,128)} %bitcast.44, bf16[4,32,1024]{2,1,0:T(8,128)(2,1)S(1)} %all-to-all-done.3.refs_0_, bf16[4,32,1024]{2,1,0:T(8,128)(2,1)S(1)} %collective-permute-done.13.refs_1_, ...), custom_call_target="tpu_custom_call" | custom-call | tf_op jit(solution)/shard_map/gate_up/pallas_call | solution.py:150
  184.3 6.1 %collective-permute-done.26.sent_ref = bf16[128,1152]{1,0:T(8,128)(2,1)S(1)} collective-permute-done((bf16[128,1152]{1,0:T(8,128)(2,1)S(1)}, bf16[128,1152]{1,0:T(8,128)(2,1)S(1)}, u32[]{:S(2)}, u32[]{:S(2)}) %collective-permute-start.26) | collective-permute-done | bytes 294944 | tf_op jit(solution)/shard_map/ppermute | solution.py:400
  194.7 3.6 %collective-permute-done.27.other_ref = bf16[128,512]{1,0:T(8,128)(2,1)S(1)} collective-permute-done((bf16[128,512]{1,0:T(8,128)(2,1)S(1)}, bf16[128,512]{1,0:T(8,128)(2,1)S(1)}, u32[]{:S(2)}, u32[]{:S(2)}) %collective-permute-start.27) | collective-permute-done | bytes 131104 | tf_op jit(solution)/shard_map/ppermute | solution.py:403
  198.3 3.2 %down_give.1 = bf16[4,128,1024]{2,1,0:T(8,128)(2,1)S(1)} custom-call(s32[4]{0:T(128)} %pad_add_fusion.place_ref, bf16[128,512]{1,0:T(8,128)(2,1)S(1)} %hidden.1.hidden_ref, bf16[128,512]{1,0:T(8,128)(2,1)S(1)} %collective-permute-done.27.other_ref, bf16[512,1024]{1,0:T(8,128)(2,1)} %refs_0_.3, bf16[512,1024]{1,0:T(8,128)(2,1)} %collective-permute-done.28.refs_1_, ...), custom_call_target="tpu_custom_call" | custom-call | tf_op jit(solution)/shard_map/down_give/pallas_call | solution.py:211
  201.6 3.2 %down_keep.1 = f32[4,128,1024]{2,1,0:T(8,128)S(1)} custom-call(s32[4]{0:T(128)} %pad_add_fusion.place_ref, bf16[128,512]{1,0:T(8,128)(2,1)S(1)} %hidden.1.hidden_ref, bf16[128,512]{1,0:T(8,128)(2,1)S(1)} %collective-permute-done.27.other_ref, bf16[512,1024]{1,0:T(8,128)(2,1)} %refs_0_.3, bf16[512,1024]{1,0:T(8,128)(2,1)} %collective-permute-done.28.refs_1_, ...), custom_call_target="tpu_custom_call" | custom-call | tf_op jit(solution)/shard_map/down_keep/pallas_call | solution.py:211
  209.8 5.2 %collective-permute-done.33 = bf16[4,32,1024]{2,1,0:T(8,128)(2,1)S(1)} collective-permute-done((bf16[4,32,1024]{2,1,0:T(8,128)(2,1)S(1)}, bf16[4,32,1024]{2,1,0:T(8,128)(2,1)S(1)}, u32[]{:S(2)}, u32[]{:S(2)}) %collective-permute-start.33) | collective-permute-done | bytes 262176 | tf_op jit(solution)/shard_map/ppermute | solution.py:43
  215.8 6.0 %collective-permute-done.35 = bf16[4,32,1024]{2,1,0:T(8,128)(2,1)S(1)} collective-permute-done((bf16[4,32,1024]{2,1,0:T(8,128)(2,1)S(1)}, bf16[4,32,1024]{2,1,0:T(8,128)(2,1)S(1)}, u32[]{:S(2)}, u32[]{:S(2)}) %collective-permute-start.35) | collective-permute-done | bytes 262176 | tf_op jit(solution)/shard_map/ppermute | solution.py:43
  222.9 15.3 %all_to_all.26 = bf16[4,32,1024]{2,1,0:T(8,128)(2,1)S(1)} all-to-all(bf16[4,32,1024]{2,1,0:T(8,128)(2,1)S(1)} %fusion.6), channel_id=1, replica_groups=mesh['c'=2,'yh'=2,'x'=4,'zh'=4,'zl'=2,'yl'=2] {'zh'}, dimensions={0} | all-to-all | bytes 524288 | tf_op jit(solution)/shard_map/all_to_all | solution.py:39
  240.8 10.1 %collective-permute-done.36 = bf16[32,1024]{1,0:T(8,128)(2,1)S(1)} collective-permute-done((bf16[32,1024]{1,0:T(8,128)(2,1)S(1)}, bf16[32,1024]{1,0:T(8,128)(2,1)S(1)}, u32[]{:S(2)}, u32[]{:S(2)}) %collective-permute-start.36) | collective-permute-done | bytes 65568 | tf_op jit(solution)/shard_map/ppermute | solution.py:57
  (119 shorter events, 71.3 us)
Async XLA Ops:
  23.7 10.5 %collective-permute-start.6 = (bf16[4,128,256]{2,1,0:T(8,128)(2,1)S(1)}, bf16[4,128,256]{2,1,0:T(8,128)(2,1)S(1)}, u32[]{:S(2)}, u32[]{:S(2)}) collective-permute-start(bf16[4,128,256]{2,1,0:T(8,128)(2,1)S(1)} %all_to_all.25.refs_0_), channel_id=1, source_target_pairs={{0,128},{128,0},{1,129},{129,1},{2,130},{130,2},{3,131},{131,3},{4... | collective-permute-start | bytes 786440 | tf_op jit(solution)/shard_map/ppermute | solution.py:318
  43.0 21.5 %all-to-all-start.1 = ((bf16[32,64,128]{2,1,0:T(8,128)(2,1)}), bf16[32,64,128]{2,1,0:T(8,128)(2,1)S(1)}, u32[]{:S(2)}, u32[]{:S(2)}) async-start(bf16[32,64,128]{2,1,0:T(8,128)(2,1)} %broadcast_in_dim.10), calls=%async_computation.1 | async-start | bytes 1048576 | tf_op jit(solution)/shard_map/all_to_all | solution.py:39
  72.2 31.0 %collective-permute-start.20 = (bf16[1024,512]{1,0:T(8,128)(2,1)}, bf16[1024,512]{1,0:T(8,128)(2,1)}, u32[]{:S(2)}, u32[]{:S(2)}) collective-permute-start(bf16[1024,512]{1,0:T(8,128)(2,1)} %refs_8_.1), channel_id=1, source_target_pairs={{0,48},{16,0},{32,16},{48,32},{1,49},{17,1},{33,17},{49,33},{2,50}... | collective-permute-start | bytes 3145736 | tf_op jit(solution)/shard_map/ppermute | solution.py:233
  79.8 12.1 %collective-permute-start.11 = (bf16[4,32,1024]{2,1,0:T(8,128)(2,1)}, bf16[4,32,1024]{2,1,0:T(8,128)(2,1)}, u32[]{:S(2)}, u32[]{:S(2)}) collective-permute-start(bf16[4,32,1024]{2,1,0:T(8,128)(2,1)} %get-tuple-element.25), channel_id=1, source_target_pairs={{0,3},{1,2},{2,1},{3,0},{4,7},{5,6},{6,5},{7,4},{8,11},{9,10},{10,... | collective-permute-start | bytes 786440 | tf_op jit(solution)/shard_map/ppermute | solution.py:43
  80.1 13.6 %collective-permute-start.9 = (bf16[4,32,1024]{2,1,0:T(8,128)(2,1)}, bf16[4,32,1024]{2,1,0:T(8,128)(2,1)}, u32[]{:S(2)}, u32[]{:S(2)}) collective-permute-start(bf16[4,32,1024]{2,1,0:T(8,128)(2,1)} %get-tuple-element.24), channel_id=1, source_target_pairs={{0,1},{1,0},{2,3},{3,2},{4,5},{5,4},{6,7},{7,6},{8,9},{9,8},{10,11... | collective-permute-start | bytes 786440 | tf_op jit(solution)/shard_map/ppermute | solution.py:43
  81.9 30.0 %collective-permute-start.24 = (bf16[1024,512]{1,0:T(8,128)(2,1)}, bf16[1024,512]{1,0:T(8,128)(2,1)}, u32[]{:S(2)}, u32[]{:S(2)}) collective-permute-start(bf16[1024,512]{1,0:T(8,128)(2,1)} %refs_12_.1), channel_id=1, source_target_pairs={{0,16},{16,32},{32,48},{48,0},{1,17},{17,33},{33,49},{49,1},{2,18}... | collective-permute-start | bytes 3145736 | tf_op jit(solution)/shard_map/ppermute | solution.py:233
  87.5 43.0 %collective-permute-start.22 = (bf16[1024,512]{1,0:T(8,128)(2,1)}, bf16[1024,512]{1,0:T(8,128)(2,1)S(1)}, u32[]{:S(2)}, u32[]{:S(2)}) collective-permute-start(bf16[1024,512]{1,0:T(8,128)(2,1)} %refs_8_.1), channel_id=1, source_target_pairs={{0,16},{16,32},{32,48},{48,0},{1,17},{17,33},{33,49},{49,1},{2,18}... | collective-permute-start | bytes 3145736 | tf_op jit(solution)/shard_map/ppermute | solution.py:233
  92.0 45.7 %collective-permute-start.23 = (bf16[1024,512]{1,0:T(8,128)(2,1)}, bf16[1024,512]{1,0:T(8,128)(2,1)}, u32[]{:S(2)}, u32[]{:S(2)}) collective-permute-start(bf16[1024,512]{1,0:T(8,128)(2,1)} %refs_12_.1), channel_id=1, source_target_pairs={{0,48},{16,0},{32,16},{48,32},{1,49},{17,1},{33,17},{49,33},{2,50}... | collective-permute-start | bytes 3145736 | tf_op jit(solution)/shard_map/ppermute | solution.py:233
  93.7 53.6 %collective-permute-start.28 = (bf16[512,1024]{1,0:T(8,128)(2,1)}, bf16[512,1024]{1,0:T(8,128)(2,1)}, u32[]{:S(2)}, u32[]{:S(2)}) collective-permute-start(bf16[512,1024]{1,0:T(8,128)(2,1)} %refs_0_.3), channel_id=1, source_target_pairs={{0,48},{16,0},{32,16},{48,32},{1,49},{17,1},{33,17},{49,33},{2,50}... | collective-permute-start | bytes 3145736 | tf_op jit(solution)/shard_map/ppermute | solution.py:233
  97.3 14.5 %all-to-all-start.2 = ((bf16[4,32,1024]{2,1,0:T(8,128)(2,1)}), bf16[4,32,1024]{2,1,0:T(8,128)(2,1)S(1)}, u32[]{:S(2)}, u32[]{:S(2)}) async-start(bf16[4,32,1024]{2,1,0:T(8,128)(2,1)} %fusion.11), calls=%async_computation.2 | async-start | bytes 524288 | tf_op jit(solution)/shard_map/all_to_all | solution.py:39
  103.2 49.9 %collective-permute-start.30 = (bf16[512,1024]{1,0:T(8,128)(2,1)}, bf16[512,1024]{1,0:T(8,128)(2,1)}, u32[]{:S(2)}, u32[]{:S(2)}) collective-permute-start(bf16[512,1024]{1,0:T(8,128)(2,1)} %refs_0_.3), channel_id=1, source_target_pairs={{0,16},{16,32},{32,48},{48,0},{1,17},{17,33},{33,49},{49,1},{2,18}... | collective-permute-start | bytes 3145736 | tf_op jit(solution)/shard_map/ppermute | solution.py:233
  111.8 53.4 %collective-permute-start.21 = (bf16[1024,512]{1,0:T(8,128)(2,1)}, bf16[1024,512]{1,0:T(8,128)(2,1)}, u32[]{:S(2)}, u32[]{:S(2)}) collective-permute-start(bf16[1024,512]{1,0:T(8,128)(2,1)} %collective-permute-done.20.refs_9_), channel_id=1, source_target_pairs={{0,48},{16,0},{32,16},{48,32},{1,49},{17,1},{33,17},{49,33},{2,50}... | collective-permute-start | bytes 3145736 | tf_op jit(solution)/shard_map/ppermute | solution.py:233
  131.3 42.4 %collective-permute-start.25 = (bf16[1024,512]{1,0:T(8,128)(2,1)}, bf16[1024,512]{1,0:T(8,128)(2,1)}, u32[]{:S(2)}, u32[]{:S(2)}) collective-permute-start(bf16[1024,512]{1,0:T(8,128)(2,1)} %collective-permute-done.24.refs_15_), channel_id=1, source_target_pairs={{0,16},{16,32},{32,48},{48,0},{1,17},{17,33},{33,49},{49,1},{2,18}... | collective-permute-start | bytes 3145736 | tf_op jit(solution)/shard_map/ppermute | solution.py:233
  133.5 13.2 %all-to-all-start.3 = ((bf16[4,32,1024]{2,1,0:T(8,128)(2,1)}), bf16[4,32,1024]{2,1,0:T(8,128)(2,1)S(1)}, u32[]{:S(2)}, u32[]{:S(2)}) async-start(bf16[4,32,1024]{2,1,0:T(8,128)(2,1)} %broadcast_in_dim.12), calls=%async_computation.3 | async-start | bytes 524288 | tf_op jit(solution)/shard_map/all_to_all | solution.py:39
  146.7 18.5 %collective-permute-start.13 = (bf16[4,32,1024]{2,1,0:T(8,128)(2,1)S(1)}, bf16[4,32,1024]{2,1,0:T(8,128)(2,1)S(1)}, u32[]{:S(2)}, u32[]{:S(2)}) collective-permute-start(bf16[4,32,1024]{2,1,0:T(8,128)(2,1)S(1)} %all-to-all-done.3.refs_0_), channel_id=1, source_target_pairs={{0,1},{1,0},{2,3},{3,2},{4,5},{5,4},{6,7},{7,6},{8,9},{9,8},{10,11... | collective-permute-start | bytes 786440 | tf_op jit(solution)/shard_map/ppermute | solution.py:43
  147.3 18.5 %collective-permute-start.14 = (bf16[4,32,1024]{2,1,0:T(8,128)(2,1)S(1)}, bf16[4,32,1024]{2,1,0:T(8,128)(2,1)S(1)}, u32[]{:S(2)}, u32[]{:S(2)}) collective-permute-start(bf16[4,32,1024]{2,1,0:T(8,128)(2,1)S(1)} %all-to-all-done.3.refs_0_), channel_id=1, source_target_pairs={{0,2},{1,3},{2,0},{3,1},{4,6},{5,7},{6,4},{7,5},{8,10},{9,11},{10,... | collective-permute-start | bytes 786440 | tf_op jit(solution)/shard_map/ppermute | solution.py:43
  153.2 12.7 %collective-permute-start.15 = (bf16[4,32,1024]{2,1,0:T(8,128)(2,1)S(1)}, bf16[4,32,1024]{2,1,0:T(8,128)(2,1)S(1)}, u32[]{:S(2)}, u32[]{:S(2)}) collective-permute-start(bf16[4,32,1024]{2,1,0:T(8,128)(2,1)S(1)} %all-to-all-done.3.refs_0_), channel_id=1, source_target_pairs={{0,3},{1,2},{2,1},{3,0},{4,7},{5,6},{6,5},{7,4},{8,11},{9,10},{10,... | collective-permute-start | bytes 786440 | tf_op jit(solution)/shard_map/ppermute | solution.py:43
  165.2 11.1 %collective-permute-start.17 = (bf16[4,32,1024]{2,1,0:T(8,128)(2,1)S(1)}, bf16[4,32,1024]{2,1,0:T(8,128)(2,1)S(1)}, u32[]{:S(2)}, u32[]{:S(2)}) collective-permute-start(bf16[4,32,1024]{2,1,0:T(8,128)(2,1)S(1)} %collective-permute-done.13.refs_1_), channel_id=1, source_target_pairs={{0,128},{128,0},{1,129},{129,1},{2,130},{130,2},{3,131},{131,3},{4... | collective-permute-start | bytes 786440 | tf_op jit(solution)/shard_map/ppermute | solution.py:318
  165.7 10.6 %collective-permute-start.18 = (bf16[4,32,1024]{2,1,0:T(8,128)(2,1)S(1)}, bf16[4,32,1024]{2,1,0:T(8,128)(2,1)S(1)}, u32[]{:S(2)}, u32[]{:S(2)}) collective-permute-start(bf16[4,32,1024]{2,1,0:T(8,128)(2,1)S(1)} %collective-permute-done.14.refs_2_), channel_id=1, source_target_pairs={{0,128},{128,0},{1,129},{129,1},{2,130},{130,2},{3,131},{131,3},{4... | collective-permute-start | bytes 786440 | tf_op jit(solution)/shard_map/ppermute | solution.py:318
  165.8 10.5 %collective-permute-start.19 = (bf16[4,32,1024]{2,1,0:T(8,128)(2,1)S(1)}, bf16[4,32,1024]{2,1,0:T(8,128)(2,1)S(1)}, u32[]{:S(2)}, u32[]{:S(2)}) collective-permute-start(bf16[4,32,1024]{2,1,0:T(8,128)(2,1)S(1)} %collective-permute-done.15.refs_3_), channel_id=1, source_target_pairs={{0,128},{128,0},{1,129},{129,1},{2,130},{130,2},{3,131},{131,3},{4... | collective-permute-start | bytes 786440 | tf_op jit(solution)/shard_map/ppermute | solution.py:318
  173.6 20.3 %collective-permute-start.29 = (bf16[256,1024]{1,0:T(8,128)(2,1)}, bf16[256,1024]{1,0:T(8,128)(2,1)S(1)}, u32[]{:S(2)}, u32[]{:S(2)}) collective-permute-start(bf16[256,1024]{1,0:T(8,128)(2,1)} %slice.118), channel_id=1, source_target_pairs={{0,48},{16,0},{32,16},{48,32},{1,49},{17,1},{33,17},{49,33},{2,50}... | collective-permute-start | bytes 1572872 | tf_op jit(solution)/shard_map/ppermute | solution.py:233
  175.1 18.8 %collective-permute-start.31 = (bf16[256,1024]{1,0:T(8,128)(2,1)}, bf16[256,1024]{1,0:T(8,128)(2,1)}, u32[]{:S(2)}, u32[]{:S(2)}) collective-permute-start(bf16[256,1024]{1,0:T(8,128)(2,1)} %slice.119), channel_id=1, source_target_pairs={{0,16},{16,32},{32,48},{48,0},{1,17},{17,33},{33,49},{49,1},{2,18}... | collective-permute-start | bytes 1572872 | tf_op jit(solution)/shard_map/ppermute | solution.py:233
  208.3 13.5 %collective-permute-start.35 = (bf16[4,32,1024]{2,1,0:T(8,128)(2,1)S(1)}, bf16[4,32,1024]{2,1,0:T(8,128)(2,1)S(1)}, u32[]{:S(2)}, u32[]{:S(2)}) collective-permute-start(bf16[4,32,1024]{2,1,0:T(8,128)(2,1)S(1)} %get-tuple-element.22), channel_id=1, source_target_pairs={{0,3},{1,2},{2,1},{3,0},{4,7},{5,6},{6,5},{7,4},{8,11},{9,10},{10,... | collective-permute-start | bytes 786440 | tf_op jit(solution)/shard_map/ppermute | solution.py:43
  238.3 12.6 %collective-permute-start.36 = (bf16[32,1024]{1,0:T(8,128)(2,1)S(1)}, bf16[32,1024]{1,0:T(8,128)(2,1)S(1)}, u32[]{:S(2)}, u32[]{:S(2)}) collective-permute-start(bf16[32,1024]{1,0:T(8,128)(2,1)S(1)} %add_convert_fusion), channel_id=1, source_target_pairs={{0,0},{1,1},{2,2},{3,3},{4,16},{5,17},{6,18},{7,19},{8,32},{9,33},... | collective-permute-start | bytes 196616 | tf_op jit(solution)/shard_map/ppermute | solution.py:57
  (24 other events, 237.3 us)

commit v3 on v2

--- a/solution.py
+++ b/solution.py
@@ -187,15 +187,12 @@
 
 def down_terms(place, hidden, other, weights, give):
     n, rows = len(weights), hidden.shape[0]
-    depth, cols = weights[0][0].shape
-    arrays = [(t, k, i * t.shape[0]) for k, parts in enumerate(weights) for i, t in enumerate(parts)]
-    count = len(arrays)
+    depth, cols = weights[0].shape
 
     def body(place_ref, hidden_ref, other_ref, *refs):
-        weights, out_ref, w, sem = refs[:count], refs[count], refs[count + 1], refs[count + 2]
+        weights, out_ref, w, sem = refs[:n], refs[n], refs[n + 1], refs[n + 2]
         copies = [
-            pltpu.make_async_copy(ref, w.at[k, pl.ds(at, t.shape[0])], sem.at[i])
-            for i, (ref, (t, k, at)) in enumerate(zip(weights, arrays))
+            pltpu.make_async_copy(weights[k], w.at[k], sem.at[k]) for k in range(n)
         ]
         for copy in copies:
             copy.start()
@@ -203,19 +200,17 @@
         own = jnp.logical_not(same) if give else same
         lhs = jnp.where(own, hidden_ref[...], other_ref[...])
         for k in range(n):
-            for copy, (_, owner, _) in zip(copies, arrays):
-                if owner == k:
-                    copy.wait()
+            copies[k].wait()
             out_ref[k] = dot(lhs, w[k]).astype(out_ref.dtype)
 
     return pl.pallas_call(
         body,
         out_shape=pltpu.VMEM((n, rows, cols), BF16 if give else F32),
-        in_specs=[SMEM, VMEM, VMEM] + [HBM] * count,
+        in_specs=[SMEM, VMEM, VMEM] + [HBM] * n,
         out_specs=VMEM,
-        scratch_shapes=[pltpu.VMEM((n, depth, cols), BF16), pltpu.SemaphoreType.DMA((count,))],
+        scratch_shapes=[pltpu.VMEM((n, depth, cols), BF16), pltpu.SemaphoreType.DMA((n,))],
         name="down_give" if give else "down_keep",
-    )(place, *in_vmem(hidden, other), *[t for t, _, _ in arrays])
+    )(place, *in_vmem(hidden, other), *weights)
 
 
 def rope_tables(positions):
@@ -299,7 +294,7 @@
     )(place, *in_vmem(gains), w_query, w_keyval, *in_vmem(*arrays, *(sums or ())))
 
 
-def summed(terms, sent):
+def over_square(terms, sent):
     quarter = terms.shape[1] // 4
 
     def both(s):
@@ -307,9 +302,7 @@
         return terms[:, rows] + sent[:, rows].astype(F32)
 
     got = [from_sq(both(s).astype(BF16), s) for s in (1, 2, 3)]
-    mine = both(0) + sum(t.astype(F32) for t in got)
-    tiles = exchange(mine.astype(BF16), "zh")
-    return tiles.astype(F32).sum(axis=0)
+    return (both(0) + sum(t.astype(F32) for t in got)).astype(BF16)
 
 
 def gathered(piece):
@@ -329,16 +322,13 @@
     block_d = dim // 8
     total = rows * n_dp
     quarter = rows // 4
-    hid = w_gate.shape[1]
 
     gate_next, gate_last = from_x(w_gate, 1), from_x(w_gate, 3)
     up_next, up_last = from_x(w_up, 1), from_x(w_up, 3)
     gate_all = [w_gate, gate_next, from_x(gate_next, 1), gate_last]
     up_all = [w_up, up_next, from_x(up_last, 3), up_last]
     down_next, down_last = from_x(w_down, 1), from_x(w_down, 3)
-    part = hid // 2
-    down_far = (from_x(down_next[:part], 1), from_x(down_last[part:], 3))
-    down_all = [(w_down,), (down_next,), down_far, (down_last,)]
+    down_all = [w_down, down_next, from_x(down_next, 1), down_last]
 
     ours, theirs = gathered(tokens_in)
     place = jnp.stack([core, spot, x, y_hi]).astype(jnp.int32)
@@ -390,10 +380,14 @@
     ]
     resid = jnp.stack(resid, axis=0)
     resid = jnp.concatenate([pick(resid, j ^ spot) for j in range(4)], axis=1)
-    mid_part = (resid.astype(F32) + summed(terms, sent)).astype(BF16)
+    tiles = over_square(terms, sent)
+    tiles = exchange(tiles, "zh")
+    mid_part = (resid.astype(F32) + tiles.astype(F32).sum(axis=0)).astype(BF16)
     mid_own = move(mid_part, lambda c, yh, **_: {"c": yh, "yh": c})
 
     ours, theirs = gathered(mid_own)
+
+    resid = move(mid_own, lambda x, zh, **_: {"x": (x + zh) % NX, "zh": x})
 
     gains_mlp = gain_mlp.astype(F32).reshape(n_dp, 1, block_d)
     sent, keep, square = gate_up_terms(place, gains_mlp, ours + theirs, gate_all, up_all)
@@ -404,8 +398,16 @@
     sent = down_terms(place, hidden, other, down_all, True)
     sent = lax.ppermute(sent, "c", SWAP)
     terms = down_terms(place, hidden, other, down_all, False)
-    done = (mid_own.astype(F32) + summed(terms, sent)).astype(BF16)
-    return move(done, lambda x, zh, **_: {"x": (x + zh) % NX, "zh": x})
+    tiles = over_square(terms, sent)
+    got = [
+        move(
+            pick(tiles, (z_hi + r) % NX),
+            lambda x, zh, r=r, **_: {"x": (x + zh + r) % NX, "zh": x},
+        )
+        for r in range(NX)
+    ]
+    done = resid.astype(F32) + sum(t.astype(F32) for t in got)
+    return done.astype(BF16)
 
 
 def solution(mesh):

time: 253 us -> 270 us (1.067)
  the two profiles are of different devices: /device:TPU:4 before, /device:TPU:2 now
where the time goes in v3:
time: 270 us; the launch traced here: 269 us
  waiting for transfers between devices  123 us (46%)
  starting transfers between devices  82 us (30%)
  Pallas kernels  26.1 us (10%)
  blocking collectives  19.3 us (7%)
  other arithmetic  11.8 us (4%)
  local copies, waits for them, and re-layouts  5.54 us (2%)
    ppermute x9, waiting for transfers between devices, from_x(): return lax.ppermute(array, 'x', [(i, (i - r) % NX) for i in range(NX)])  43.1 us
    ppermute x12, waiting for transfers between devices, from_sq(): return lax.ppermute(array, ('zl', 'yl'), [(i, i ^ s) for i in range(4)])  30.9 us
    ppermute x7, starting transfers between devices, move(): return lax.ppermute(array, EVERY, moves)  29.5 us
    all_to_all x3, waiting for transfers between devices, exchange(): return lax.all_to_all(tiles, axis, 0, 0, tiled=True)  26.6 us
    all_to_all x3, starting transfers between devices, exchange(): return lax.all_to_all(tiles, axis, 0, 0, tiled=True)  21.8 us
    all_to_all x1, blocking collectives, exchange(): return lax.all_to_all(tiles, axis, 0, 0, tiled=True)  19.3 us
    ppermute x12, starting transfers between devices, from_sq(): return lax.ppermute(array, ('zl', 'yl'), [(i, i ^ s) for i in range(4)])  12.8 us
    ppermute x9, starting transfers between devices, from_x(): return lax.ppermute(array, 'x', [(i, (i - r) % NX) for i in range(NX)])  10 us
  transfers between devices with their start and end apart: 43, of which 20 were waited for; matrix products, arithmetic and copies ran while one was open for 3% of the time, Pallas kernels for 6%

profile of v3, /device:TPU:2, one launch (start us, length us, event | category | flops | bytes accessed | tf_op | source)
XLA Modules:
  0.0 269.2 jit_solution(16329786214578973909)
XLA Ops:
  0.9 19.3 %all_to_all.20.refs_0_ = bf16[4,128,256]{2,1,0:T(8,128)(2,1)S(1)} all-to-all(bf16[4,128,256]{2,1,0:T(8,128)(2,1)S(1)} %broadcast_in_dim.9), channel_id=1, replica_groups=mesh['c'=2,'yh'=2,'x'=4,'zh'=4,'zl'=2,'yl'=2] {'zh'}, dimensions={0} | all-to-all | bytes 524288 | tf_op jit(solution)/shard_map/all_to_all | solution.py:39
  23.7 5.7 %collective-permute-done.refs_0_ = bf16[4,128,256]{2,1,0:T(8,128)(2,1)S(1)} collective-permute-done((bf16[4,128,256]{2,1,0:T(8,128)(2,1)S(1)}, bf16[4,128,256]{2,1,0:T(8,128)(2,1)S(1)}, u32[]{:S(2)}, u32[]{:S(2)}) %collective-permute-start) | collective-permute-done | bytes 262176 | tf_op jit(solution)/shard_map/ppermute | solution.py:43
  36.7 4.7 %project_last.1 = (f32[128,256]{1,0:T(8,128)S(1)}, f32[64,128]{1,0:T(8,128)S(1)}, f32[128,256]{1,0:T(8,128)}) custom-call(s32[4]{0:T(128)} %pad_add_fusion.place_ref, f32[32,1,256]{2,1,0:T(1,128)S(1)} %bitcast.47, bf16[8192,256]{1,0:T(8,128)(2,1)} %wq_hbm.3, bf16[64,8192]{1,0:T(8,128)(2,1)} %bitcast.49, ...), custom_call_target="tpu_custom_call" | custom-call | tf_op jit(solution)/shard_map/project_last/pallas_call | solution.py:282
  43.0 12.9 %all-to-all-start.1 = ((bf16[32,64,128]{2,1,0:T(8,128)(2,1)}), bf16[32,64,128]{2,1,0:T(8,128)(2,1)S(1)}, u32[]{:S(2)}, u32[]{:S(2)}) async-start(bf16[32,64,128]{2,1,0:T(8,128)(2,1)} %broadcast_in_dim.10), calls=%async_computation.1 | async-start | bytes 1048576 | tf_op jit(solution)/shard_map/all_to_all | solution.py:39
  56.4 8.6 %all-to-all-done.1 = bf16[32,64,128]{2,1,0:T(8,128)(2,1)S(1)} async-done(((bf16[32,64,128]{2,1,0:T(8,128)(2,1)}), bf16[32,64,128]{2,1,0:T(8,128)(2,1)S(1)}, u32[]{:S(2)}, u32[]{:S(2)}) %all-to-all-start.1) | async-done | bytes 524320 | tf_op jit(solution)/shard_map/all_to_all | solution.py:39
  87.9 3.8 %collective-permute-done.11 = bf16[4,32,1024]{2,1,0:T(8,128)(2,1)S(1)} collective-permute-done((bf16[4,32,1024]{2,1,0:T(8,128)(2,1)}, bf16[4,32,1024]{2,1,0:T(8,128)(2,1)S(1)}, u32[]{:S(2)}, u32[]{:S(2)}) %collective-permute-start.11) | collective-permute-done | bytes 262176 | tf_op jit(solution)/shard_map/ppermute | solution.py:43
  96.5 4.5 %all-to-all-start.2 = ((bf16[4,32,1024]{2,1,0:T(8,128)(2,1)}), bf16[4,32,1024]{2,1,0:T(8,128)(2,1)S(1)}, u32[]{:S(2)}, u32[]{:S(2)}) async-start(bf16[4,32,1024]{2,1,0:T(8,128)(2,1)} %fusion.11), calls=%async_computation.2 | async-start | bytes 524288 | tf_op jit(solution)/shard_map/all_to_all | solution.py:39
  102.4 8.7 %all-to-all-done.2 = bf16[4,32,1024]{2,1,0:T(8,128)(2,1)S(1)} async-done(((bf16[4,32,1024]{2,1,0:T(8,128)(2,1)}), bf16[4,32,1024]{2,1,0:T(8,128)(2,1)S(1)}, u32[]{:S(2)}, u32[]{:S(2)}) %all-to-all-start.2) | async-done | bytes 262176 | tf_op jit(solution)/shard_map/all_to_all | solution.py:39
  111.8 17.8 %collective-permute-done.25.refs_15_ = bf16[1024,512]{1,0:T(8,128)(2,1)} collective-permute-done((bf16[1024,512]{1,0:T(8,128)(2,1)}, bf16[1024,512]{1,0:T(8,128)(2,1)}, u32[]{:S(2)}, u32[]{:S(2)}) %collective-permute-start.25) | collective-permute-done | bytes 1048608 | tf_op jit(solution)/shard_map/ppermute | solution.py:228
  133.9 4.5 %all-to-all-start.3 = ((bf16[4,32,1024]{2,1,0:T(8,128)(2,1)}), bf16[4,32,1024]{2,1,0:T(8,128)(2,1)S(1)}, u32[]{:S(2)}, u32[]{:S(2)}) async-start(bf16[4,32,1024]{2,1,0:T(8,128)(2,1)} %broadcast_in_dim.12), calls=%async_computation.3 | async-start | bytes 524288 | tf_op jit(solution)/shard_map/all_to_all | solution.py:39
  138.3 9.3 %all-to-all-done.3.refs_0_ = bf16[4,32,1024]{2,1,0:T(8,128)(2,1)S(1)} async-done(((bf16[4,32,1024]{2,1,0:T(8,128)(2,1)}), bf16[4,32,1024]{2,1,0:T(8,128)(2,1)S(1)}, u32[]{:S(2)}, u32[]{:S(2)}) %all-to-all-start.3) | async-done | bytes 262176 | tf_op jit(solution)/shard_map/all_to_all | solution.py:39
  148.3 4.3 %collective-permute-done.29.refs_1_ = bf16[512,1024]{1,0:T(8,128)(2,1)} collective-permute-done((bf16[512,1024]{1,0:T(8,128)(2,1)}, bf16[512,1024]{1,0:T(8,128)(2,1)}, u32[]{:S(2)}, u32[]{:S(2)}) %collective-permute-start.29) | collective-permute-done | bytes 1048608 | tf_op jit(solution)/shard_map/ppermute | solution.py:228
  154.0 21.0 %collective-permute-done.22.refs_10_ = bf16[1024,512]{1,0:T(8,128)(2,1)} collective-permute-done((bf16[1024,512]{1,0:T(8,128)(2,1)}, bf16[1024,512]{1,0:T(8,128)(2,1)}, u32[]{:S(2)}, u32[]{:S(2)}) %collective-permute-start.22) | collective-permute-done | bytes 1048608 | tf_op jit(solution)/shard_map/ppermute | solution.py:228
  176.8 5.9 %collective-permute-done.15.refs_2_ = bf16[4,32,1024]{2,1,0:T(8,128)(2,1)S(1)} collective-permute-done((bf16[4,32,1024]{2,1,0:T(8,128)(2,1)S(1)}, bf16[4,32,1024]{2,1,0:T(8,128)(2,1)S(1)}, u32[]{:S(2)}, u32[]{:S(2)}) %collective-permute-start.15) | collective-permute-done | bytes 262176 | tf_op jit(solution)/shard_map/ppermute | solution.py:43
  187.2 5.9 %gate_up.1 = (bf16[128,1152]{1,0:T(8,128)(2,1)S(1)}, f32[128,1024]{1,0:T(8,128)}, f32[128,128]{1,0:T(8,128)}) custom-call(s32[4]{0:T(128)} %pad_add_fusion.place_ref, f32[8,1,1024]{2,1,0:T(1,128)} %bitcast.52, bf16[4,32,1024]{2,1,0:T(8,128)(2,1)S(1)} %all-to-all-done.3.refs_0_, bf16[4,32,1024]{2,1,0:T(8,128)(2,1)S(1)} %collective-permute-done.14.refs_1_, ...), custom_call_target="tpu_custom_call" | custom-call | tf_op jit(solution)/shard_map/gate_up/pallas_call | solution.py:150
  195.3 8.4 %collective-permute-done.27.sent_ref = bf16[128,1152]{1,0:T(8,128)(2,1)S(1)} collective-permute-done((bf16[128,1152]{1,0:T(8,128)(2,1)S(1)}, bf16[128,1152]{1,0:T(8,128)(2,1)S(1)}, u32[]{:S(2)}, u32[]{:S(2)}) %collective-permute-start.27) | collective-permute-done | bytes 294944 | tf_op jit(solution)/shard_map/ppermute | solution.py:394
  207.2 4.3 %collective-permute-done.28.other_ref = bf16[128,512]{1,0:T(8,128)(2,1)S(1)} collective-permute-done((bf16[128,512]{1,0:T(8,128)(2,1)S(1)}, bf16[128,512]{1,0:T(8,128)(2,1)S(1)}, u32[]{:S(2)}, u32[]{:S(2)}) %collective-permute-start.28) | collective-permute-done | bytes 131104 | tf_op jit(solution)/shard_map/ppermute | solution.py:397
  211.6 3.2 %down_give.1 = bf16[4,128,1024]{2,1,0:T(8,128)(2,1)S(1)} custom-call(s32[4]{0:T(128)} %pad_add_fusion.place_ref, bf16[128,512]{1,0:T(8,128)(2,1)S(1)} %hidden.1.hidden_ref, bf16[128,512]{1,0:T(8,128)(2,1)S(1)} %collective-permute-done.28.other_ref, bf16[512,1024]{1,0:T(8,128)(2,1)} %refs_0_.3, bf16[512,1024]{1,0:T(8,128)(2,1)} %collective-permute-done.29.refs_1_, ...), custom_call_target="tpu_custom_call" | custom-call | tf_op jit(solution)/shard_map/down_give/pallas_call | solution.py:206
  214.8 3.2 %down_keep.1 = f32[4,128,1024]{2,1,0:T(8,128)S(1)} custom-call(s32[4]{0:T(128)} %pad_add_fusion.place_ref, bf16[128,512]{1,0:T(8,128)(2,1)S(1)} %hidden.1.hidden_ref, bf16[128,512]{1,0:T(8,128)(2,1)S(1)} %collective-permute-done.28.other_ref, bf16[512,1024]{1,0:T(8,128)(2,1)} %refs_0_.3, bf16[512,1024]{1,0:T(8,128)(2,1)} %collective-permute-done.29.refs_1_, ...), custom_call_target="tpu_custom_call" | custom-call | tf_op jit(solution)/shard_map/down_keep/pallas_call | solution.py:206
  223.7 5.6 %collective-permute-start.13 = (bf16[32,1024]{1,0:T(8,128)(2,1)S(1)}, bf16[32,1024]{1,0:T(8,128)(2,1)S(1)}, u32[]{:S(2)}, u32[]{:S(2)}) collective-permute-start(bf16[32,1024]{1,0:T(8,128)(2,1)S(1)} %copy-done.4), channel_id=1, source_target_pairs={{0,0},{1,1},{2,2},{3,3},{4,16},{5,17},{6,18},{7,19},{8,32},{9,33},... | collective-permute-start | bytes 196616 | tf_op jit(solution)/shard_map/ppermute | solution.py:57
  231.0 4.6 %collective-permute-done.35 = bf16[4,32,1024]{2,1,0:T(8,128)(2,1)S(1)} collective-permute-done((bf16[4,32,1024]{2,1,0:T(8,128)(2,1)S(1)}, bf16[4,32,1024]{2,1,0:T(8,128)(2,1)S(1)}, u32[]{:S(2)}, u32[]{:S(2)}) %collective-permute-start.35) | collective-permute-done | bytes 262176 | tf_op jit(solution)/shard_map/ppermute | solution.py:43
  236.8 7.1 %collective-permute-start.36 = (bf16[32,1024]{1,0:T(8,128)(2,1)S(1)}, bf16[32,1024]{1,0:T(8,128)(2,1)S(1)}, u32[]{:S(2)}, u32[]{:S(2)}) collective-permute-start(bf16[32,1024]{1,0:T(8,128)(2,1)S(1)} %get-tuple-element.31), channel_id=1, source_target_pairs={{0,0},{1,1},{2,2},{3,3},{4,16},{5,17},{6,18},{7,19},{8,32},{9,33},... | collective-permute-start | bytes 196616 | tf_op jit(solution)/shard_map/ppermute | solution.py:57
  247.1 10.4 %collective-permute-start.38 = (bf16[32,1024]{1,0:T(8,128)(2,1)S(1)}, bf16[32,1024]{1,0:T(8,128)(2,1)S(1)}, u32[]{:S(2)}, u32[]{:S(2)}) collective-permute-start(bf16[32,1024]{1,0:T(8,128)(2,1)S(1)} %get-tuple-element.33), channel_id=1, source_target_pairs={{0,32},{1,33},{2,34},{3,35},{4,48},{5,49},{6,50},{7,51},{8,0},{9,1... | collective-permute-start | bytes 196616 | tf_op jit(solution)/shard_map/ppermute | solution.py:57
  259.5 9.0 %collective-permute-done.39 = bf16[32,1024]{1,0:T(8,128)(2,1)S(1)} collective-permute-done((bf16[32,1024]{1,0:T(8,128)(2,1)S(1)}, bf16[32,1024]{1,0:T(8,128)(2,1)S(1)}, u32[]{:S(2)}, u32[]{:S(2)}) %collective-permute-start.39) | collective-permute-done | bytes 65568 | tf_op jit(solution)/shard_map/ppermute | solution.py:57
  (117 shorter events, 76.0 us)
Async XLA Ops:
  23.7 10.4 %collective-permute-start.6 = (bf16[4,128,256]{2,1,0:T(8,128)(2,1)S(1)}, bf16[4,128,256]{2,1,0:T(8,128)(2,1)S(1)}, u32[]{:S(2)}, u32[]{:S(2)}) collective-permute-start(bf16[4,128,256]{2,1,0:T(8,128)(2,1)S(1)} %all_to_all.20.refs_0_), channel_id=1, source_target_pairs={{0,128},{128,0},{1,129},{129,1},{2,130},{130,2},{3,131},{131,3},{4... | collective-permute-start | bytes 786440 | tf_op jit(solution)/shard_map/ppermute | solution.py:311
  43.0 21.9 %all-to-all-start.1 = ((bf16[32,64,128]{2,1,0:T(8,128)(2,1)}), bf16[32,64,128]{2,1,0:T(8,128)(2,1)S(1)}, u32[]{:S(2)}, u32[]{:S(2)}) async-start(bf16[32,64,128]{2,1,0:T(8,128)(2,1)} %broadcast_in_dim.10), calls=%async_computation.1 | async-start | bytes 1048576 | tf_op jit(solution)/shard_map/all_to_all | solution.py:39
  79.3 12.5 %collective-permute-start.11 = (bf16[4,32,1024]{2,1,0:T(8,128)(2,1)}, bf16[4,32,1024]{2,1,0:T(8,128)(2,1)S(1)}, u32[]{:S(2)}, u32[]{:S(2)}) collective-permute-start(bf16[4,32,1024]{2,1,0:T(8,128)(2,1)} %get-tuple-element.25), channel_id=1, source_target_pairs={{0,3},{1,2},{2,1},{3,0},{4,7},{5,6},{6,5},{7,4},{8,11},{9,10},{10,... | collective-permute-start | bytes 786440 | tf_op jit(solution)/shard_map/ppermute | solution.py:43
  79.5 14.0 %collective-permute-start.9 = (bf16[4,32,1024]{2,1,0:T(8,128)(2,1)S(1)}, bf16[4,32,1024]{2,1,0:T(8,128)(2,1)S(1)}, u32[]{:S(2)}, u32[]{:S(2)}) collective-permute-start(bf16[4,32,1024]{2,1,0:T(8,128)(2,1)S(1)} %get-tuple-element.24), channel_id=1, source_target_pairs={{0,1},{1,0},{2,3},{3,2},{4,5},{5,4},{6,7},{7,6},{8,9},{9,8},{10,11... | collective-permute-start | bytes 786440 | tf_op jit(solution)/shard_map/ppermute | solution.py:43
  81.3 29.8 %collective-permute-start.21 = (bf16[1024,512]{1,0:T(8,128)(2,1)}, bf16[1024,512]{1,0:T(8,128)(2,1)}, u32[]{:S(2)}, u32[]{:S(2)}) collective-permute-start(bf16[1024,512]{1,0:T(8,128)(2,1)} %refs_8_.1), channel_id=1, source_target_pairs={{0,48},{16,0},{32,16},{48,32},{1,49},{17,1},{33,17},{49,33},{2,50}... | collective-permute-start | bytes 3145736 | tf_op jit(solution)/shard_map/ppermute | solution.py:228
  82.8 55.6 %collective-permute-start.23 = (bf16[1024,512]{1,0:T(8,128)(2,1)}, bf16[1024,512]{1,0:T(8,128)(2,1)}, u32[]{:S(2)}, u32[]{:S(2)}) collective-permute-start(bf16[1024,512]{1,0:T(8,128)(2,1)} %refs_8_.1), channel_id=1, source_target_pairs={{0,16},{16,32},{32,48},{48,0},{1,17},{17,33},{33,49},{49,1},{2,18}... | collective-permute-start | bytes 3145736 | tf_op jit(solution)/shard_map/ppermute | solution.py:228
  87.2 42.4 %collective-permute-start.25 = (bf16[1024,512]{1,0:T(8,128)(2,1)}, bf16[1024,512]{1,0:T(8,128)(2,1)}, u32[]{:S(2)}, u32[]{:S(2)}) collective-permute-start(bf16[1024,512]{1,0:T(8,128)(2,1)} %refs_12_.1), channel_id=1, source_target_pairs={{0,16},{16,32},{32,48},{48,0},{1,17},{17,33},{33,49},{49,1},{2,18}... | collective-permute-start | bytes 3145736 | tf_op jit(solution)/shard_map/ppermute | solution.py:228
  91.8 56.5 %collective-permute-start.24 = (bf16[1024,512]{1,0:T(8,128)(2,1)}, bf16[1024,512]{1,0:T(8,128)(2,1)}, u32[]{:S(2)}, u32[]{:S(2)}) collective-permute-start(bf16[1024,512]{1,0:T(8,128)(2,1)} %refs_12_.1), channel_id=1, source_target_pairs={{0,48},{16,0},{32,16},{48,32},{1,49},{17,1},{33,17},{49,33},{2,50}... | collective-permute-start | bytes 3145736 | tf_op jit(solution)/shard_map/ppermute | solution.py:228
  93.5 59.1 %collective-permute-start.29 = (bf16[512,1024]{1,0:T(8,128)(2,1)}, bf16[512,1024]{1,0:T(8,128)(2,1)}, u32[]{:S(2)}, u32[]{:S(2)}) collective-permute-start(bf16[512,1024]{1,0:T(8,128)(2,1)} %refs_0_.3), channel_id=1, source_target_pairs={{0,48},{16,0},{32,16},{48,32},{1,49},{17,1},{33,17},{49,33},{2,50}... | collective-permute-start | bytes 3145736 | tf_op jit(solution)/shard_map/ppermute | solution.py:228
  96.5 14.6 %all-to-all-start.2 = ((bf16[4,32,1024]{2,1,0:T(8,128)(2,1)}), bf16[4,32,1024]{2,1,0:T(8,128)(2,1)S(1)}, u32[]{:S(2)}, u32[]{:S(2)}) async-start(bf16[4,32,1024]{2,1,0:T(8,128)(2,1)} %fusion.11), calls=%async_computation.2 | async-start | bytes 524288 | tf_op jit(solution)/shard_map/all_to_all | solution.py:39
  111.1 21.4 %collective-permute-start.12 = (bf16[32,1024]{1,0:T(8,128)(2,1)S(1)}, bf16[32,1024]{1,0:T(8,128)(2,1)S(1)}, u32[]{:S(2)}, u32[]{:S(2)}) collective-permute-start(bf16[32,1024]{1,0:T(8,128)(2,1)S(1)} %add_convert_fusion.1), channel_id=1, source_target_pairs={{0,0},{1,1},{2,2},{3,3},{4,4},{5,5},{6,6},{7,7},{8,8},{9,9},{10,10... | collective-permute-start | bytes 196616 | tf_op jit(solution)/shard_map/ppermute | solution.py:57
  129.6 45.5 %collective-permute-start.22 = (bf16[1024,512]{1,0:T(8,128)(2,1)}, bf16[1024,512]{1,0:T(8,128)(2,1)}, u32[]{:S(2)}, u32[]{:S(2)}) collective-permute-start(bf16[1024,512]{1,0:T(8,128)(2,1)} %collective-permute-done.21.refs_9_), channel_id=1, source_target_pairs={{0,48},{16,0},{32,16},{48,32},{1,49},{17,1},{33,17},{49,33},{2,50}... | collective-permute-start | bytes 3145736 | tf_op jit(solution)/shard_map/ppermute | solution.py:228
  132.5 44.0 %collective-permute-start.26 = (bf16[1024,512]{1,0:T(8,128)(2,1)}, bf16[1024,512]{1,0:T(8,128)(2,1)}, u32[]{:S(2)}, u32[]{:S(2)}) collective-permute-start(bf16[1024,512]{1,0:T(8,128)(2,1)} %collective-permute-done.25.refs_15_), channel_id=1, source_target_pairs={{0,16},{16,32},{32,48},{48,0},{1,17},{17,33},{33,49},{49,1},{2,18}... | collective-permute-start | bytes 3145736 | tf_op jit(solution)/shard_map/ppermute | solution.py:228
  133.9 13.8 %all-to-all-start.3 = ((bf16[4,32,1024]{2,1,0:T(8,128)(2,1)}), bf16[4,32,1024]{2,1,0:T(8,128)(2,1)S(1)}, u32[]{:S(2)}, u32[]{:S(2)}) async-start(bf16[4,32,1024]{2,1,0:T(8,128)(2,1)} %broadcast_in_dim.12), calls=%async_computation.3 | async-start | bytes 524288 | tf_op jit(solution)/shard_map/all_to_all | solution.py:39
  147.6 29.2 %collective-permute-start.14 = (bf16[4,32,1024]{2,1,0:T(8,128)(2,1)S(1)}, bf16[4,32,1024]{2,1,0:T(8,128)(2,1)S(1)}, u32[]{:S(2)}, u32[]{:S(2)}) collective-permute-start(bf16[4,32,1024]{2,1,0:T(8,128)(2,1)S(1)} %all-to-all-done.3.refs_0_), channel_id=1, source_target_pairs={{0,1},{1,0},{2,3},{3,2},{4,5},{5,4},{6,7},{7,6},{8,9},{9,8},{10,11... | collective-permute-start | bytes 786440 | tf_op jit(solution)/shard_map/ppermute | solution.py:43
  148.3 59.0 %collective-permute-start.31 = (bf16[512,1024]{1,0:T(8,128)(2,1)}, bf16[512,1024]{1,0:T(8,128)(2,1)}, u32[]{:S(2)}, u32[]{:S(2)}) collective-permute-start(bf16[512,1024]{1,0:T(8,128)(2,1)} %refs_0_.3), channel_id=1, source_target_pairs={{0,16},{16,32},{32,48},{48,0},{1,17},{17,33},{33,49},{49,1},{2,18}... | collective-permute-start | bytes 3145736 | tf_op jit(solution)/shard_map/ppermute | solution.py:228
  152.6 54.6 %collective-permute-start.30 = (bf16[512,1024]{1,0:T(8,128)(2,1)}, bf16[512,1024]{1,0:T(8,128)(2,1)}, u32[]{:S(2)}, u32[]{:S(2)}) collective-permute-start(bf16[512,1024]{1,0:T(8,128)(2,1)} %collective-permute-done.29.refs_1_), channel_id=1, source_target_pairs={{0,48},{16,0},{32,16},{48,32},{1,49},{17,1},{33,17},{49,33},{2,50}... | collective-permute-start | bytes 3145736 | tf_op jit(solution)/shard_map/ppermute | solution.py:228
  193.1 10.6 %collective-permute-start.27 = (bf16[128,1152]{1,0:T(8,128)(2,1)S(1)}, bf16[128,1152]{1,0:T(8,128)(2,1)S(1)}, u32[]{:S(2)}, u32[]{:S(2)}) collective-permute-start(bf16[128,1152]{1,0:T(8,128)(2,1)S(1)} %get-tuple-element.20), channel_id=1, source_target_pairs={{0,64},{64,0},{1,65},{65,1},{2,66},{66,2},{3,67},{67,3},{4,68},{68... | collective-permute-start | bytes 884744 | tf_op jit(solution)/shard_map/ppermute | solution.py:394
  223.3 12.3 %collective-permute-start.35 = (bf16[4,32,1024]{2,1,0:T(8,128)(2,1)S(1)}, bf16[4,32,1024]{2,1,0:T(8,128)(2,1)S(1)}, u32[]{:S(2)}, u32[]{:S(2)}) collective-permute-start(bf16[4,32,1024]{2,1,0:T(8,128)(2,1)S(1)} %get-tuple-element.22), channel_id=1, source_target_pairs={{0,3},{1,2},{2,1},{3,0},{4,7},{5,6},{6,5},{7,4},{8,11},{9,10},{10,... | collective-permute-start | bytes 786440 | tf_op jit(solution)/shard_map/ppermute | solution.py:43
  223.7 35.8 %collective-permute-start.13 = (bf16[32,1024]{1,0:T(8,128)(2,1)S(1)}, bf16[32,1024]{1,0:T(8,128)(2,1)S(1)}, u32[]{:S(2)}, u32[]{:S(2)}) collective-permute-start(bf16[32,1024]{1,0:T(8,128)(2,1)S(1)} %copy-done.4), channel_id=1, source_target_pairs={{0,0},{1,1},{2,2},{3,3},{4,16},{5,17},{6,18},{7,19},{8,32},{9,33},... | collective-permute-start | bytes 196616 | tf_op jit(solution)/shard_map/ppermute | solution.py:57
  236.8 22.6 %collective-permute-start.36 = (bf16[32,1024]{1,0:T(8,128)(2,1)S(1)}, bf16[32,1024]{1,0:T(8,128)(2,1)S(1)}, u32[]{:S(2)}, u32[]{:S(2)}) collective-permute-start(bf16[32,1024]{1,0:T(8,128)(2,1)S(1)} %get-tuple-element.31), channel_id=1, source_target_pairs={{0,0},{1,1},{2,2},{3,3},{4,16},{5,17},{6,18},{7,19},{8,32},{9,33},... | collective-permute-start | bytes 196616 | tf_op jit(solution)/shard_map/ppermute | solution.py:57
  243.9 15.6 %collective-permute-start.37 = (bf16[32,1024]{1,0:T(8,128)(2,1)S(1)}, bf16[32,1024]{1,0:T(8,128)(2,1)S(1)}, u32[]{:S(2)}, u32[]{:S(2)}) collective-permute-start(bf16[32,1024]{1,0:T(8,128)(2,1)S(1)} %get-tuple-element.34), channel_id=1, source_target_pairs={{0,16},{1,17},{2,18},{3,19},{4,32},{5,33},{6,34},{7,35},{8,48},{9,... | collective-permute-start | bytes 196616 | tf_op jit(solution)/shard_map/ppermute | solution.py:57
  247.1 12.4 %collective-permute-start.38 = (bf16[32,1024]{1,0:T(8,128)(2,1)S(1)}, bf16[32,1024]{1,0:T(8,128)(2,1)S(1)}, u32[]{:S(2)}, u32[]{:S(2)}) collective-permute-start(bf16[32,1024]{1,0:T(8,128)(2,1)S(1)} %get-tuple-element.33), channel_id=1, source_target_pairs={{0,32},{1,33},{2,34},{3,35},{4,48},{5,49},{6,50},{7,51},{8,0},{9,1... | collective-permute-start | bytes 196616 | tf_op jit(solution)/shard_map/ppermute | solution.py:57
  257.5 11.0 %collective-permute-start.39 = (bf16[32,1024]{1,0:T(8,128)(2,1)S(1)}, bf16[32,1024]{1,0:T(8,128)(2,1)S(1)}, u32[]{:S(2)}, u32[]{:S(2)}) collective-permute-start(bf16[32,1024]{1,0:T(8,128)(2,1)S(1)} %get-tuple-element.32), channel_id=1, source_target_pairs={{0,48},{1,49},{2,50},{3,51},{4,0},{5,1},{6,2},{7,3},{8,16},{9,17},... | collective-permute-start | bytes 196616 | tf_op jit(solution)/shard_map/ppermute | solution.py:57
  (25 other events, 246.7 us)

commit v4 on v1

--- a/solution.py
+++ b/solution.py
@@ -104,77 +104,76 @@
     )(place, *in_vmem(attended), w_out)
 
 
-def gate_up_terms(place, gains, pieces, weights):
+def hidden_terms(place, gains, pieces, weights, first):
     n, part, depth = pieces[0].shape
     rows, cols, count = 4 * part, weights[0].shape[1], len(pieces)
 
     def body(place_ref, gain_ref, *refs):
         pieces, weights, refs = refs[:count], refs[count : count + n], refs[count + n :]
-        give_ref, keep_ref, square_ref, w, acc, sq, sem = refs
+        give_ref, keep_ref = refs[:2]
+        w, acc, sq, sem = refs[-4:]
         copies = [
             pltpu.make_async_copy(weights[k], w.at[k], sem.at[k]) for k in range(n)
         ]
         for copy in copies:
             copy.start()
         for k in range(n):
-            lhs = jnp.concatenate([p[k] for p in pieces], axis=0)
-            wide = lhs.astype(F32)
-            square = jnp.sum(wide * wide, axis=1, keepdims=True)
+            wide = jnp.concatenate([p[k] for p in pieces], axis=0).astype(F32)
+            gain = gain_ref[place_ref[3] * n + (place_ref[2] + k) % n]
+            lhs = (wide * gain).astype(BF16)
             copies[k].wait()
-            gain = gain_ref[place_ref[3] * n + (place_ref[2] + k) % n]
-            out = dot((wide * gain).astype(BF16), w[k])
-            if k == 0:
-                acc[...], sq[...] = out, jnp.broadcast_to(square, sq.shape)
-            else:
-                acc[...] += out
-                sq[...] += square
+            out = dot(lhs, w[k])
+            acc[...] = out if k == 0 else acc[...] + out
+            if first:
+                square = jnp.sum(wide * wide, axis=1, keepdims=True)
+                square = jnp.broadcast_to(square, sq.shape)
+                sq[...] = square if k == 0 else sq[...] + square
         keep = pl.multiple_of((place_ref[3] ^ place_ref[0]) * rows, rows)
         give = pl.multiple_of(((1 - place_ref[3]) ^ place_ref[0]) * rows, rows)
         give_ref[:, :cols] = acc[pl.ds(give, rows)].astype(BF16)
-        square = sq[pl.ds(give, rows)]
-        top = square.astype(BF16)
-        low = (square - top.astype(F32)).astype(BF16)
-        lane = lax.broadcasted_iota(jnp.int32, square.shape, 1)
-        give_ref[:, cols:] = jnp.where(lane == 0, top.astype(F32), low.astype(F32)).astype(BF16)
         keep_ref[...] = acc[pl.ds(keep, rows)]
-        square_ref[...] = sq[pl.ds(keep, rows)]
-
+        if first:
+            square = sq[pl.ds(give, rows)]
+            top = square.astype(BF16).astype(F32)
+            lane = lax.broadcasted_iota(jnp.int32, square.shape, 1)
+            give_ref[:, cols:] = jnp.where(lane == 0, top, square - top).astype(BF16)
+            refs[2][...] = sq[pl.ds(keep, rows)]
+
+    keeps = [(rows, cols), (rows, 128)][: 2 if first else 1]
     return pl.pallas_call(
         body,
-        out_shape=[
-            pltpu.VMEM((rows, cols + 128), BF16),
-            jax.ShapeDtypeStruct((rows, cols), F32),
-            jax.ShapeDtypeStruct((rows, 128), F32),
-        ],
+        out_shape=[pltpu.VMEM((rows, cols + (128 if first else 0)), BF16)]
+        + [jax.ShapeDtypeStruct(shape, F32) for shape in keeps],
         in_specs=[SMEM, VMEM] + [VMEM] * count + [HBM] * n,
-        out_specs=[VMEM] * 3,
+        out_specs=[VMEM] * (1 + len(keeps)),
         scratch_shapes=[
             pltpu.VMEM((n, depth, cols), BF16),
             pltpu.VMEM((2 * rows, cols), F32),
             pltpu.VMEM((2 * rows, 128), F32),
             pltpu.SemaphoreType.DMA((n,)),
         ],
-        name="gate_up",
+        name="gate" if first else "up",
     )(place, gains, *in_vmem(*pieces), *weights)
 
 
-def hidden_units(keep, square, sent, dim):
-    rows, cols = keep.shape
-
-    def body(keep_ref, square_ref, sent_ref, out_ref):
-        extra = sent_ref[:, cols:].astype(F32)
+def hidden_units(gate, up, square, sent_gate, sent_up, dim):
+    rows, cols = gate.shape
+
+    def body(gate_ref, up_ref, square_ref, sent_gate_ref, sent_up_ref, out_ref):
+        extra = sent_gate_ref[:, cols:].astype(F32)
         mean = (square_ref[:, :1] + extra[:, :1] + extra[:, 1:2]) / dim
-        out = (keep_ref[...] + sent_ref[:, :cols].astype(F32)) * lax.rsqrt(mean + EPS)
-        gate, up = out[:, : cols // 2], out[:, cols // 2 :]
+        factor = lax.rsqrt(mean + EPS)
+        gate = (gate_ref[...] + sent_gate_ref[:, :cols].astype(F32)) * factor
+        up = (up_ref[...] + sent_up_ref[...].astype(F32)) * factor
         out_ref[...] = (gate / (1.0 + jnp.exp(-gate)) * up).astype(BF16)
 
     return pl.pallas_call(
         body,
-        out_shape=pltpu.VMEM((rows, cols // 2), BF16),
-        in_specs=[VMEM] * 3,
+        out_shape=pltpu.VMEM((rows, cols), BF16),
+        in_specs=[VMEM] * 5,
         out_specs=VMEM,
         name="hidden",
-    )(keep, square, *in_vmem(sent))
+    )(gate, up, square, *in_vmem(sent_gate, sent_up))
 
 
 def down_terms(place, hidden, other, weights, give):
@@ -220,73 +219,95 @@
     return lax.ppermute(array, "x", [(i, (i - r) % NX) for i in range(NX)])
 
 
-def project(place, pieces, gains, w_query, w_keyval, sums):
+def project(place, pieces, gains, w_query, w_keyval, mode, sums=()):
     arrays = [piece for piece, _, _ in pieces]
     n_z, rows, width = arrays[0].shape
     n_q, n_kv = w_query.shape[1], w_keyval.shape[0]
     steps = n_z * len(arrays)
-    last = sums is not None
+    do_q, do_kv = mode != "kv", mode != "q"
 
     def body(place_ref, gain_ref, wq_hbm, wkv_hbm, *refs):
         refs, rest = refs[: len(arrays)], refs[len(arrays) :]
-        before, rest = (rest[:3], rest[3:]) if last else (None, rest)
-        q_ref, kv_ref, sq_ref, wq, wkv, sem_q, sem_kv = rest
+        before, rest = rest[: len(sums)], rest[len(sums) :]
+        if mode == "first":
+            q_ref, kv_ref, sq_ref = rest[:3]
+        elif mode == "kv":
+            (kv_ref, factor_ref), sq_ref = rest[:2], rest[2]
+        else:
+            q_ref = rest[0]
+        wq, wkv, sem_q, sem_kv = rest[-4:]
 
         def at(i):
             _, s, rc = pieces[i // n_z]
             return ((place_ref[0] ^ rc) * n_z + i % n_z) * 4 + (place_ref[1] ^ s)
 
         def copies(i):
-            g = at(i) * width
-            return (
-                pltpu.make_async_copy(wq_hbm.at[pl.ds(g, width)], wq.at[i], sem_q.at[i]),
-                pltpu.make_async_copy(wkv_hbm.at[:, pl.ds(g, width)], wkv.at[i], sem_kv.at[i]),
-            )
+            g, out = at(i) * width, []
+            if do_q:
+                rows_q = wq_hbm.at[pl.ds(g, width)]
+                out.append(pltpu.make_async_copy(rows_q, wq.at[i], sem_q.at[i]))
+            if do_kv:
+                cols_kv = wkv_hbm.at[:, pl.ds(g, width)]
+                out.append(pltpu.make_async_copy(cols_kv, wkv.at[i], sem_kv.at[i]))
+            return out
 
         for i in range(steps):
             for copy in copies(i):
                 copy.start()
-        if last:
-            for ref, old in zip((q_ref, kv_ref, sq_ref), before):
-                ref[...] = old[...]
-        else:
+        if mode == "first":
             for ref in (q_ref, kv_ref, sq_ref):
                 ref[...] = jnp.zeros(ref.shape, F32)
+        elif mode == "kv":
+            kv_ref[...], sq_ref[...] = before[0][...], before[1][...]
+        else:
+            q_ref[...] = before[0][...]
         for p, ref in enumerate(refs):
-            q, kv = q_ref[...], kv_ref[...]
+            q = q_ref[...] if do_q else None
+            kv = kv_ref[...] if do_kv else None
             for r in range(n_z):
                 i = p * n_z + r
                 piece = ref[r].astype(F32)
                 lhs = (piece * gain_ref[at(i)]).astype(BF16)
-                sq_ref[...] += piece * piece
                 for copy in copies(i):
                     copy.wait()
-                q, kv = q + dot(lhs, wq[i]), kv + dot_t(wkv[i], lhs)
-            q_ref[...], kv_ref[...] = q, kv
-        if last:
+                if do_q:
+                    q = q + dot(lhs, wq[i])
+                if do_kv:
+                    sq_ref[...] += piece * piece
+                    kv = kv + dot_t(wkv[i], lhs)
+            if do_q:
+                q_ref[...] = q
+            if do_kv:
+                kv_ref[...] = kv
+        if mode == "kv":
             mean = jnp.sum(sq_ref[...], axis=1, keepdims=True) / (32 * width)
-            factor = lax.rsqrt(mean + EPS)
-            q_ref[...] = q_ref[...] * factor
-            across = jnp.broadcast_to(factor, (rows, rows)).T[:1]
-            kv_ref[...] = kv_ref[...] * across
-
-    shapes = [(rows, n_q), (n_kv, rows), (rows, width)]
+            factor = jnp.broadcast_to(lax.rsqrt(mean + EPS), (rows, rows))
+            factor_ref[...] = factor
+            kv_ref[...] = kv_ref[...] * factor.T[:1]
+        elif mode == "q":
+            q_ref[...] = q_ref[...] * before[1][:, :1]
+
+    shapes = {
+        "first": [(rows, n_q), (n_kv, rows), (rows, width)],
+        "kv": [(n_kv, rows), (rows, rows)],
+        "q": [(rows, n_q)],
+    }[mode]
     return pl.pallas_call(
         body,
         out_shape=[pltpu.VMEM(shape, F32) for shape in shapes],
-        in_specs=[SMEM, VMEM, HBM, HBM] + [VMEM] * (len(arrays) + (3 if last else 0)),
-        out_specs=[VMEM] * 3,
-        scratch_shapes=[
-            pltpu.VMEM((steps, width, n_q), BF16),
-            pltpu.VMEM((steps, n_kv, width), BF16),
+        in_specs=[SMEM, VMEM, HBM, HBM] + [VMEM] * (len(arrays) + len(sums)),
+        out_specs=[VMEM] * len(shapes),
+        scratch_shapes=([pltpu.VMEM((rows, width), F32)] if mode == "kv" else [])
+        + [
+            pltpu.VMEM((steps if do_q else 1, width, n_q), BF16),
+            pltpu.VMEM((steps if do_kv else 1, n_kv, width), BF16),
             pltpu.SemaphoreType.DMA((steps,)),
             pltpu.SemaphoreType.DMA((steps,)),
         ],
-        name="project_last" if last else "project_first",
-    )(place, *in_vmem(gains), w_query, w_keyval, *in_vmem(*arrays, *(sums or ())))
-
-
-def summed(terms, sent):
+    )(place, *in_vmem(gains), w_query, w_keyval, *in_vmem(*arrays, *sums))
+
+
+def over_square(terms, sent):
     quarter = terms.shape[1] // 4
 
     def both(s):
@@ -294,9 +315,7 @@
         return terms[:, rows] + sent[:, rows].astype(F32)
 
     got = [from_sq(both(s).astype(BF16), s) for s in (1, 2, 3)]
-    mine = both(0) + sum(t.astype(F32) for t in got)
-    tiles = exchange(mine.astype(BF16), "zh")
-    return tiles.astype(F32).sum(axis=0)
+    return (both(0) + sum(t.astype(F32) for t in got)).astype(BF16)
 
 
 def gathered(piece):
@@ -317,11 +336,12 @@
     total = rows * n_dp
     quarter = rows // 4
 
-    gate_up_w = jnp.concatenate([w_gate, w_up], axis=1)
-    gate_up_next, gate_up_last = from_x(gate_up_w, 1), from_x(gate_up_w, 3)
-    gate_up_all = [gate_up_w, gate_up_next, from_x(gate_up_w, 2), gate_up_last]
+    gate_next, gate_last = from_x(w_gate, 1), from_x(w_gate, 3)
+    up_next, up_last = from_x(w_up, 1), from_x(w_up, 3)
+    gate_all = [w_gate, gate_next, from_x(gate_next, 1), gate_last]
+    up_all = [w_up, up_next, from_x(up_last, 3), up_last]
     down_next, down_last = from_x(w_down, 1), from_x(w_down, 3)
-    down_all = [w_down, down_next, from_x(w_down, 2), down_last]
+    down_all = [w_down, down_next, from_x(down_next, 1), down_last]
 
     ours, theirs = gathered(tokens_in)
     place = jnp.stack([core, spot, x, y_hi]).astype(jnp.int32)
@@ -330,8 +350,9 @@
     early = [p for p in pieces if p[1] == 0]
     late = [p for p in pieces if p[1] != 0]
     w_kv = w_keyval.T
-    sums = project(place, early, gains, w_query, w_kv, None)
-    query, kv_part, _ = project(place, late, gains, w_query, w_kv, sums)
+    q_sum, kv_sum, squares = project(place, early, gains, w_query, w_kv, "first")
+    kv_part, factor = project(place, late, gains, w_query, w_kv, "kv", (kv_sum, squares))
+    (query,) = project(place, late, gains, w_query, w_kv, "q", (q_sum, factor))
 
     kv_here = move(
         kv_part.astype(BF16),
@@ -373,21 +394,27 @@
     ]
     resid = jnp.stack(resid, axis=0)
     resid = jnp.concatenate([pick(resid, j ^ spot) for j in range(4)], axis=1)
-    mid_part = (resid.astype(F32) + summed(terms, sent)).astype(BF16)
+    tiles = over_square(terms, sent)
+    tiles = exchange(tiles, "zh")
+    mid_part = (resid.astype(F32) + tiles.astype(F32).sum(axis=0)).astype(BF16)
     mid_own = move(mid_part, lambda c, yh, **_: {"c": yh, "yh": c})
 
     ours, theirs = gathered(mid_own)
 
     gains_mlp = gain_mlp.astype(F32).reshape(n_dp, 1, block_d)
-    sent, keep, square = gate_up_terms(place, gains_mlp, ours + theirs, gate_up_all)
-    sent = lax.ppermute(sent, "yh", SWAP)
-    hidden = hidden_units(keep, square, sent, dim)
+    mids = ours + theirs
+    sent, gate, square = hidden_terms(place, gains_mlp, mids, gate_all, True)
+    sent_gate = lax.ppermute(sent, "yh", SWAP)
+    sent, up = hidden_terms(place, gains_mlp, mids, up_all, False)
+    sent_up = lax.ppermute(sent, "yh", SWAP)
+    hidden = hidden_units(gate, up, square, sent_gate, sent_up, dim)
 
     other = lax.ppermute(hidden, "yh", SWAP)
     sent = down_terms(place, hidden, other, down_all, True)
     sent = lax.ppermute(sent, "c", SWAP)
     terms = down_terms(place, hidden, other, down_all, False)
-    done = (mid_own.astype(F32) + summed(terms, sent)).astype(BF16)
+    tiles = exchange(over_square(terms, sent), "zh")
+    done = (mid_own.astype(F32) + tiles.astype(F32).sum(axis=0)).astype(BF16)
     return move(done, lambda x, zh, **_: {"x": (x + zh) % NX, "zh": x})
 
 

time: 279 us -> 241 us (0.86)
  the two profiles are of different devices: /device:TPU:4 before, /device:TPU:6 now
where the time goes in v4:
time: 241 us; the launch traced here: 240 us
  waiting for transfers between devices  91.8 us (38%)
  starting transfers between devices  54.1 us (22%)
  blocking collectives  46.9 us (19%)
  Pallas kernels  33 us (14%)
  other arithmetic  10.6 us (4%)
  local copies, waits for them, and re-layouts  2.68 us (1%)
    all_to_all x3, blocking collectives, exchange(): return lax.all_to_all(tiles, axis, 0, 0, tiled=True)  46.9 us
    ppermute x12, waiting for transfers between devices, from_sq(): return lax.ppermute(array, ('zl', 'yl'), [(i, i ^ s) for i in range(4)])  32.1 us
    ppermute x9, waiting for transfers between devices, from_x(): return lax.ppermute(array, 'x', [(i, (i - r) % NX) for i in range(NX)])  29.2 us
    all_to_all x2, starting transfers between devices, exchange(): return lax.all_to_all(tiles, axis, 0, 0, tiled=True)  17.1 us
    all_to_all x2, waiting for transfers between devices, exchange(): return lax.all_to_all(tiles, axis, 0, 0, tiled=True)  14.2 us
    ppermute x9, starting transfers between devices, from_x(): return lax.ppermute(array, 'x', [(i, (i - r) % NX) for i in range(NX)])  14.1 us
    ppermute x12, starting transfers between devices, from_sq(): return lax.ppermute(array, ('zl', 'yl'), [(i, i ^ s) for i in range(4)])  13.4 us
    pallas_call x3, Pallas kernels, project(): pl.pallas_call(body, out_shape=[pltpu.VMEM(shape, F32) for shape in shape...  9.83 us
  transfers between devices with their start and end apart: 39, of which 21 were waited for; matrix products, arithmetic and copies ran while one was open for 3% of the time, Pallas kernels for 9%

profile of v4, /device:TPU:6, one launch (start us, length us, event | category | flops | bytes accessed | tf_op | source)
XLA Modules:
  0.0 240.2 jit_solution(13816584325223569387)
XLA Ops:
  0.9 19.3 %all_to_all.25.refs_0_ = bf16[4,128,256]{2,1,0:T(8,128)(2,1)S(1)} all-to-all(bf16[4,128,256]{2,1,0:T(8,128)(2,1)S(1)} %broadcast_in_dim.9), channel_id=1, replica_groups=mesh['c'=2,'yh'=2,'x'=4,'zh'=4,'zl'=2,'yl'=2] {'zh'}, dimensions={0} | all-to-all | bytes 524288 | tf_op jit(solution)/shard_map/all_to_all | solution.py:39
  23.7 5.7 %collective-permute-done.refs_0_ = bf16[4,128,256]{2,1,0:T(8,128)(2,1)S(1)} collective-permute-done((bf16[4,128,256]{2,1,0:T(8,128)(2,1)S(1)}, bf16[4,128,256]{2,1,0:T(8,128)(2,1)S(1)}, u32[]{:S(2)}, u32[]{:S(2)}) %collective-permute-start) | collective-permute-done | bytes 262176 | tf_op jit(solution)/shard_map/ppermute | solution.py:43
  36.7 3.4 %shard_map.92 = (f32[64,128]{1,0:T(8,128)S(1)}, f32[128,128]{1,0:T(8,128)S(1)}) custom-call(s32[4]{0:T(128)} %pad_add_fusion.place_ref, f32[32,1,256]{2,1,0:T(1,128)S(1)} %bitcast.39, bf16[8192,256]{1,0:T(8,128)(2,1)} %wq_hbm.5, bf16[64,8192]{1,0:T(8,128)(2,1)} %bitcast.42, bf16[4,128,256]{2,1,0:T(8,128)(2,1)S(1)} %collective-permute-done.refs_0_, ...), custom_call_target="tpu_custom_call" | custom-call | tf_op jit(solution)/shard_map/pallas_call | solution.py:295
  41.7 12.8 %all-to-all-start.1 = ((bf16[32,64,128]{2,1,0:T(8,128)(2,1)}), bf16[32,64,128]{2,1,0:T(8,128)(2,1)S(1)}, u32[]{:S(2)}, u32[]{:S(2)}) async-start(bf16[32,64,128]{2,1,0:T(8,128)(2,1)} %broadcast_in_dim.10), calls=%async_computation.1 | async-start | bytes 1048576 | tf_op jit(solution)/shard_map/all_to_all | solution.py:39
  54.7 3.9 %shard_map.93 = f32[128,256]{1,0:T(8,128)S(1)} custom-call(s32[4]{0:T(128)} %pad_add_fusion.place_ref, f32[32,1,256]{2,1,0:T(1,128)S(1)} %bitcast.40, bf16[8192,256]{1,0:T(8,128)(2,1)} %wq_hbm.5, bf16[64,8192]{1,0:T(8,128)(2,1)} %bitcast.43, bf16[4,128,256]{2,1,0:T(8,128)(2,1)S(1)} %collective-permute-done.refs_0_, ...), custom_call_target="tpu_custom_call" | custom-call | tf_op jit(solution)/shard_map/pallas_call | solution.py:295
  58.9 5.5 %all-to-all-done.1 = bf16[32,64,128]{2,1,0:T(8,128)(2,1)S(1)} async-done(((bf16[32,64,128]{2,1,0:T(8,128)(2,1)}), bf16[32,64,128]{2,1,0:T(8,128)(2,1)S(1)}, u32[]{:S(2)}, u32[]{:S(2)}) %all-to-all-start.1) | async-done | bytes 524320 | tf_op jit(solution)/shard_map/all_to_all | solution.py:39
  67.0 3.7 %out_give.1 = bf16[4,128,1024]{2,1,0:T(8,128)(2,1)} custom-call(s32[4]{0:T(128)} %pad_add_fusion.place_ref, bf16[256,128]{1,0:T(8,128)(2,1)S(1)} %convolution_convert_fusion.lhs_ref, bf16[256,8192]{1,0:T(8,128)(2,1)} %w_hbm.3), custom_call_target="tpu_custom_call" | custom-call | tf_op jit(solution)/shard_map/out_give/pallas_call | solution.py:94
  95.0 4.3 %all-to-all-start.2 = ((bf16[4,32,1024]{2,1,0:T(8,128)(2,1)}), bf16[4,32,1024]{2,1,0:T(8,128)(2,1)S(1)}, u32[]{:S(2)}, u32[]{:S(2)}) async-start(bf16[4,32,1024]{2,1,0:T(8,128)(2,1)} %fusion.11), calls=%async_computation.2 | async-start | bytes 524288 | tf_op jit(solution)/shard_map/all_to_all | solution.py:39
  101.0 8.7 %all-to-all-done.2 = bf16[4,32,1024]{2,1,0:T(8,128)(2,1)S(1)} async-done(((bf16[4,32,1024]{2,1,0:T(8,128)(2,1)}), bf16[4,32,1024]{2,1,0:T(8,128)(2,1)S(1)}, u32[]{:S(2)}, u32[]{:S(2)}) %all-to-all-start.2) | async-done | bytes 262176 | tf_op jit(solution)/shard_map/all_to_all | solution.py:39
  110.4 13.0 %all_to_all.26.refs_0_ = bf16[4,32,1024]{2,1,0:T(8,128)(2,1)S(1)} all-to-all(bf16[4,32,1024]{2,1,0:T(8,128)(2,1)S(1)} %broadcast_in_dim.12), channel_id=1, replica_groups=mesh['c'=2,'yh'=2,'x'=4,'zh'=4,'zl'=2,'yl'=2] {'zh'}, dimensions={0} | all-to-all | bytes 524288 | tf_op jit(solution)/shard_map/all_to_all | solution.py:39
  124.9 3.6 %collective-permute-done.24.refs_11_ = bf16[1024,512]{1,0:T(8,128)(2,1)} collective-permute-done((bf16[1024,512]{1,0:T(8,128)(2,1)}, bf16[1024,512]{1,0:T(8,128)(2,1)}, u32[]{:S(2)}, u32[]{:S(2)}) %collective-permute-start.24) | collective-permute-done | bytes 1048608 | tf_op jit(solution)/shard_map/ppermute | solution.py:219
  132.9 12.1 %collective-permute-done.21.refs_10_ = bf16[1024,512]{1,0:T(8,128)(2,1)} collective-permute-done((bf16[1024,512]{1,0:T(8,128)(2,1)}, bf16[1024,512]{1,0:T(8,128)(2,1)}, u32[]{:S(2)}, u32[]{:S(2)}) %collective-permute-start.21) | collective-permute-done | bytes 1048608 | tf_op jit(solution)/shard_map/ppermute | solution.py:219
  146.2 6.3 %collective-permute-done.15.refs_3_ = bf16[4,32,1024]{2,1,0:T(8,128)(2,1)S(1)} collective-permute-done((bf16[4,32,1024]{2,1,0:T(8,128)(2,1)S(1)}, bf16[4,32,1024]{2,1,0:T(8,128)(2,1)S(1)}, u32[]{:S(2)}, u32[]{:S(2)}) %collective-permute-start.15) | collective-permute-done | bytes 262176 | tf_op jit(solution)/shard_map/ppermute | solution.py:43
  157.6 4.6 %gate.1 = (bf16[128,640]{1,0:T(8,128)(2,1)S(1)}, f32[128,512]{1,0:T(8,128)}, f32[128,128]{1,0:T(8,128)}) custom-call(s32[4]{0:T(128)} %pad_add_fusion.place_ref, f32[8,1,1024]{2,1,0:T(1,128)} %bitcast.45, bf16[4,32,1024]{2,1,0:T(8,128)(2,1)S(1)} %all_to_all.26.refs_0_, bf16[4,32,1024]{2,1,0:T(8,128)(2,1)S(1)} %collective-permute-done.13.refs_1_, ...), custom_call_target="tpu_custom_call" | custom-call | tf_op jit(solution)/shard_map/gate/pallas_call | solution.py:143
  163.1 4.4 %collective-permute-done.23.refs_9_ = bf16[1024,512]{1,0:T(8,128)(2,1)} collective-permute-done((bf16[1024,512]{1,0:T(8,128)(2,1)}, bf16[1024,512]{1,0:T(8,128)(2,1)}, u32[]{:S(2)}, u32[]{:S(2)}) %collective-permute-start.23) | collective-permute-done | bytes 1048608 | tf_op jit(solution)/shard_map/ppermute | solution.py:219
  167.5 4.5 %up.1 = (bf16[128,512]{1,0:T(8,128)(2,1)S(1)}, f32[128,512]{1,0:T(8,128)}) custom-call(s32[4]{0:T(128)} %pad_add_fusion.place_ref, f32[8,1,1024]{2,1,0:T(1,128)} %bitcast.46, bf16[4,32,1024]{2,1,0:T(8,128)(2,1)S(1)} %all_to_all.26.refs_0_, bf16[4,32,1024]{2,1,0:T(8,128)(2,1)S(1)} %collective-permute-done.13.refs_1_, ...), custom_call_target="tpu_custom_call" | custom-call | tf_op jit(solution)/shard_map/up/pallas_call | solution.py:143
  173.0 5.7 %collective-permute-done.27.sent_up_ref = bf16[128,512]{1,0:T(8,128)(2,1)S(1)} collective-permute-done((bf16[128,512]{1,0:T(8,128)(2,1)S(1)}, bf16[128,512]{1,0:T(8,128)(2,1)S(1)}, u32[]{:S(2)}, u32[]{:S(2)}) %collective-permute-start.27) | collective-permute-done | bytes 131104 | tf_op jit(solution)/shard_map/ppermute | solution.py:409
  180.8 8.3 %collective-permute-done.30.refs_2_ = bf16[512,1024]{1,0:T(8,128)(2,1)} collective-permute-done((bf16[512,1024]{1,0:T(8,128)(2,1)}, bf16[512,1024]{1,0:T(8,128)(2,1)}, u32[]{:S(2)}, u32[]{:S(2)}) %collective-permute-start.30) | collective-permute-done | bytes 1048608 | tf_op jit(solution)/shard_map/ppermute | solution.py:219
  189.1 3.2 %down_give.1 = bf16[4,128,1024]{2,1,0:T(8,128)(2,1)S(1)} custom-call(s32[4]{0:T(128)} %pad_add_fusion.place_ref, bf16[128,512]{1,0:T(8,128)(2,1)S(1)} %hidden.1.hidden_ref, bf16[128,512]{1,0:T(8,128)(2,1)S(1)} %collective-permute-done.28.other_ref, bf16[512,1024]{1,0:T(8,128)(2,1)} %refs_0_.3, bf16[512,1024]{1,0:T(8,128)(2,1)} %collective-permute-done.29.refs_1_, ...), custom_call_target="tpu_custom_call" | custom-call | tf_op jit(solution)/shard_map/down_give/pallas_call | solution.py:197
  192.4 3.2 %down_keep.1 = f32[4,128,1024]{2,1,0:T(8,128)S(1)} custom-call(s32[4]{0:T(128)} %pad_add_fusion.place_ref, bf16[128,512]{1,0:T(8,128)(2,1)S(1)} %hidden.1.hidden_ref, bf16[128,512]{1,0:T(8,128)(2,1)S(1)} %collective-permute-done.28.other_ref, bf16[512,1024]{1,0:T(8,128)(2,1)} %refs_0_.3, bf16[512,1024]{1,0:T(8,128)(2,1)} %collective-permute-done.29.refs_1_, ...), custom_call_target="tpu_custom_call" | custom-call | tf_op jit(solution)/shard_map/down_keep/pallas_call | solution.py:197
  200.6 5.2 %collective-permute-done.33 = bf16[4,32,1024]{2,1,0:T(8,128)(2,1)S(1)} collective-permute-done((bf16[4,32,1024]{2,1,0:T(8,128)(2,1)S(1)}, bf16[4,32,1024]{2,1,0:T(8,128)(2,1)S(1)}, u32[]{:S(2)}, u32[]{:S(2)}) %collective-permute-start.33) | collective-permute-done | bytes 262176 | tf_op jit(solution)/shard_map/ppermute | solution.py:43
  206.4 6.2 %collective-permute-done.35 = bf16[4,32,1024]{2,1,0:T(8,128)(2,1)S(1)} collective-permute-done((bf16[4,32,1024]{2,1,0:T(8,128)(2,1)S(1)}, bf16[4,32,1024]{2,1,0:T(8,128)(2,1)S(1)}, u32[]{:S(2)}, u32[]{:S(2)}) %collective-permute-start.35) | collective-permute-done | bytes 262176 | tf_op jit(solution)/shard_map/ppermute | solution.py:43
  213.7 14.6 %all_to_all.27 = bf16[4,32,1024]{2,1,0:T(8,128)(2,1)S(1)} all-to-all(bf16[4,32,1024]{2,1,0:T(8,128)(2,1)S(1)} %fusion.6), channel_id=1, replica_groups=mesh['c'=2,'yh'=2,'x'=4,'zh'=4,'zl'=2,'yl'=2] {'zh'}, dimensions={0} | all-to-all | bytes 524288 | tf_op jit(solution)/shard_map/all_to_all | solution.py:39
  231.2 8.3 %collective-permute-done.36 = bf16[32,1024]{1,0:T(8,128)(2,1)S(1)} collective-permute-done((bf16[32,1024]{1,0:T(8,128)(2,1)S(1)}, bf16[32,1024]{1,0:T(8,128)(2,1)S(1)}, u32[]{:S(2)}, u32[]{:S(2)}) %collective-permute-start.36) | collective-permute-done | bytes 65568 | tf_op jit(solution)/shard_map/ppermute | solution.py:57
  (108 shorter events, 69.3 us)
Async XLA Ops:
  20.2 9.2 %collective-permute-start = (bf16[4,128,256]{2,1,0:T(8,128)(2,1)S(1)}, bf16[4,128,256]{2,1,0:T(8,128)(2,1)S(1)}, u32[]{:S(2)}, u32[]{:S(2)}) collective-permute-start(bf16[4,128,256]{2,1,0:T(8,128)(2,1)S(1)} %all_to_all.25.refs_0_), channel_id=1, source_target_pairs={{0,1},{1,0},{2,3},{3,2},{4,5},{5,4},{6,7},{7,6},{8,9},{9,8},{10,11... | collective-permute-start | bytes 786440 | tf_op jit(solution)/shard_map/ppermute | solution.py:43
  22.7 10.1 %collective-permute-start.2 = (bf16[4,128,256]{2,1,0:T(8,128)(2,1)S(1)}, bf16[4,128,256]{2,1,0:T(8,128)(2,1)S(1)}, u32[]{:S(2)}, u32[]{:S(2)}) collective-permute-start(bf16[4,128,256]{2,1,0:T(8,128)(2,1)S(1)} %all_to_all.25.refs_0_), channel_id=1, source_target_pairs={{0,3},{1,2},{2,1},{3,0},{4,7},{5,6},{6,5},{7,4},{8,11},{9,10},{10,... | collective-permute-start | bytes 786440 | tf_op jit(solution)/shard_map/ppermute | solution.py:43
  23.7 10.5 %collective-permute-start.6 = (bf16[4,128,256]{2,1,0:T(8,128)(2,1)S(1)}, bf16[4,128,256]{2,1,0:T(8,128)(2,1)S(1)}, u32[]{:S(2)}, u32[]{:S(2)}) collective-permute-start(bf16[4,128,256]{2,1,0:T(8,128)(2,1)S(1)} %all_to_all.25.refs_0_), channel_id=1, source_target_pairs={{0,128},{128,0},{1,129},{129,1},{2,130},{130,2},{3,131},{131,3},{4... | collective-permute-start | bytes 786440 | tf_op jit(solution)/shard_map/ppermute | solution.py:324
  41.7 22.7 %all-to-all-start.1 = ((bf16[32,64,128]{2,1,0:T(8,128)(2,1)}), bf16[32,64,128]{2,1,0:T(8,128)(2,1)S(1)}, u32[]{:S(2)}, u32[]{:S(2)}) async-start(bf16[32,64,128]{2,1,0:T(8,128)(2,1)} %broadcast_in_dim.10), calls=%async_computation.1 | async-start | bytes 1048576 | tf_op jit(solution)/shard_map/all_to_all | solution.py:39
  72.5 27.6 %collective-permute-start.20 = (bf16[1024,512]{1,0:T(8,128)(2,1)}, bf16[1024,512]{1,0:T(8,128)(2,1)}, u32[]{:S(2)}, u32[]{:S(2)}) collective-permute-start(bf16[1024,512]{1,0:T(8,128)(2,1)} %refs_8_.2), channel_id=1, source_target_pairs={{0,48},{16,0},{32,16},{48,32},{1,49},{17,1},{33,17},{49,33},{2,50}... | collective-permute-start | bytes 3145736 | tf_op jit(solution)/shard_map/ppermute | solution.py:219
  77.6 9.4 %collective-permute-start.10 = (bf16[4,32,1024]{2,1,0:T(8,128)(2,1)}, bf16[4,32,1024]{2,1,0:T(8,128)(2,1)S(1)}, u32[]{:S(2)}, u32[]{:S(2)}) collective-permute-start(bf16[4,32,1024]{2,1,0:T(8,128)(2,1)} %get-tuple-element.30), channel_id=1, source_target_pairs={{0,2},{1,3},{2,0},{3,1},{4,6},{5,7},{6,4},{7,5},{8,10},{9,11},{10,... | collective-permute-start | bytes 786440 | tf_op jit(solution)/shard_map/ppermute | solution.py:43
  78.3 13.2 %collective-permute-start.11 = (bf16[4,32,1024]{2,1,0:T(8,128)(2,1)}, bf16[4,32,1024]{2,1,0:T(8,128)(2,1)}, u32[]{:S(2)}, u32[]{:S(2)}) collective-permute-start(bf16[4,32,1024]{2,1,0:T(8,128)(2,1)} %get-tuple-element.29), channel_id=1, source_target_pairs={{0,3},{1,2},{2,1},{3,0},{4,7},{5,6},{6,5},{7,4},{8,11},{9,10},{10,... | collective-permute-start | bytes 786440 | tf_op jit(solution)/shard_map/ppermute | solution.py:43
  79.5 13.5 %collective-permute-start.9 = (bf16[4,32,1024]{2,1,0:T(8,128)(2,1)}, bf16[4,32,1024]{2,1,0:T(8,128)(2,1)}, u32[]{:S(2)}, u32[]{:S(2)}) collective-permute-start(bf16[4,32,1024]{2,1,0:T(8,128)(2,1)} %get-tuple-element.28), channel_id=1, source_target_pairs={{0,1},{1,0},{2,3},{3,2},{4,5},{5,4},{6,7},{7,6},{8,9},{9,8},{10,11... | collective-permute-start | bytes 786440 | tf_op jit(solution)/shard_map/ppermute | solution.py:43
  81.1 48.1 %collective-permute-start.22 = (bf16[1024,512]{1,0:T(8,128)(2,1)}, bf16[1024,512]{1,0:T(8,128)(2,1)}, u32[]{:S(2)}, u32[]{:S(2)}) collective-permute-start(bf16[1024,512]{1,0:T(8,128)(2,1)} %refs_8_.2), channel_id=1, source_target_pairs={{0,16},{16,32},{32,48},{48,0},{1,17},{17,33},{33,49},{49,1},{2,18}... | collective-permute-start | bytes 3145736 | tf_op jit(solution)/shard_map/ppermute | solution.py:219
  87.0 41.5 %collective-permute-start.24 = (bf16[1024,512]{1,0:T(8,128)(2,1)}, bf16[1024,512]{1,0:T(8,128)(2,1)}, u32[]{:S(2)}, u32[]{:S(2)}) collective-permute-start(bf16[1024,512]{1,0:T(8,128)(2,1)} %refs_8_.3), channel_id=1, source_target_pairs={{0,16},{16,32},{32,48},{48,0},{1,17},{17,33},{33,49},{49,1},{2,18}... | collective-permute-start | bytes 3145736 | tf_op jit(solution)/shard_map/ppermute | solution.py:219
  91.5 39.1 %collective-permute-start.29 = (bf16[512,1024]{1,0:T(8,128)(2,1)}, bf16[512,1024]{1,0:T(8,128)(2,1)}, u32[]{:S(2)}, u32[]{:S(2)}) collective-permute-start(bf16[512,1024]{1,0:T(8,128)(2,1)} %refs_0_.3), channel_id=1, source_target_pairs={{0,48},{16,0},{32,16},{48,32},{1,49},{17,1},{33,17},{49,33},{2,50}... | collective-permute-start | bytes 3145736 | tf_op jit(solution)/shard_map/ppermute | solution.py:219
  95.0 14.6 %all-to-all-start.2 = ((bf16[4,32,1024]{2,1,0:T(8,128)(2,1)}), bf16[4,32,1024]{2,1,0:T(8,128)(2,1)S(1)}, u32[]{:S(2)}, u32[]{:S(2)}) async-start(bf16[4,32,1024]{2,1,0:T(8,128)(2,1)} %fusion.11), calls=%async_computation.2 | async-start | bytes 524288 | tf_op jit(solution)/shard_map/all_to_all | solution.py:39
  100.1 44.9 %collective-permute-start.21 = (bf16[1024,512]{1,0:T(8,128)(2,1)}, bf16[1024,512]{1,0:T(8,128)(2,1)}, u32[]{:S(2)}, u32[]{:S(2)}) collective-permute-start(bf16[1024,512]{1,0:T(8,128)(2,1)} %collective-permute-done.20.refs_9_), channel_id=1, source_target_pairs={{0,48},{16,0},{32,16},{48,32},{1,49},{17,1},{33,17},{49,33},{2,50}... | collective-permute-start | bytes 3145736 | tf_op jit(solution)/shard_map/ppermute | solution.py:219
  123.4 22.4 %collective-permute-start.13 = (bf16[4,32,1024]{2,1,0:T(8,128)(2,1)S(1)}, bf16[4,32,1024]{2,1,0:T(8,128)(2,1)S(1)}, u32[]{:S(2)}, u32[]{:S(2)}) collective-permute-start(bf16[4,32,1024]{2,1,0:T(8,128)(2,1)S(1)} %all_to_all.26.refs_0_), channel_id=1, source_target_pairs={{0,1},{1,0},{2,3},{3,2},{4,5},{5,4},{6,7},{7,6},{8,9},{9,8},{10,11... | collective-permute-start | bytes 786440 | tf_op jit(solution)/shard_map/ppermute | solution.py:43
  128.5 17.3 %collective-permute-start.14 = (bf16[4,32,1024]{2,1,0:T(8,128)(2,1)S(1)}, bf16[4,32,1024]{2,1,0:T(8,128)(2,1)S(1)}, u32[]{:S(2)}, u32[]{:S(2)}) collective-permute-start(bf16[4,32,1024]{2,1,0:T(8,128)(2,1)S(1)} %all_to_all.26.refs_0_), channel_id=1, source_target_pairs={{0,2},{1,3},{2,0},{3,1},{4,6},{5,7},{6,4},{7,5},{8,10},{9,11},{10,... | collective-permute-start | bytes 786440 | tf_op jit(solution)/shard_map/ppermute | solution.py:43
  129.1 38.4 %collective-permute-start.23 = (bf16[1024,512]{1,0:T(8,128)(2,1)}, bf16[1024,512]{1,0:T(8,128)(2,1)}, u32[]{:S(2)}, u32[]{:S(2)}) collective-permute-start(bf16[1024,512]{1,0:T(8,128)(2,1)} %refs_8_.3), channel_id=1, source_target_pairs={{0,48},{16,0},{32,16},{48,32},{1,49},{17,1},{33,17},{49,33},{2,50}... | collective-permute-start | bytes 3145736 | tf_op jit(solution)/shard_map/ppermute | solution.py:219
  130.6 36.9 %collective-permute-start.25 = (bf16[1024,512]{1,0:T(8,128)(2,1)}, bf16[1024,512]{1,0:T(8,128)(2,1)}, u32[]{:S(2)}, u32[]{:S(2)}) collective-permute-start(bf16[1024,512]{1,0:T(8,128)(2,1)} %collective-permute-done.24.refs_11_), channel_id=1, source_target_pairs={{0,16},{16,32},{32,48},{48,0},{1,17},{17,33},{33,49},{49,1},{2,18}... | collective-permute-start | bytes 3145736 | tf_op jit(solution)/shard_map/ppermute | solution.py:219
  152.5 28.3 %collective-permute-start.31 = (bf16[512,1024]{1,0:T(8,128)(2,1)}, bf16[512,1024]{1,0:T(8,128)(2,1)}, u32[]{:S(2)}, u32[]{:S(2)}) collective-permute-start(bf16[512,1024]{1,0:T(8,128)(2,1)} %refs_0_.3), channel_id=1, source_target_pairs={{0,16},{16,32},{32,48},{48,0},{1,17},{17,33},{33,49},{49,1},{2,18}... | collective-permute-start | bytes 3145736 | tf_op jit(solution)/shard_map/ppermute | solution.py:219
  152.8 36.3 %collective-permute-start.30 = (bf16[512,1024]{1,0:T(8,128)(2,1)}, bf16[512,1024]{1,0:T(8,128)(2,1)}, u32[]{:S(2)}, u32[]{:S(2)}) collective-permute-start(bf16[512,1024]{1,0:T(8,128)(2,1)} %collective-permute-done.29.refs_1_), channel_id=1, source_target_pairs={{0,48},{16,0},{32,16},{48,32},{1,49},{17,1},{33,17},{49,33},{2,50}... | collective-permute-start | bytes 3145736 | tf_op jit(solution)/shard_map/ppermute | solution.py:219
  162.2 16.4 %collective-permute-start.26 = (bf16[128,640]{1,0:T(8,128)(2,1)S(1)}, bf16[128,640]{1,0:T(8,128)(2,1)S(1)}, u32[]{:S(2)}, u32[]{:S(2)}) collective-permute-start(bf16[128,640]{1,0:T(8,128)(2,1)S(1)} %get-tuple-element.23), channel_id=1, source_target_pairs={{0,64},{64,0},{1,65},{65,1},{2,66},{66,2},{3,67},{67,3},{4,68},{68... | collective-permute-start | bytes 491528 | tf_op jit(solution)/shard_map/ppermute | solution.py:407
  179.9 9.2 %collective-permute-start.28 = (bf16[128,512]{1,0:T(8,128)(2,1)S(1)}, bf16[128,512]{1,0:T(8,128)(2,1)S(1)}, u32[]{:S(2)}, u32[]{:S(2)}) collective-permute-start(bf16[128,512]{1,0:T(8,128)(2,1)S(1)} %hidden.1.hidden_ref), channel_id=1, source_target_pairs={{0,64},{64,0},{1,65},{65,1},{2,66},{66,2},{3,67},{67,3},{4,68},{68... | collective-permute-start | bytes 393224 | tf_op jit(solution)/shard_map/ppermute | solution.py:412
  197.1 9.3 %collective-permute-start.34 = (bf16[4,32,1024]{2,1,0:T(8,128)(2,1)S(1)}, bf16[4,32,1024]{2,1,0:T(8,128)(2,1)S(1)}, u32[]{:S(2)}, u32[]{:S(2)}) collective-permute-start(bf16[4,32,1024]{2,1,0:T(8,128)(2,1)S(1)} %get-tuple-element.27), channel_id=1, source_target_pairs={{0,2},{1,3},{2,0},{3,1},{4,6},{5,7},{6,4},{7,5},{8,10},{9,11},{10,... | collective-permute-start | bytes 786440 | tf_op jit(solution)/shard_map/ppermute | solution.py:43
  198.3 14.3 %collective-permute-start.35 = (bf16[4,32,1024]{2,1,0:T(8,128)(2,1)S(1)}, bf16[4,32,1024]{2,1,0:T(8,128)(2,1)S(1)}, u32[]{:S(2)}, u32[]{:S(2)}) collective-permute-start(bf16[4,32,1024]{2,1,0:T(8,128)(2,1)S(1)} %get-tuple-element.26), channel_id=1, source_target_pairs={{0,3},{1,2},{2,1},{3,0},{4,7},{5,6},{6,5},{7,4},{8,11},{9,10},{10,... | collective-permute-start | bytes 786440 | tf_op jit(solution)/shard_map/ppermute | solution.py:43
  228.4 11.2 %collective-permute-start.36 = (bf16[32,1024]{1,0:T(8,128)(2,1)S(1)}, bf16[32,1024]{1,0:T(8,128)(2,1)S(1)}, u32[]{:S(2)}, u32[]{:S(2)}) collective-permute-start(bf16[32,1024]{1,0:T(8,128)(2,1)S(1)} %add_convert_fusion), channel_id=1, source_target_pairs={{0,0},{1,1},{2,2},{3,3},{4,16},{5,17},{6,18},{7,19},{8,32},{9,33},... | collective-permute-start | bytes 196616 | tf_op jit(solution)/shard_map/ppermute | solution.py:57
  (18 other events, 227.9 us)

commit v5 on v3

--- a/solution.py
+++ b/solution.py
@@ -387,8 +387,6 @@
 
     ours, theirs = gathered(mid_own)
 
-    resid = move(mid_own, lambda x, zh, **_: {"x": (x + zh) % NX, "zh": x})
-
     gains_mlp = gain_mlp.astype(F32).reshape(n_dp, 1, block_d)
     sent, keep, square = gate_up_terms(place, gains_mlp, ours + theirs, gate_all, up_all)
     sent = lax.ppermute(sent, "yh", SWAP)
@@ -398,16 +396,9 @@
     sent = down_terms(place, hidden, other, down_all, True)
     sent = lax.ppermute(sent, "c", SWAP)
     terms = down_terms(place, hidden, other, down_all, False)
-    tiles = over_square(terms, sent)
-    got = [
-        move(
-            pick(tiles, (z_hi + r) % NX),
-            lambda x, zh, r=r, **_: {"x": (x + zh + r) % NX, "zh": x},
-        )
-        for r in range(NX)
-    ]
-    done = resid.astype(F32) + sum(t.astype(F32) for t in got)
-    return done.astype(BF16)
+    tiles = exchange(over_square(terms, sent), "zh")
+    done = (mid_own.astype(F32) + tiles.astype(F32).sum(axis=0)).astype(BF16)
+    return move(done, lambda x, zh, **_: {"x": (x + zh) % NX, "zh": x})
 
 
 def solution(mesh):

time: 270 us -> 266 us (0.985)
  the two profiles are of different devices: /device:TPU:2 before, /device:TPU:6 now
where the time goes in v5:
time: 266 us; the launch traced here: 264 us
  waiting for transfers between devices  132 us (50%)
  starting transfers between devices  55 us (21%)
  blocking collectives  34.3 us (13%)
  Pallas kernels  26.1 us (10%)
  other arithmetic  10.5 us (4%)
  local copies, waits for them, and re-layouts  5.56 us (2%)
    ppermute x9, waiting for transfers between devices, from_x(): return lax.ppermute(array, 'x', [(i, (i - r) % NX) for i in range(NX)])  44.9 us
    ppermute x12, waiting for transfers between devices, from_sq(): return lax.ppermute(array, ('zl', 'yl'), [(i, i ^ s) for i in range(4)])  35.6 us
    all_to_all x2, blocking collectives, exchange(): return lax.all_to_all(tiles, axis, 0, 0, tiled=True)  34.3 us
    all_to_all x3, waiting for transfers between devices, exchange(): return lax.all_to_all(tiles, axis, 0, 0, tiled=True)  27.8 us
    all_to_all x3, starting transfers between devices, exchange(): return lax.all_to_all(tiles, axis, 0, 0, tiled=True)  21.8 us
    ppermute x12, starting transfers between devices, from_sq(): return lax.ppermute(array, ('zl', 'yl'), [(i, i ^ s) for i in range(4)])  12.6 us
    ppermute x9, starting transfers between devices, from_x(): return lax.ppermute(array, 'x', [(i, (i - r) % NX) for i in range(NX)])  11.1 us
    ppermute x1, waiting for transfers between devices, layer(): sent = lax.ppermute(sent, 'yh', SWAP)  9.18 us
  transfers between devices with their start and end apart: 39, of which 22 were waited for; matrix products, arithmetic and copies ran while one was open for 3% of the time, Pallas kernels for 6%

profile of v5, /device:TPU:6, one launch (start us, length us, event | category | flops | bytes accessed | tf_op | source)
XLA Modules:
  0.0 264.4 jit_solution(16160636484014416292)
XLA Ops:
  0.9 19.3 %all_to_all.25.refs_0_ = bf16[4,128,256]{2,1,0:T(8,128)(2,1)S(1)} all-to-all(bf16[4,128,256]{2,1,0:T(8,128)(2,1)S(1)} %broadcast_in_dim.9), channel_id=1, replica_groups=mesh['c'=2,'yh'=2,'x'=4,'zh'=4,'zl'=2,'yl'=2] {'zh'}, dimensions={0} | all-to-all | bytes 524288 | tf_op jit(solution)/shard_map/all_to_all | solution.py:39
  23.7 5.7 %collective-permute-done.refs_0_ = bf16[4,128,256]{2,1,0:T(8,128)(2,1)S(1)} collective-permute-done((bf16[4,128,256]{2,1,0:T(8,128)(2,1)S(1)}, bf16[4,128,256]{2,1,0:T(8,128)(2,1)S(1)}, u32[]{:S(2)}, u32[]{:S(2)}) %collective-permute-start) | collective-permute-done | bytes 262176 | tf_op jit(solution)/shard_map/ppermute | solution.py:43
  36.8 4.7 %project_last.1 = (f32[128,256]{1,0:T(8,128)S(1)}, f32[64,128]{1,0:T(8,128)S(1)}, f32[128,256]{1,0:T(8,128)}) custom-call(s32[4]{0:T(128)} %pad_add_fusion.place_ref, f32[32,1,256]{2,1,0:T(1,128)S(1)} %bitcast.39, bf16[8192,256]{1,0:T(8,128)(2,1)} %wq_hbm.3, bf16[64,8192]{1,0:T(8,128)(2,1)} %bitcast.41, ...), custom_call_target="tpu_custom_call" | custom-call | tf_op jit(solution)/shard_map/project_last/pallas_call | solution.py:282
  43.1 12.8 %all-to-all-start.1 = ((bf16[32,64,128]{2,1,0:T(8,128)(2,1)}), bf16[32,64,128]{2,1,0:T(8,128)(2,1)S(1)}, u32[]{:S(2)}, u32[]{:S(2)}) async-start(bf16[32,64,128]{2,1,0:T(8,128)(2,1)} %broadcast_in_dim.10), calls=%async_computation.1 | async-start | bytes 1048576 | tf_op jit(solution)/shard_map/all_to_all | solution.py:39
  56.4 9.4 %all-to-all-done.1 = bf16[32,64,128]{2,1,0:T(8,128)(2,1)S(1)} async-done(((bf16[32,64,128]{2,1,0:T(8,128)(2,1)}), bf16[32,64,128]{2,1,0:T(8,128)(2,1)S(1)}, u32[]{:S(2)}, u32[]{:S(2)}) %all-to-all-start.1) | async-done | bytes 524320 | tf_op jit(solution)/shard_map/all_to_all | solution.py:39
  81.4 3.1 %collective-permute-start.22 = (bf16[1024,512]{1,0:T(8,128)(2,1)}, bf16[1024,512]{1,0:T(8,128)(2,1)}, u32[]{:S(2)}, u32[]{:S(2)}) collective-permute-start(bf16[1024,512]{1,0:T(8,128)(2,1)} %refs_8_.1), channel_id=1, source_target_pairs={{0,16},{16,32},{32,48},{48,0},{1,17},{17,33},{33,49},{49,1},{2,18}... | collective-permute-start | bytes 3145736 | tf_op jit(solution)/shard_map/ppermute | solution.py:228
  95.0 4.5 %all-to-all-start.2 = ((bf16[4,32,1024]{2,1,0:T(8,128)(2,1)}), bf16[4,32,1024]{2,1,0:T(8,128)(2,1)S(1)}, u32[]{:S(2)}, u32[]{:S(2)}) async-start(bf16[4,32,1024]{2,1,0:T(8,128)(2,1)} %fusion.11), calls=%async_computation.2 | async-start | bytes 524288 | tf_op jit(solution)/shard_map/all_to_all | solution.py:39
  101.0 9.1 %all-to-all-done.2 = bf16[4,32,1024]{2,1,0:T(8,128)(2,1)S(1)} async-done(((bf16[4,32,1024]{2,1,0:T(8,128)(2,1)}), bf16[4,32,1024]{2,1,0:T(8,128)(2,1)S(1)}, u32[]{:S(2)}, u32[]{:S(2)}) %all-to-all-start.2) | async-done | bytes 262176 | tf_op jit(solution)/shard_map/all_to_all | solution.py:39
  110.8 18.1 %collective-permute-done.24.refs_15_ = bf16[1024,512]{1,0:T(8,128)(2,1)} collective-permute-done((bf16[1024,512]{1,0:T(8,128)(2,1)}, bf16[1024,512]{1,0:T(8,128)(2,1)}, u32[]{:S(2)}, u32[]{:S(2)}) %collective-permute-start.24) | collective-permute-done | bytes 1048608 | tf_op jit(solution)/shard_map/ppermute | solution.py:228
  129.5 3.1 %collective-permute-start.25 = (bf16[1024,512]{1,0:T(8,128)(2,1)}, bf16[1024,512]{1,0:T(8,128)(2,1)}, u32[]{:S(2)}, u32[]{:S(2)}) collective-permute-start(bf16[1024,512]{1,0:T(8,128)(2,1)} %collective-permute-done.24.refs_15_), channel_id=1, source_target_pairs={{0,16},{16,32},{32,48},{48,0},{1,17},{17,33},{33,49},{49,1},{2,18}... | collective-permute-start | bytes 3145736 | tf_op jit(solution)/shard_map/ppermute | solution.py:228
  133.4 4.5 %all-to-all-start.3 = ((bf16[4,32,1024]{2,1,0:T(8,128)(2,1)}), bf16[4,32,1024]{2,1,0:T(8,128)(2,1)S(1)}, u32[]{:S(2)}, u32[]{:S(2)}) async-start(bf16[4,32,1024]{2,1,0:T(8,128)(2,1)} %broadcast_in_dim.12), calls=%async_computation.3 | async-start | bytes 524288 | tf_op jit(solution)/shard_map/all_to_all | solution.py:39
  137.8 9.3 %all-to-all-done.3.refs_0_ = bf16[4,32,1024]{2,1,0:T(8,128)(2,1)S(1)} async-done(((bf16[4,32,1024]{2,1,0:T(8,128)(2,1)}), bf16[4,32,1024]{2,1,0:T(8,128)(2,1)S(1)}, u32[]{:S(2)}, u32[]{:S(2)}) %all-to-all-start.3) | async-done | bytes 262176 | tf_op jit(solution)/shard_map/all_to_all | solution.py:39
  149.4 4.4 %collective-permute-done.28.refs_1_ = bf16[512,1024]{1,0:T(8,128)(2,1)} collective-permute-done((bf16[512,1024]{1,0:T(8,128)(2,1)}, bf16[512,1024]{1,0:T(8,128)(2,1)}, u32[]{:S(2)}, u32[]{:S(2)}) %collective-permute-start.28) | collective-permute-done | bytes 1048608 | tf_op jit(solution)/shard_map/ppermute | solution.py:228
  153.8 22.5 %collective-permute-done.21.refs_10_ = bf16[1024,512]{1,0:T(8,128)(2,1)} collective-permute-done((bf16[1024,512]{1,0:T(8,128)(2,1)}, bf16[1024,512]{1,0:T(8,128)(2,1)}, u32[]{:S(2)}, u32[]{:S(2)}) %collective-permute-start.21) | collective-permute-done | bytes 1048608 | tf_op jit(solution)/shard_map/ppermute | solution.py:228
  177.7 6.2 %collective-permute-done.14.refs_2_ = bf16[4,32,1024]{2,1,0:T(8,128)(2,1)S(1)} collective-permute-done((bf16[4,32,1024]{2,1,0:T(8,128)(2,1)S(1)}, bf16[4,32,1024]{2,1,0:T(8,128)(2,1)S(1)}, u32[]{:S(2)}, u32[]{:S(2)}) %collective-permute-start.14) | collective-permute-done | bytes 262176 | tf_op jit(solution)/shard_map/ppermute | solution.py:43
  188.6 5.8 %gate_up.1 = (bf16[128,1152]{1,0:T(8,128)(2,1)S(1)}, f32[128,1024]{1,0:T(8,128)}, f32[128,128]{1,0:T(8,128)}) custom-call(s32[4]{0:T(128)} %pad_add_fusion.place_ref, f32[8,1,1024]{2,1,0:T(1,128)} %bitcast.44, bf16[4,32,1024]{2,1,0:T(8,128)(2,1)S(1)} %all-to-all-done.3.refs_0_, bf16[4,32,1024]{2,1,0:T(8,128)(2,1)S(1)} %collective-permute-done.13.refs_1_, ...), custom_call_target="tpu_custom_call" | custom-call | tf_op jit(solution)/shard_map/gate_up/pallas_call | solution.py:150
  195.9 9.2 %collective-permute-done.26.sent_ref = bf16[128,1152]{1,0:T(8,128)(2,1)S(1)} collective-permute-done((bf16[128,1152]{1,0:T(8,128)(2,1)S(1)}, bf16[128,1152]{1,0:T(8,128)(2,1)S(1)}, u32[]{:S(2)}, u32[]{:S(2)}) %collective-permute-start.26) | collective-permute-done | bytes 294944 | tf_op jit(solution)/shard_map/ppermute | solution.py:392
  207.9 5.1 %collective-permute-done.27.other_ref = bf16[128,512]{1,0:T(8,128)(2,1)S(1)} collective-permute-done((bf16[128,512]{1,0:T(8,128)(2,1)S(1)}, bf16[128,512]{1,0:T(8,128)(2,1)S(1)}, u32[]{:S(2)}, u32[]{:S(2)}) %collective-permute-start.27) | collective-permute-done | bytes 131104 | tf_op jit(solution)/shard_map/ppermute | solution.py:395
  213.0 3.2 %down_give.1 = bf16[4,128,1024]{2,1,0:T(8,128)(2,1)S(1)} custom-call(s32[4]{0:T(128)} %pad_add_fusion.place_ref, bf16[128,512]{1,0:T(8,128)(2,1)S(1)} %hidden.1.hidden_ref, bf16[128,512]{1,0:T(8,128)(2,1)S(1)} %collective-permute-done.27.other_ref, bf16[512,1024]{1,0:T(8,128)(2,1)} %refs_0_.3, bf16[512,1024]{1,0:T(8,128)(2,1)} %collective-permute-done.28.refs_1_, ...), custom_call_target="tpu_custom_call" | custom-call | tf_op jit(solution)/shard_map/down_give/pallas_call | solution.py:206
  216.3 3.2 %down_keep.1 = f32[4,128,1024]{2,1,0:T(8,128)S(1)} custom-call(s32[4]{0:T(128)} %pad_add_fusion.place_ref, bf16[128,512]{1,0:T(8,128)(2,1)S(1)} %hidden.1.hidden_ref, bf16[128,512]{1,0:T(8,128)(2,1)S(1)} %collective-permute-done.27.other_ref, bf16[512,1024]{1,0:T(8,128)(2,1)} %refs_0_.3, bf16[512,1024]{1,0:T(8,128)(2,1)} %collective-permute-done.28.refs_1_, ...), custom_call_target="tpu_custom_call" | custom-call | tf_op jit(solution)/shard_map/down_keep/pallas_call | solution.py:206
  224.4 5.2 %collective-permute-done.32 = bf16[4,32,1024]{2,1,0:T(8,128)(2,1)S(1)} collective-permute-done((bf16[4,32,1024]{2,1,0:T(8,128)(2,1)S(1)}, bf16[4,32,1024]{2,1,0:T(8,128)(2,1)S(1)}, u32[]{:S(2)}, u32[]{:S(2)}) %collective-permute-start.32) | collective-permute-done | bytes 262176 | tf_op jit(solution)/shard_map/ppermute | solution.py:43
  231.6 4.9 %collective-permute-done.34 = bf16[4,32,1024]{2,1,0:T(8,128)(2,1)S(1)} collective-permute-done((bf16[4,32,1024]{2,1,0:T(8,128)(2,1)S(1)}, bf16[4,32,1024]{2,1,0:T(8,128)(2,1)S(1)}, u32[]{:S(2)}, u32[]{:S(2)}) %collective-permute-start.34) | collective-permute-done | bytes 262176 | tf_op jit(solution)/shard_map/ppermute | solution.py:43
  237.6 15.0 %all_to_all.26 = bf16[4,32,1024]{2,1,0:T(8,128)(2,1)S(1)} all-to-all(bf16[4,32,1024]{2,1,0:T(8,128)(2,1)S(1)} %fusion.6), channel_id=1, replica_groups=mesh['c'=2,'yh'=2,'x'=4,'zh'=4,'zl'=2,'yl'=2] {'zh'}, dimensions={0} | all-to-all | bytes 524288 | tf_op jit(solution)/shard_map/all_to_all | solution.py:39
  255.5 8.3 %collective-permute-done.35 = bf16[32,1024]{1,0:T(8,128)(2,1)S(1)} collective-permute-done((bf16[32,1024]{1,0:T(8,128)(2,1)S(1)}, bf16[32,1024]{1,0:T(8,128)(2,1)S(1)}, u32[]{:S(2)}, u32[]{:S(2)}) %collective-permute-start.35) | collective-permute-done | bytes 65568 | tf_op jit(solution)/shard_map/ppermute | solution.py:57
  (111 shorter events, 67.7 us)
Async XLA Ops:
  20.2 9.2 %collective-permute-start = (bf16[4,128,256]{2,1,0:T(8,128)(2,1)S(1)}, bf16[4,128,256]{2,1,0:T(8,128)(2,1)S(1)}, u32[]{:S(2)}, u32[]{:S(2)}) collective-permute-start(bf16[4,128,256]{2,1,0:T(8,128)(2,1)S(1)} %all_to_all.25.refs_0_), channel_id=1, source_target_pairs={{0,1},{1,0},{2,3},{3,2},{4,5},{5,4},{6,7},{7,6},{8,9},{9,8},{10,11... | collective-permute-start | bytes 786440 | tf_op jit(solution)/shard_map/ppermute | solution.py:43
  22.7 10.1 %collective-permute-start.2 = (bf16[4,128,256]{2,1,0:T(8,128)(2,1)S(1)}, bf16[4,128,256]{2,1,0:T(8,128)(2,1)S(1)}, u32[]{:S(2)}, u32[]{:S(2)}) collective-permute-start(bf16[4,128,256]{2,1,0:T(8,128)(2,1)S(1)} %all_to_all.25.refs_0_), channel_id=1, source_target_pairs={{0,3},{1,2},{2,1},{3,0},{4,7},{5,6},{6,5},{7,4},{8,11},{9,10},{10,... | collective-permute-start | bytes 786440 | tf_op jit(solution)/shard_map/ppermute | solution.py:43
  23.7 10.5 %collective-permute-start.6 = (bf16[4,128,256]{2,1,0:T(8,128)(2,1)S(1)}, bf16[4,128,256]{2,1,0:T(8,128)(2,1)S(1)}, u32[]{:S(2)}, u32[]{:S(2)}) collective-permute-start(bf16[4,128,256]{2,1,0:T(8,128)(2,1)S(1)} %all_to_all.25.refs_0_), channel_id=1, source_target_pairs={{0,128},{128,0},{1,129},{129,1},{2,130},{130,2},{3,131},{131,3},{4... | collective-permute-start | bytes 786440 | tf_op jit(solution)/shard_map/ppermute | solution.py:311
  43.1 22.7 %all-to-all-start.1 = ((bf16[32,64,128]{2,1,0:T(8,128)(2,1)}), bf16[32,64,128]{2,1,0:T(8,128)(2,1)S(1)}, u32[]{:S(2)}, u32[]{:S(2)}) async-start(bf16[32,64,128]{2,1,0:T(8,128)(2,1)} %broadcast_in_dim.10), calls=%async_computation.1 | async-start | bytes 1048576 | tf_op jit(solution)/shard_map/all_to_all | solution.py:39
  77.8 9.4 %collective-permute-start.10 = (bf16[4,32,1024]{2,1,0:T(8,128)(2,1)}, bf16[4,32,1024]{2,1,0:T(8,128)(2,1)S(1)}, u32[]{:S(2)}, u32[]{:S(2)}) collective-permute-start(bf16[4,32,1024]{2,1,0:T(8,128)(2,1)} %get-tuple-element.26), channel_id=1, source_target_pairs={{0,2},{1,3},{2,0},{3,1},{4,6},{5,7},{6,4},{7,5},{8,10},{9,11},{10,... | collective-permute-start | bytes 786440 | tf_op jit(solution)/shard_map/ppermute | solution.py:43
  78.5 12.9 %collective-permute-start.11 = (bf16[4,32,1024]{2,1,0:T(8,128)(2,1)}, bf16[4,32,1024]{2,1,0:T(8,128)(2,1)S(1)}, u32[]{:S(2)}, u32[]{:S(2)}) collective-permute-start(bf16[4,32,1024]{2,1,0:T(8,128)(2,1)} %get-tuple-element.25), channel_id=1, source_target_pairs={{0,3},{1,2},{2,1},{3,0},{4,7},{5,6},{6,5},{7,4},{8,11},{9,10},{10,... | collective-permute-start | bytes 786440 | tf_op jit(solution)/shard_map/ppermute | solution.py:43
  79.2 13.7 %collective-permute-start.9 = (bf16[4,32,1024]{2,1,0:T(8,128)(2,1)S(1)}, bf16[4,32,1024]{2,1,0:T(8,128)(2,1)S(1)}, u32[]{:S(2)}, u32[]{:S(2)}) collective-permute-start(bf16[4,32,1024]{2,1,0:T(8,128)(2,1)S(1)} %get-tuple-element.24), channel_id=1, source_target_pairs={{0,1},{1,0},{2,3},{3,2},{4,5},{5,4},{6,7},{7,6},{8,9},{9,8},{10,11... | collective-permute-start | bytes 786440 | tf_op jit(solution)/shard_map/ppermute | solution.py:43
  81.3 28.8 %collective-permute-start.20 = (bf16[1024,512]{1,0:T(8,128)(2,1)}, bf16[1024,512]{1,0:T(8,128)(2,1)}, u32[]{:S(2)}, u32[]{:S(2)}) collective-permute-start(bf16[1024,512]{1,0:T(8,128)(2,1)} %refs_8_.1), channel_id=1, source_target_pairs={{0,48},{16,0},{32,16},{48,32},{1,49},{17,1},{33,17},{49,33},{2,50}... | collective-permute-start | bytes 3145736 | tf_op jit(solution)/shard_map/ppermute | solution.py:228
  81.4 56.4 %collective-permute-start.22 = (bf16[1024,512]{1,0:T(8,128)(2,1)}, bf16[1024,512]{1,0:T(8,128)(2,1)}, u32[]{:S(2)}, u32[]{:S(2)}) collective-permute-start(bf16[1024,512]{1,0:T(8,128)(2,1)} %refs_8_.1), channel_id=1, source_target_pairs={{0,16},{16,32},{32,48},{48,0},{1,17},{17,33},{33,49},{49,1},{2,18}... | collective-permute-start | bytes 3145736 | tf_op jit(solution)/shard_map/ppermute | solution.py:228
  87.2 41.7 %collective-permute-start.24 = (bf16[1024,512]{1,0:T(8,128)(2,1)}, bf16[1024,512]{1,0:T(8,128)(2,1)}, u32[]{:S(2)}, u32[]{:S(2)}) collective-permute-start(bf16[1024,512]{1,0:T(8,128)(2,1)} %refs_12_.1), channel_id=1, source_target_pairs={{0,16},{16,32},{32,48},{48,0},{1,17},{17,33},{33,49},{49,1},{2,18}... | collective-permute-start | bytes 3145736 | tf_op jit(solution)/shard_map/ppermute | solution.py:228
  91.4 56.4 %collective-permute-start.23 = (bf16[1024,512]{1,0:T(8,128)(2,1)}, bf16[1024,512]{1,0:T(8,128)(2,1)}, u32[]{:S(2)}, u32[]{:S(2)}) collective-permute-start(bf16[1024,512]{1,0:T(8,128)(2,1)} %refs_12_.1), channel_id=1, source_target_pairs={{0,48},{16,0},{32,16},{48,32},{1,49},{17,1},{33,17},{49,33},{2,50}... | collective-permute-start | bytes 3145736 | tf_op jit(solution)/shard_map/ppermute | solution.py:228
  92.9 60.9 %collective-permute-start.28 = (bf16[512,1024]{1,0:T(8,128)(2,1)}, bf16[512,1024]{1,0:T(8,128)(2,1)}, u32[]{:S(2)}, u32[]{:S(2)}) collective-permute-start(bf16[512,1024]{1,0:T(8,128)(2,1)} %refs_0_.3), channel_id=1, source_target_pairs={{0,48},{16,0},{32,16},{48,32},{1,49},{17,1},{33,17},{49,33},{2,50}... | collective-permute-start | bytes 3145736 | tf_op jit(solution)/shard_map/ppermute | solution.py:228
  95.0 15.0 %all-to-all-start.2 = ((bf16[4,32,1024]{2,1,0:T(8,128)(2,1)}), bf16[4,32,1024]{2,1,0:T(8,128)(2,1)S(1)}, u32[]{:S(2)}, u32[]{:S(2)}) async-start(bf16[4,32,1024]{2,1,0:T(8,128)(2,1)} %fusion.11), calls=%async_computation.2 | async-start | bytes 524288 | tf_op jit(solution)/shard_map/all_to_all | solution.py:39
  110.1 19.4 %collective-permute-start.12 = (bf16[32,1024]{1,0:T(8,128)(2,1)S(1)}, bf16[32,1024]{1,0:T(8,128)(2,1)S(1)}, u32[]{:S(2)}, u32[]{:S(2)}) collective-permute-start(bf16[32,1024]{1,0:T(8,128)(2,1)S(1)} %add_convert_fusion.1), channel_id=1, source_target_pairs={{0,0},{1,1},{2,2},{3,3},{4,4},{5,5},{6,6},{7,7},{8,8},{9,9},{10,10... | collective-permute-start | bytes 196616 | tf_op jit(solution)/shard_map/ppermute | solution.py:57
  128.8 47.4 %collective-permute-start.21 = (bf16[1024,512]{1,0:T(8,128)(2,1)}, bf16[1024,512]{1,0:T(8,128)(2,1)}, u32[]{:S(2)}, u32[]{:S(2)}) collective-permute-start(bf16[1024,512]{1,0:T(8,128)(2,1)} %collective-permute-done.20.refs_9_), channel_id=1, source_target_pairs={{0,48},{16,0},{32,16},{48,32},{1,49},{17,1},{33,17},{49,33},{2,50}... | collective-permute-start | bytes 3145736 | tf_op jit(solution)/shard_map/ppermute | solution.py:228
  129.5 47.4 %collective-permute-start.25 = (bf16[1024,512]{1,0:T(8,128)(2,1)}, bf16[1024,512]{1,0:T(8,128)(2,1)}, u32[]{:S(2)}, u32[]{:S(2)}) collective-permute-start(bf16[1024,512]{1,0:T(8,128)(2,1)} %collective-permute-done.24.refs_15_), channel_id=1, source_target_pairs={{0,16},{16,32},{32,48},{48,0},{1,17},{17,33},{33,49},{49,1},{2,18}... | collective-permute-start | bytes 3145736 | tf_op jit(solution)/shard_map/ppermute | solution.py:228
  133.4 13.8 %all-to-all-start.3 = ((bf16[4,32,1024]{2,1,0:T(8,128)(2,1)}), bf16[4,32,1024]{2,1,0:T(8,128)(2,1)S(1)}, u32[]{:S(2)}, u32[]{:S(2)}) async-start(bf16[4,32,1024]{2,1,0:T(8,128)(2,1)} %broadcast_in_dim.12), calls=%async_computation.3 | async-start | bytes 524288 | tf_op jit(solution)/shard_map/all_to_all | solution.py:39
  147.1 30.6 %collective-permute-start.13 = (bf16[4,32,1024]{2,1,0:T(8,128)(2,1)S(1)}, bf16[4,32,1024]{2,1,0:T(8,128)(2,1)S(1)}, u32[]{:S(2)}, u32[]{:S(2)}) collective-permute-start(bf16[4,32,1024]{2,1,0:T(8,128)(2,1)S(1)} %all-to-all-done.3.refs_0_), channel_id=1, source_target_pairs={{0,1},{1,0},{2,3},{3,2},{4,5},{5,4},{6,7},{7,6},{8,9},{9,8},{10,11... | collective-permute-start | bytes 786440 | tf_op jit(solution)/shard_map/ppermute | solution.py:43
  147.8 60.1 %collective-permute-start.30 = (bf16[512,1024]{1,0:T(8,128)(2,1)}, bf16[512,1024]{1,0:T(8,128)(2,1)}, u32[]{:S(2)}, u32[]{:S(2)}) collective-permute-start(bf16[512,1024]{1,0:T(8,128)(2,1)} %refs_0_.3), channel_id=1, source_target_pairs={{0,16},{16,32},{32,48},{48,0},{1,17},{17,33},{33,49},{49,1},{2,18}... | collective-permute-start | bytes 3145736 | tf_op jit(solution)/shard_map/ppermute | solution.py:228
  153.8 54.1 %collective-permute-start.29 = (bf16[512,1024]{1,0:T(8,128)(2,1)}, bf16[512,1024]{1,0:T(8,128)(2,1)}, u32[]{:S(2)}, u32[]{:S(2)}) collective-permute-start(bf16[512,1024]{1,0:T(8,128)(2,1)} %collective-permute-done.28.refs_1_), channel_id=1, source_target_pairs={{0,48},{16,0},{32,16},{48,32},{1,49},{17,1},{33,17},{49,33},{2,50}... | collective-permute-start | bytes 3145736 | tf_op jit(solution)/shard_map/ppermute | solution.py:228
  176.9 9.8 %collective-permute-start.15 = (bf16[4,32,1024]{2,1,0:T(8,128)(2,1)S(1)}, bf16[4,32,1024]{2,1,0:T(8,128)(2,1)S(1)}, u32[]{:S(2)}, u32[]{:S(2)}) collective-permute-start(bf16[4,32,1024]{2,1,0:T(8,128)(2,1)S(1)} %all-to-all-done.3.refs_0_), channel_id=1, source_target_pairs={{0,3},{1,2},{2,1},{3,0},{4,7},{5,6},{6,5},{7,4},{8,11},{9,10},{10,... | collective-permute-start | bytes 786440 | tf_op jit(solution)/shard_map/ppermute | solution.py:43
  194.5 10.6 %collective-permute-start.26 = (bf16[128,1152]{1,0:T(8,128)(2,1)S(1)}, bf16[128,1152]{1,0:T(8,128)(2,1)S(1)}, u32[]{:S(2)}, u32[]{:S(2)}) collective-permute-start(bf16[128,1152]{1,0:T(8,128)(2,1)S(1)} %get-tuple-element.20), channel_id=1, source_target_pairs={{0,64},{64,0},{1,65},{65,1},{2,66},{66,2},{3,67},{67,3},{4,68},{68... | collective-permute-start | bytes 884744 | tf_op jit(solution)/shard_map/ppermute | solution.py:392
  223.1 13.4 %collective-permute-start.34 = (bf16[4,32,1024]{2,1,0:T(8,128)(2,1)S(1)}, bf16[4,32,1024]{2,1,0:T(8,128)(2,1)S(1)}, u32[]{:S(2)}, u32[]{:S(2)}) collective-permute-start(bf16[4,32,1024]{2,1,0:T(8,128)(2,1)S(1)} %get-tuple-element.22), channel_id=1, source_target_pairs={{0,3},{1,2},{2,1},{3,0},{4,7},{5,6},{6,5},{7,4},{8,11},{9,10},{10,... | collective-permute-start | bytes 786440 | tf_op jit(solution)/shard_map/ppermute | solution.py:43
  252.6 11.2 %collective-permute-start.35 = (bf16[32,1024]{1,0:T(8,128)(2,1)S(1)}, bf16[32,1024]{1,0:T(8,128)(2,1)S(1)}, u32[]{:S(2)}, u32[]{:S(2)}) collective-permute-start(bf16[32,1024]{1,0:T(8,128)(2,1)S(1)} %add_convert_fusion), channel_id=1, source_target_pairs={{0,0},{1,1},{2,2},{3,3},{4,16},{5,17},{6,18},{7,19},{8,32},{9,33},... | collective-permute-start | bytes 196616 | tf_op jit(solution)/shard_map/ppermute | solution.py:57
  (21 other events, 238.1 us)

commit v6 on v5

--- a/solution.py
+++ b/solution.py
@@ -228,21 +228,22 @@
     return lax.ppermute(array, "x", [(i, (i - r) % NX) for i in range(NX)])
 
 
-def project(place, pieces, gains, w_query, w_keyval, sums):
+def project(place, pieces, gains, w_query, w_keyval, sums, last=False):
     arrays = [piece for piece, _, _ in pieces]
     n_z, rows, width = arrays[0].shape
     n_q, n_kv = w_query.shape[1], w_keyval.shape[0]
     steps = n_z * len(arrays)
-    last = sums is not None
+    more = sums is not None
 
     def body(place_ref, gain_ref, wq_hbm, wkv_hbm, *refs):
         refs, rest = refs[: len(arrays)], refs[len(arrays) :]
-        before, rest = (rest[:3], rest[3:]) if last else (None, rest)
+        before, rest = (rest[:3], rest[3:]) if more else (None, rest)
         q_ref, kv_ref, sq_ref, wq, wkv, sem_q, sem_kv = rest
 
         def at(i):
             _, s, rc = pieces[i // n_z]
-            return ((place_ref[0] ^ rc) * n_z + i % n_z) * 4 + (place_ref[1] ^ s)
+            zh = (place_ref[4] + i % n_z) % n_z
+            return ((place_ref[0] ^ rc) * n_z + zh) * 4 + (place_ref[1] ^ s)
 
         def copies(i):
             g = at(i) * width
@@ -254,7 +255,7 @@
         for i in range(steps):
             for copy in copies(i):
                 copy.start()
-        if last:
+        if more:
             for ref, old in zip((q_ref, kv_ref, sq_ref), before):
                 ref[...] = old[...]
         else:
@@ -282,7 +283,7 @@
     return pl.pallas_call(
         body,
         out_shape=[pltpu.VMEM(shape, F32) for shape in shapes],
-        in_specs=[SMEM, VMEM, HBM, HBM] + [VMEM] * (len(arrays) + (3 if last else 0)),
+        in_specs=[SMEM, VMEM, HBM, HBM] + [VMEM] * (len(arrays) + (3 if more else 0)),
         out_specs=[VMEM] * 3,
         scratch_shapes=[
             pltpu.VMEM((steps, width, n_q), BF16),
@@ -290,7 +291,7 @@
             pltpu.SemaphoreType.DMA((steps,)),
             pltpu.SemaphoreType.DMA((steps,)),
         ],
-        name="project_last" if last else "project_first",
+        name="project_last" if last else "project_next" if more else "project_first",
     )(place, *in_vmem(gains), w_query, w_keyval, *in_vmem(*arrays, *(sums or ())))
 
 
@@ -305,9 +306,17 @@
     return (both(0) + sum(t.astype(F32) for t in got)).astype(BF16)
 
 
-def gathered(piece):
-    near = to_all(piece, "zh")
-    ours = [near] + [from_sq(near, s) for s in (1, 2, 3)]
+def gathered(piece, relative=False):
+    if relative:
+        near = [piece]
+        for r in range(1, NX):
+            hop = [(i, (i - r) % NX) for i in range(NX)]
+            near.append(lax.ppermute(piece, "zh", hop))
+        near = jnp.stack(near, axis=0)
+    else:
+        near = to_all(piece, "zh")
+    ours = [near] + [from_sq(near, s) for s in (1, 2)]
+    ours.append(from_sq(near, 3))
     theirs = [lax.ppermute(t, "c", SWAP) for t in ours]
     return ours, theirs
 
@@ -330,15 +339,17 @@
     down_next, down_last = from_x(w_down, 1), from_x(w_down, 3)
     down_all = [w_down, down_next, from_x(down_next, 1), down_last]
 
-    ours, theirs = gathered(tokens_in)
-    place = jnp.stack([core, spot, x, y_hi]).astype(jnp.int32)
+    ours, theirs = gathered(tokens_in, relative=True)
+    place = jnp.stack([core, spot, x, y_hi, z_hi]).astype(jnp.int32)
     gains = gain_attn.astype(F32).reshape(4 * n_z, 1, width)
     pieces = [(t, s, rc) for rc, side in ((0, ours), (1, theirs)) for s, t in enumerate(side)]
     early = [p for p in pieces if p[1] == 0]
-    late = [p for p in pieces if p[1] != 0]
+    middle = [p for p in pieces if p[1] in (1, 2) and p[2] == 0]
+    late = [p for p in pieces if p[1] == 3 or (p[1] != 0 and p[2] == 1)]
     w_kv = w_keyval.T
     sums = project(place, early, gains, w_query, w_kv, None)
-    query, kv_part, _ = project(place, late, gains, w_query, w_kv, sums)
+    sums = project(place, middle, gains, w_query, w_kv, sums)
+    query, kv_part, _ = project(place, late, gains, w_query, w_kv, sums, last=True)
 
     kv_here = move(
         kv_part.astype(BF16),
@@ -375,7 +386,7 @@
     sent = lax.ppermute(out_terms(place, attended, w_out, True), "c", SWAP)
     terms = out_terms(place, attended, w_out, False)
     resid = [
-        lax.dynamic_slice(t, ((x + z_hi) % NX, spot * quarter, 0), (1, quarter, width))[0]
+        lax.dynamic_slice(t, (x, spot * quarter, 0), (1, quarter, width))[0]
         for t in ours
     ]
     resid = jnp.stack(resid, axis=0)

time: 266 us -> 268 us (level)
  blocking collectives: 34.3 us -> 17.4 us
  starting transfers between devices: 55 us -> 70.2 us
    all_to_all x2 -> x1, blocking collectives: 34.3 us -> 17.4 us  [exchange(): return lax.all_to_all(tiles, axis, 0, 0, tiled=True)]
    ppermute x0 -> x3, starting transfers between devices: none -> 10.1 us  [gathered(): near.append(lax.ppermute(piece, 'zh', hop))]
    ppermute x0 -> x3, waiting for transfers between devices: none -> 5.68 us  [gathered(): near.append(lax.ppermute(piece, 'zh', hop))]
    all_to_all x3, starting transfers between devices: 21.8 us -> 27 us  [exchange(): return lax.all_to_all(tiles, axis, 0, 0, tiled=True)]
    ppermute x9, waiting for transfers between devices: 44.9 us -> 40.6 us  [from_x(): return lax.ppermute(array, 'x', [(i, (i - r) % NX) for i in range(NX)])]
    pallas_call x2 -> x3, Pallas kernels: 7.2 us -> 8.91 us  [project(): pl.pallas_call(body, out_shape=[pltpu.VMEM(shape, F32) for shape in shape...]
  transfers between devices with their start and end apart: 39 -> 42, of which waited for: 22 -> 23; matrix products, arithmetic and copies ran while one was open for 3% -> 3% of each run, Pallas kernels for 6% -> 7%
where the time goes in v6:
time: 268 us; the launch traced here: 266 us
  waiting for transfers between devices  134 us (50%)
  starting transfers between devices  70.2 us (26%)
  Pallas kernels  27.8 us (10%)
  blocking collectives  17.4 us (6%)
  other arithmetic  10.7 us (4%)
  local copies, waits for them, and re-layouts  5.37 us (2%)
    ppermute x9, waiting for transfers between devices, from_x(): return lax.ppermute(array, 'x', [(i, (i - r) % NX) for i in range(NX)])  40.6 us
    ppermute x12, waiting for transfers between devices, from_sq(): return lax.ppermute(array, ('zl', 'yl'), [(i, i ^ s) for i in range(4)])  36.7 us
    all_to_all x3, waiting for transfers between devices, exchange(): return lax.all_to_all(tiles, axis, 0, 0, tiled=True)  27.3 us
    all_to_all x3, starting transfers between devices, exchange(): return lax.all_to_all(tiles, axis, 0, 0, tiled=True)  27 us
    all_to_all x1, blocking collectives, exchange(): return lax.all_to_all(tiles, axis, 0, 0, tiled=True)  17.4 us
    ppermute x12, starting transfers between devices, from_sq(): return lax.ppermute(array, ('zl', 'yl'), [(i, i ^ s) for i in range(4)])  12.7 us
    ppermute x9, starting transfers between devices, from_x(): return lax.ppermute(array, 'x', [(i, (i - r) % NX) for i in range(NX)])  10.8 us
    ppermute x3, starting transfers between devices, gathered(): near.append(lax.ppermute(piece, 'zh', hop))  10.1 us
  transfers between devices with their start and end apart: 42, of which 23 were waited for; matrix products, arithmetic and copies ran while one was open for 3% of the time, Pallas kernels for 7%

profile of v6, /device:TPU:6, one launch (start us, length us, event | category | flops | bytes accessed | tf_op | source)
XLA Modules:
  0.0 266.4 jit_solution(364901635595192145)
XLA Ops:
  0.0 6.3 %collective-permute-start = (bf16[128,256]{1,0:T(8,128)(2,1)}, bf16[128,256]{1,0:T(8,128)(2,1)S(1)}, u32[]{:S(2)}, u32[]{:S(2)}) collective-permute-start(bf16[128,256]{1,0:T(8,128)(2,1)} %param.9), channel_id=1, source_target_pairs={{0,12},{4,0},{8,4},{12,8},{1,13},{5,1},{9,5},{13,9},{2,14},{6,2},{... | collective-permute-start | bytes 196616 | tf_op jit(solution)/shard_map/ppermute | solution.py:314
  11.5 4.3 %collective-permute-done.1 = bf16[128,256]{1,0:T(8,128)(2,1)S(1)} collective-permute-done((bf16[128,256]{1,0:T(8,128)(2,1)}, bf16[128,256]{1,0:T(8,128)(2,1)S(1)}, u32[]{:S(2)}, u32[]{:S(2)}) %collective-permute-start.1) | collective-permute-done | bytes 65568 | tf_op jit(solution)/shard_map/ppermute | solution.py:314
  20.3 4.4 %collective-permute-done.3.refs_0_ = bf16[4,128,256]{2,1,0:T(8,128)(2,1)S(1)} collective-permute-done((bf16[4,128,256]{2,1,0:T(8,128)(2,1)S(1)}, bf16[4,128,256]{2,1,0:T(8,128)(2,1)S(1)}, u32[]{:S(2)}, u32[]{:S(2)}) %collective-permute-start.3) | collective-permute-done | bytes 262176 | tf_op jit(solution)/shard_map/ppermute | solution.py:43
  36.7 3.9 %project_last.1 = (f32[128,256]{1,0:T(8,128)S(1)}, f32[64,128]{1,0:T(8,128)S(1)}, f32[128,256]{1,0:T(8,128)}) custom-call(s32[5]{0:T(128)} %stack.47.place_ref, f32[32,1,256]{2,1,0:T(1,128)S(1)} %bitcast.45, bf16[8192,256]{1,0:T(8,128)(2,1)} %wq_hbm.5, bf16[64,8192]{1,0:T(8,128)(2,1)} %bitcast.48, bf16[4,128,256]{2,1,0:T(8,128)(2,1)S(1)} %collective-permute-done.5.refs_0_, ...), custom_call_target="tpu_custom_call" | custom-call | tf_op jit(solution)/shard_map/project_last/pallas_call | solution.py:283
  42.1 13.1 %all-to-all-start = ((bf16[32,64,128]{2,1,0:T(8,128)(2,1)}), bf16[32,64,128]{2,1,0:T(8,128)(2,1)S(1)}, u32[]{:S(2)}, u32[]{:S(2)}) async-start(bf16[32,64,128]{2,1,0:T(8,128)(2,1)} %broadcast_in_dim.7), calls=%async_computation | async-start | bytes 1048576 | tf_op jit(solution)/shard_map/all_to_all | solution.py:39
  55.7 9.6 %all-to-all-done = bf16[32,64,128]{2,1,0:T(8,128)(2,1)S(1)} async-done(((bf16[32,64,128]{2,1,0:T(8,128)(2,1)}), bf16[32,64,128]{2,1,0:T(8,128)(2,1)S(1)}, u32[]{:S(2)}, u32[]{:S(2)}) %all-to-all-start) | async-done | bytes 524320 | tf_op jit(solution)/shard_map/all_to_all | solution.py:39
  87.8 4.8 %collective-permute-done.14 = bf16[4,32,1024]{2,1,0:T(8,128)(2,1)S(1)} collective-permute-done((bf16[4,32,1024]{2,1,0:T(8,128)(2,1)S(1)}, bf16[4,32,1024]{2,1,0:T(8,128)(2,1)S(1)}, u32[]{:S(2)}, u32[]{:S(2)}) %collective-permute-start.14) | collective-permute-done | bytes 262176 | tf_op jit(solution)/shard_map/ppermute | solution.py:43
  94.6 6.9 %all-to-all-start.1 = ((bf16[4,32,1024]{2,1,0:T(8,128)(2,1)}), bf16[4,32,1024]{2,1,0:T(8,128)(2,1)S(1)}, u32[]{:S(2)}, u32[]{:S(2)}) async-start(bf16[4,32,1024]{2,1,0:T(8,128)(2,1)} %fusion.11), calls=%async_computation.1 | async-start | bytes 524288 | tf_op jit(solution)/shard_map/all_to_all | solution.py:39
  103.0 8.4 %all-to-all-done.1 = bf16[4,32,1024]{2,1,0:T(8,128)(2,1)S(1)} async-done(((bf16[4,32,1024]{2,1,0:T(8,128)(2,1)}), bf16[4,32,1024]{2,1,0:T(8,128)(2,1)S(1)}, u32[]{:S(2)}, u32[]{:S(2)}) %all-to-all-start.1) | async-done | bytes 262176 | tf_op jit(solution)/shard_map/all_to_all | solution.py:39
  112.1 16.2 %collective-permute-done.27.refs_15_ = bf16[1024,512]{1,0:T(8,128)(2,1)} collective-permute-done((bf16[1024,512]{1,0:T(8,128)(2,1)}, bf16[1024,512]{1,0:T(8,128)(2,1)}, u32[]{:S(2)}, u32[]{:S(2)}) %collective-permute-start.27) | collective-permute-done | bytes 1048608 | tf_op jit(solution)/shard_map/ppermute | solution.py:228
  129.0 3.1 %collective-permute-start.28 = (bf16[1024,512]{1,0:T(8,128)(2,1)}, bf16[1024,512]{1,0:T(8,128)(2,1)}, u32[]{:S(2)}, u32[]{:S(2)}) collective-permute-start(bf16[1024,512]{1,0:T(8,128)(2,1)} %collective-permute-done.27.refs_15_), channel_id=1, source_target_pairs={{0,16},{16,32},{32,48},{48,0},{1,17},{17,33},{33,49},{49,1},{2,18}... | collective-permute-start | bytes 3145736 | tf_op jit(solution)/shard_map/ppermute | solution.py:228
  132.8 6.9 %all-to-all-start.2 = ((bf16[4,32,1024]{2,1,0:T(8,128)(2,1)}), bf16[4,32,1024]{2,1,0:T(8,128)(2,1)S(1)}, u32[]{:S(2)}, u32[]{:S(2)}) async-start(bf16[4,32,1024]{2,1,0:T(8,128)(2,1)} %broadcast_in_dim.9), calls=%async_computation.2 | async-start | bytes 524288 | tf_op jit(solution)/shard_map/all_to_all | solution.py:39
  139.8 9.3 %all-to-all-done.2.refs_0_ = bf16[4,32,1024]{2,1,0:T(8,128)(2,1)S(1)} async-done(((bf16[4,32,1024]{2,1,0:T(8,128)(2,1)}), bf16[4,32,1024]{2,1,0:T(8,128)(2,1)S(1)}, u32[]{:S(2)}, u32[]{:S(2)}) %all-to-all-start.2) | async-done | bytes 262176 | tf_op jit(solution)/shard_map/all_to_all | solution.py:39
  153.3 22.5 %collective-permute-done.24.refs_10_ = bf16[1024,512]{1,0:T(8,128)(2,1)} collective-permute-done((bf16[1024,512]{1,0:T(8,128)(2,1)}, bf16[1024,512]{1,0:T(8,128)(2,1)}, u32[]{:S(2)}, u32[]{:S(2)}) %collective-permute-start.24) | collective-permute-done | bytes 1048608 | tf_op jit(solution)/shard_map/ppermute | solution.py:228
  177.2 6.2 %collective-permute-done.17.refs_2_ = bf16[4,32,1024]{2,1,0:T(8,128)(2,1)S(1)} collective-permute-done((bf16[4,32,1024]{2,1,0:T(8,128)(2,1)S(1)}, bf16[4,32,1024]{2,1,0:T(8,128)(2,1)S(1)}, u32[]{:S(2)}, u32[]{:S(2)}) %collective-permute-start.17) | collective-permute-done | bytes 262176 | tf_op jit(solution)/shard_map/ppermute | solution.py:43
  188.1 5.9 %gate_up.1 = (bf16[128,1152]{1,0:T(8,128)(2,1)S(1)}, f32[128,1024]{1,0:T(8,128)}, f32[128,128]{1,0:T(8,128)}) custom-call(s32[5]{0:T(128)} %stack.47.place_ref, f32[8,1,1024]{2,1,0:T(1,128)} %bitcast.51, bf16[4,32,1024]{2,1,0:T(8,128)(2,1)S(1)} %all-to-all-done.2.refs_0_, bf16[4,32,1024]{2,1,0:T(8,128)(2,1)S(1)} %collective-permute-done.16.refs_1_, ...), custom_call_target="tpu_custom_call" | custom-call | tf_op jit(solution)/shard_map/gate_up/pallas_call | solution.py:150
  195.5 9.2 %collective-permute-done.29.sent_ref = bf16[128,1152]{1,0:T(8,128)(2,1)S(1)} collective-permute-done((bf16[128,1152]{1,0:T(8,128)(2,1)S(1)}, bf16[128,1152]{1,0:T(8,128)(2,1)S(1)}, u32[]{:S(2)}, u32[]{:S(2)}) %collective-permute-start.29) | collective-permute-done | bytes 294944 | tf_op jit(solution)/shard_map/ppermute | solution.py:403
  207.4 5.1 %collective-permute-done.30.other_ref = bf16[128,512]{1,0:T(8,128)(2,1)S(1)} collective-permute-done((bf16[128,512]{1,0:T(8,128)(2,1)S(1)}, bf16[128,512]{1,0:T(8,128)(2,1)S(1)}, u32[]{:S(2)}, u32[]{:S(2)}) %collective-permute-start.30) | collective-permute-done | bytes 131104 | tf_op jit(solution)/shard_map/ppermute | solution.py:406
  212.5 3.2 %down_give.1 = bf16[4,128,1024]{2,1,0:T(8,128)(2,1)S(1)} custom-call(s32[5]{0:T(128)} %stack.47.place_ref, bf16[128,512]{1,0:T(8,128)(2,1)S(1)} %hidden.1.hidden_ref, bf16[128,512]{1,0:T(8,128)(2,1)S(1)} %collective-permute-done.30.other_ref, bf16[512,1024]{1,0:T(8,128)(2,1)} %refs_0_.3, bf16[512,1024]{1,0:T(8,128)(2,1)} %collective-permute-done.31.refs_1_, ...), custom_call_target="tpu_custom_call" | custom-call | tf_op jit(solution)/shard_map/down_give/pallas_call | solution.py:206
  215.8 3.2 %down_keep.1 = f32[4,128,1024]{2,1,0:T(8,128)S(1)} custom-call(s32[5]{0:T(128)} %stack.47.place_ref, bf16[128,512]{1,0:T(8,128)(2,1)S(1)} %hidden.1.hidden_ref, bf16[128,512]{1,0:T(8,128)(2,1)S(1)} %collective-permute-done.30.other_ref, bf16[512,1024]{1,0:T(8,128)(2,1)} %refs_0_.3, bf16[512,1024]{1,0:T(8,128)(2,1)} %collective-permute-done.31.refs_1_, ...), custom_call_target="tpu_custom_call" | custom-call | tf_op jit(solution)/shard_map/down_keep/pallas_call | solution.py:206
  223.9 5.2 %collective-permute-done.35 = bf16[4,32,1024]{2,1,0:T(8,128)(2,1)S(1)} collective-permute-done((bf16[4,32,1024]{2,1,0:T(8,128)(2,1)S(1)}, bf16[4,32,1024]{2,1,0:T(8,128)(2,1)S(1)}, u32[]{:S(2)}, u32[]{:S(2)}) %collective-permute-start.35) | collective-permute-done | bytes 262176 | tf_op jit(solution)/shard_map/ppermute | solution.py:43
  231.1 4.9 %collective-permute-done.37 = bf16[4,32,1024]{2,1,0:T(8,128)(2,1)S(1)} collective-permute-done((bf16[4,32,1024]{2,1,0:T(8,128)(2,1)S(1)}, bf16[4,32,1024]{2,1,0:T(8,128)(2,1)S(1)}, u32[]{:S(2)}, u32[]{:S(2)}) %collective-permute-start.37) | collective-permute-done | bytes 262176 | tf_op jit(solution)/shard_map/ppermute | solution.py:43
  237.1 17.4 %all_to_all.20 = bf16[4,32,1024]{2,1,0:T(8,128)(2,1)S(1)} all-to-all(bf16[4,32,1024]{2,1,0:T(8,128)(2,1)S(1)} %fusion.6), channel_id=1, replica_groups=mesh['c'=2,'yh'=2,'x'=4,'zh'=4,'zl'=2,'yl'=2] {'zh'}, dimensions={0} | all-to-all | bytes 524288 | tf_op jit(solution)/shard_map/all_to_all | solution.py:39
  257.4 8.3 %collective-permute-done.38 = bf16[32,1024]{1,0:T(8,128)(2,1)S(1)} collective-permute-done((bf16[32,1024]{1,0:T(8,128)(2,1)S(1)}, bf16[32,1024]{1,0:T(8,128)(2,1)S(1)}, u32[]{:S(2)}, u32[]{:S(2)}) %collective-permute-start.38) | collective-permute-done | bytes 65568 | tf_op jit(solution)/shard_map/ppermute | solution.py:57
  (117 shorter events, 77.9 us)
Async XLA Ops:
  0.0 11.5 %collective-permute-start = (bf16[128,256]{1,0:T(8,128)(2,1)}, bf16[128,256]{1,0:T(8,128)(2,1)S(1)}, u32[]{:S(2)}, u32[]{:S(2)}) collective-permute-start(bf16[128,256]{1,0:T(8,128)(2,1)} %param.9), channel_id=1, source_target_pairs={{0,12},{4,0},{8,4},{12,8},{1,13},{5,1},{9,5},{13,9},{2,14},{6,2},{... | collective-permute-start | bytes 196616 | tf_op jit(solution)/shard_map/ppermute | solution.py:314
  19.3 10.8 %collective-permute-start.5 = (bf16[4,128,256]{2,1,0:T(8,128)(2,1)S(1)}, bf16[4,128,256]{2,1,0:T(8,128)(2,1)S(1)}, u32[]{:S(2)}, u32[]{:S(2)}) collective-permute-start(bf16[4,128,256]{2,1,0:T(8,128)(2,1)S(1)} %pad_maximum_fusion.refs_0_), channel_id=1, source_target_pairs={{0,3},{1,2},{2,1},{3,0},{4,7},{5,6},{6,5},{7,4},{8,11},{9,10},{10,... | collective-permute-start | bytes 786440 | tf_op jit(solution)/shard_map/ppermute | solution.py:43
  20.3 11.3 %collective-permute-start.9 = (bf16[4,128,256]{2,1,0:T(8,128)(2,1)S(1)}, bf16[4,128,256]{2,1,0:T(8,128)(2,1)S(1)}, u32[]{:S(2)}, u32[]{:S(2)}) collective-permute-start(bf16[4,128,256]{2,1,0:T(8,128)(2,1)S(1)} %pad_maximum_fusion.refs_0_), channel_id=1, source_target_pairs={{0,128},{128,0},{1,129},{129,1},{2,130},{130,2},{3,131},{131,3},{4... | collective-permute-start | bytes 786440 | tf_op jit(solution)/shard_map/ppermute | solution.py:320
  24.7 12.0 %collective-permute-start.6 = (bf16[4,128,256]{2,1,0:T(8,128)(2,1)S(1)}, bf16[4,128,256]{2,1,0:T(8,128)(2,1)S(1)}, u32[]{:S(2)}, u32[]{:S(2)}) collective-permute-start(bf16[4,128,256]{2,1,0:T(8,128)(2,1)S(1)} %collective-permute-done.3.refs_0_), channel_id=1, source_target_pairs={{0,128},{128,0},{1,129},{129,1},{2,130},{130,2},{3,131},{131,3},{4... | collective-permute-start | bytes 786440 | tf_op jit(solution)/shard_map/ppermute | solution.py:320
  42.1 23.1 %all-to-all-start = ((bf16[32,64,128]{2,1,0:T(8,128)(2,1)}), bf16[32,64,128]{2,1,0:T(8,128)(2,1)S(1)}, u32[]{:S(2)}, u32[]{:S(2)}) async-start(bf16[32,64,128]{2,1,0:T(8,128)(2,1)} %broadcast_in_dim.7), calls=%async_computation | async-start | bytes 1048576 | tf_op jit(solution)/shard_map/all_to_all | solution.py:39
  77.3 10.0 %collective-permute-start.13 = (bf16[4,32,1024]{2,1,0:T(8,128)(2,1)}, bf16[4,32,1024]{2,1,0:T(8,128)(2,1)S(1)}, u32[]{:S(2)}, u32[]{:S(2)}) collective-permute-start(bf16[4,32,1024]{2,1,0:T(8,128)(2,1)} %get-tuple-element.32), channel_id=1, source_target_pairs={{0,2},{1,3},{2,0},{3,1},{4,6},{5,7},{6,4},{7,5},{8,10},{9,11},{10,... | collective-permute-start | bytes 786440 | tf_op jit(solution)/shard_map/ppermute | solution.py:43
  78.5 14.1 %collective-permute-start.14 = (bf16[4,32,1024]{2,1,0:T(8,128)(2,1)S(1)}, bf16[4,32,1024]{2,1,0:T(8,128)(2,1)S(1)}, u32[]{:S(2)}, u32[]{:S(2)}) collective-permute-start(bf16[4,32,1024]{2,1,0:T(8,128)(2,1)S(1)} %get-tuple-element.31), channel_id=1, source_target_pairs={{0,3},{1,2},{2,1},{3,0},{4,7},{5,6},{6,5},{7,4},{8,11},{9,10},{10,... | collective-permute-start | bytes 786440 | tf_op jit(solution)/shard_map/ppermute | solution.py:43
  80.8 30.7 %collective-permute-start.23 = (bf16[1024,512]{1,0:T(8,128)(2,1)}, bf16[1024,512]{1,0:T(8,128)(2,1)}, u32[]{:S(2)}, u32[]{:S(2)}) collective-permute-start(bf16[1024,512]{1,0:T(8,128)(2,1)} %refs_8_.1), channel_id=1, source_target_pairs={{0,48},{16,0},{32,16},{48,32},{1,49},{17,1},{33,17},{49,33},{2,50}... | collective-permute-start | bytes 3145736 | tf_op jit(solution)/shard_map/ppermute | solution.py:228
  80.9 58.8 %collective-permute-start.25 = (bf16[1024,512]{1,0:T(8,128)(2,1)}, bf16[1024,512]{1,0:T(8,128)(2,1)}, u32[]{:S(2)}, u32[]{:S(2)}) collective-permute-start(bf16[1024,512]{1,0:T(8,128)(2,1)} %refs_8_.1), channel_id=1, source_target_pairs={{0,16},{16,32},{32,48},{48,0},{1,17},{17,33},{33,49},{49,1},{2,18}... | collective-permute-start | bytes 3145736 | tf_op jit(solution)/shard_map/ppermute | solution.py:228
  85.8 42.6 %collective-permute-start.27 = (bf16[1024,512]{1,0:T(8,128)(2,1)}, bf16[1024,512]{1,0:T(8,128)(2,1)}, u32[]{:S(2)}, u32[]{:S(2)}) collective-permute-start(bf16[1024,512]{1,0:T(8,128)(2,1)} %refs_12_.1), channel_id=1, source_target_pairs={{0,16},{16,32},{32,48},{48,0},{1,17},{17,33},{33,49},{49,1},{2,18}... | collective-permute-start | bytes 3145736 | tf_op jit(solution)/shard_map/ppermute | solution.py:228
  87.3 62.5 %collective-permute-start.26 = (bf16[1024,512]{1,0:T(8,128)(2,1)}, bf16[1024,512]{1,0:T(8,128)(2,1)}, u32[]{:S(2)}, u32[]{:S(2)}) collective-permute-start(bf16[1024,512]{1,0:T(8,128)(2,1)} %refs_12_.1), channel_id=1, source_target_pairs={{0,48},{16,0},{32,16},{48,32},{1,49},{17,1},{33,17},{49,33},{2,50}... | collective-permute-start | bytes 3145736 | tf_op jit(solution)/shard_map/ppermute | solution.py:228
  92.6 60.7 %collective-permute-start.31 = (bf16[512,1024]{1,0:T(8,128)(2,1)}, bf16[512,1024]{1,0:T(8,128)(2,1)}, u32[]{:S(2)}, u32[]{:S(2)}) collective-permute-start(bf16[512,1024]{1,0:T(8,128)(2,1)} %refs_0_.3), channel_id=1, source_target_pairs={{0,48},{16,0},{32,16},{48,32},{1,49},{17,1},{33,17},{49,33},{2,50}... | collective-permute-start | bytes 3145736 | tf_op jit(solution)/shard_map/ppermute | solution.py:228
  94.6 16.8 %all-to-all-start.1 = ((bf16[4,32,1024]{2,1,0:T(8,128)(2,1)}), bf16[4,32,1024]{2,1,0:T(8,128)(2,1)S(1)}, u32[]{:S(2)}, u32[]{:S(2)}) async-start(bf16[4,32,1024]{2,1,0:T(8,128)(2,1)} %fusion.11), calls=%async_computation.1 | async-start | bytes 524288 | tf_op jit(solution)/shard_map/all_to_all | solution.py:39
  111.5 17.6 %collective-permute-start.15 = (bf16[32,1024]{1,0:T(8,128)(2,1)S(1)}, bf16[32,1024]{1,0:T(8,128)(2,1)S(1)}, u32[]{:S(2)}, u32[]{:S(2)}) collective-permute-start(bf16[32,1024]{1,0:T(8,128)(2,1)S(1)} %add_convert_fusion.1), channel_id=1, source_target_pairs={{0,0},{1,1},{2,2},{3,3},{4,4},{5,5},{6,6},{7,7},{8,8},{9,9},{10,10... | collective-permute-start | bytes 196616 | tf_op jit(solution)/shard_map/ppermute | solution.py:57
  128.3 47.4 %collective-permute-start.24 = (bf16[1024,512]{1,0:T(8,128)(2,1)}, bf16[1024,512]{1,0:T(8,128)(2,1)}, u32[]{:S(2)}, u32[]{:S(2)}) collective-permute-start(bf16[1024,512]{1,0:T(8,128)(2,1)} %collective-permute-done.23.refs_9_), channel_id=1, source_target_pairs={{0,48},{16,0},{32,16},{48,32},{1,49},{17,1},{33,17},{49,33},{2,50}... | collective-permute-start | bytes 3145736 | tf_op jit(solution)/shard_map/ppermute | solution.py:228
  129.0 47.4 %collective-permute-start.28 = (bf16[1024,512]{1,0:T(8,128)(2,1)}, bf16[1024,512]{1,0:T(8,128)(2,1)}, u32[]{:S(2)}, u32[]{:S(2)}) collective-permute-start(bf16[1024,512]{1,0:T(8,128)(2,1)} %collective-permute-done.27.refs_15_), channel_id=1, source_target_pairs={{0,16},{16,32},{32,48},{48,0},{1,17},{17,33},{33,49},{49,1},{2,18}... | collective-permute-start | bytes 3145736 | tf_op jit(solution)/shard_map/ppermute | solution.py:228
  132.8 16.2 %all-to-all-start.2 = ((bf16[4,32,1024]{2,1,0:T(8,128)(2,1)}), bf16[4,32,1024]{2,1,0:T(8,128)(2,1)S(1)}, u32[]{:S(2)}, u32[]{:S(2)}) async-start(bf16[4,32,1024]{2,1,0:T(8,128)(2,1)} %broadcast_in_dim.9), calls=%async_computation.2 | async-start | bytes 524288 | tf_op jit(solution)/shard_map/all_to_all | solution.py:39
  149.1 28.1 %collective-permute-start.16 = (bf16[4,32,1024]{2,1,0:T(8,128)(2,1)S(1)}, bf16[4,32,1024]{2,1,0:T(8,128)(2,1)S(1)}, u32[]{:S(2)}, u32[]{:S(2)}) collective-permute-start(bf16[4,32,1024]{2,1,0:T(8,128)(2,1)S(1)} %all-to-all-done.2.refs_0_), channel_id=1, source_target_pairs={{0,1},{1,0},{2,3},{3,2},{4,5},{5,4},{6,7},{7,6},{8,9},{9,8},{10,11... | collective-permute-start | bytes 786440 | tf_op jit(solution)/shard_map/ppermute | solution.py:43
  149.7 57.7 %collective-permute-start.33 = (bf16[512,1024]{1,0:T(8,128)(2,1)}, bf16[512,1024]{1,0:T(8,128)(2,1)}, u32[]{:S(2)}, u32[]{:S(2)}) collective-permute-start(bf16[512,1024]{1,0:T(8,128)(2,1)} %refs_0_.3), channel_id=1, source_target_pairs={{0,16},{16,32},{32,48},{48,0},{1,17},{17,33},{33,49},{49,1},{2,18}... | collective-permute-start | bytes 3145736 | tf_op jit(solution)/shard_map/ppermute | solution.py:228
  153.3 54.1 %collective-permute-start.32 = (bf16[512,1024]{1,0:T(8,128)(2,1)}, bf16[512,1024]{1,0:T(8,128)(2,1)}, u32[]{:S(2)}, u32[]{:S(2)}) collective-permute-start(bf16[512,1024]{1,0:T(8,128)(2,1)} %collective-permute-done.31.refs_1_), channel_id=1, source_target_pairs={{0,48},{16,0},{32,16},{48,32},{1,49},{17,1},{33,17},{49,33},{2,50}... | collective-permute-start | bytes 3145736 | tf_op jit(solution)/shard_map/ppermute | solution.py:228
  176.4 9.8 %collective-permute-start.18 = (bf16[4,32,1024]{2,1,0:T(8,128)(2,1)S(1)}, bf16[4,32,1024]{2,1,0:T(8,128)(2,1)S(1)}, u32[]{:S(2)}, u32[]{:S(2)}) collective-permute-start(bf16[4,32,1024]{2,1,0:T(8,128)(2,1)S(1)} %all-to-all-done.2.refs_0_), channel_id=1, source_target_pairs={{0,3},{1,2},{2,1},{3,0},{4,7},{5,6},{6,5},{7,4},{8,11},{9,10},{10,... | collective-permute-start | bytes 786440 | tf_op jit(solution)/shard_map/ppermute | solution.py:43
  194.0 10.6 %collective-permute-start.29 = (bf16[128,1152]{1,0:T(8,128)(2,1)S(1)}, bf16[128,1152]{1,0:T(8,128)(2,1)S(1)}, u32[]{:S(2)}, u32[]{:S(2)}) collective-permute-start(bf16[128,1152]{1,0:T(8,128)(2,1)S(1)} %get-tuple-element.26), channel_id=1, source_target_pairs={{0,64},{64,0},{1,65},{65,1},{2,66},{66,2},{3,67},{67,3},{4,68},{68... | collective-permute-start | bytes 884744 | tf_op jit(solution)/shard_map/ppermute | solution.py:403
  222.6 13.4 %collective-permute-start.37 = (bf16[4,32,1024]{2,1,0:T(8,128)(2,1)S(1)}, bf16[4,32,1024]{2,1,0:T(8,128)(2,1)S(1)}, u32[]{:S(2)}, u32[]{:S(2)}) collective-permute-start(bf16[4,32,1024]{2,1,0:T(8,128)(2,1)S(1)} %get-tuple-element.28), channel_id=1, source_target_pairs={{0,3},{1,2},{2,1},{3,0},{4,7},{5,6},{6,5},{7,4},{8,11},{9,10},{10,... | collective-permute-start | bytes 786440 | tf_op jit(solution)/shard_map/ppermute | solution.py:43
  254.6 11.2 %collective-permute-start.38 = (bf16[32,1024]{1,0:T(8,128)(2,1)S(1)}, bf16[32,1024]{1,0:T(8,128)(2,1)S(1)}, u32[]{:S(2)}, u32[]{:S(2)}) collective-permute-start(bf16[32,1024]{1,0:T(8,128)(2,1)S(1)} %add_convert_fusion), channel_id=1, source_target_pairs={{0,0},{1,1},{2,2},{3,3},{4,16},{5,17},{6,18},{7,19},{8,32},{9,33},... | collective-permute-start | bytes 196616 | tf_op jit(solution)/shard_map/ppermute | solution.py:57
  (24 other events, 278.4 us)
